TPU v7x, 32 devices: a whole 2x2x4 slice. The times are simulated.
32 devices in a mesh: fsdp: 4 (over z), context: 8 (over y, x, core).
Axes of the slice: x: 2, y: 2, z: 4, core: 2. Of those that a mesh axis runs over, the one named last changes fastest.
Arguments:
- block_input: bfloat16 [4, 1024, 1536], P('fsdp', 'context'), may hold values from -15 to 15
- cotangent: bfloat16 [4, 1024, 1536], P('fsdp', 'context'), may hold values from -6 to 6
- documents: int32 [4, 1024], P('fsdp', 'context'), may hold values from 0 to 7, as said below
- attn_weights: float32 [4608, 1536], P(('fsdp', 'context')), may hold values from -1.5 to 1.5
- ffn_weights: float32 [12288, 1536], P(('fsdp', 'context')), may hold values from -0.36 to 0.36
- norm_gains: float32 [2, 1536], replicated, may hold values from -0.5 to 0.5
- attn_moments: float32 [2, 4608, 1536], P(None, ('fsdp', 'context')), may hold values from -0.8 to 0.8, as said below
- ffn_moments: float32 [2, 12288, 1536], P(None, ('fsdp', 'context')), may hold values from -0.8 to 0.8, as said below
- gain_moments: float32 [2, 2, 1536], P(None, None, ('fsdp', 'context')), may hold values from -0.8 to 0.8, as said below
Outputs:
- block_output: float32 [4, 1024, 1536], P('fsdp', 'context')
- input_grad: float32 [4, 1024, 1536], P('fsdp', 'context')
- attn_grad: float32 [4608, 1536], P(('fsdp', 'context'))
- ffn_grad: float32 [12288, 1536], P(('fsdp', 'context'))
- gain_grad: float32 [2, 1536], P(None, ('fsdp', 'context'))
- new_attn_weights: float32 [4608, 1536], P(('fsdp', 'context'))
- new_ffn_weights: float32 [12288, 1536], P(('fsdp', 'context'))
- new_norm_gains: float32 [2, 1536], P(None, ('fsdp', 'context'))
- new_attn_moments: float32 [2, 4608, 1536], P(None, ('fsdp', 'context'))
- new_ffn_moments: float32 [2, 12288, 1536], P(None, ('fsdp', 'context'))
- new_gain_moments: float32 [2, 2, 1536], P(None, None, ('fsdp', 'context'))
Inputs may be any that keep to these rules, and one draw needn't show every extreme that they name: Segment numbers never fall along a sequence and start at 0; each sequence holds 8 documents of 50 to 640 tokens, one of exactly 640. `attn_moments`: entry 1 along the first dimension is positive. `ffn_moments`: entry 1 along the first dimension is positive. `gain_moments`: entry 1 along the first dimension is positive.
All inputs are finite; a program needn't handle non-finite values.
Results may differ from a plain program's by a relative error of at most 0.015.
Values may be sent and summed in bfloat16 or wider, within the bound.
A program may use at most 448 MiB of HBM per device.

v0:
```python
import math

import jax
import jax.numpy as jnp
from jax import lax
from jax.sharding import PartitionSpec as P

FF = 4096
QUERY_HEADS = 16
KEY_VALUE_HEADS = 8
HEAD_SIZE = 96
STEP = 3


NORM_EPS = 1e-05
ROPE_THETA = 100000.0
BETA_ONE = 0.9
BETA_TWO = 0.95
ADAM_EPS = 1e-08
LEARN_RATE = 0.02
WEIGHT_DECAY = 0.1


def product_transposed(left_matrix, right_matrix):
    return lax.dot_general(
        left_matrix, right_matrix, (((1,), (1,)), ((), ())), preferred_element_type=jnp.float32
    )


def transposed_times(left_matrix, right_matrix):
    return lax.dot_general(
        left_matrix, right_matrix, (((0,), (0,)), ((), ())), preferred_element_type=jnp.float32
    )


def plain_times(left_matrix, right_matrix):
    return jnp.dot(left_matrix, right_matrix, preferred_element_type=jnp.float32)


def rms_scale(tensor_in):
    return lax.rsqrt(jnp.mean(tensor_in * tensor_in, axis=-1, keepdims=True) + NORM_EPS)


def norm_backward(grad_in, normed, norm_scale, gain_row):
    scaled = grad_in * (1.0 + gain_row)
    return norm_scale * (scaled - normed * jnp.mean(scaled * normed, axis=-1, keepdims=True))


def rope_tables(positions):
    half_width = HEAD_SIZE // 2
    frequency = ROPE_THETA ** (-2.0 * jnp.arange(half_width, dtype=jnp.float32) / HEAD_SIZE)
    angles = positions.astype(jnp.float32)[:, None] * frequency[None, :]
    return (jnp.cos(angles), jnp.sin(angles))


def rotary_heads(tensor_in, cosine_lookup, sine_lookup, direction):
    half_width = HEAD_SIZE // 2
    first_half = tensor_in[..., :half_width]
    second_half = tensor_in[..., half_width:]
    cos_rows = cosine_lookup[:, None, :]
    sin_rows = sine_lookup[:, None, :] * direction
    return jnp.concatenate(
        [
            first_half * cos_rows - second_half * sin_rows,
            second_half * cos_rows + first_half * sin_rows,
        ],
        axis=-1,
    )


def split_weights(attn_full, ffn_full):
    query_width = QUERY_HEADS * HEAD_SIZE
    key_value_width = KEY_VALUE_HEADS * HEAD_SIZE
    return (
        attn_full[:query_width],
        attn_full[query_width : query_width + key_value_width],
        attn_full[query_width + key_value_width : query_width + 2 * key_value_width],
        attn_full[query_width + 2 * key_value_width :],
        ffn_full[:FF],
        ffn_full[FF : 2 * FF],
        ffn_full[2 * FF :],
    )


def adamw_update(parameter, gradient, moments, decay_rate):
    first_moment = BETA_ONE * moments[0] + (1.0 - BETA_ONE) * gradient
    second_moment = BETA_TWO * moments[1] + (1.0 - BETA_TWO) * gradient * gradient
    first_hat = first_moment / (1.0 - BETA_ONE**STEP)
    second_hat = second_moment / (1.0 - BETA_TWO**STEP)
    updated = parameter - LEARN_RATE * (
        first_hat / (jnp.sqrt(second_hat) + ADAM_EPS) + decay_rate * parameter
    )
    return (updated, jnp.stack([first_moment, second_moment]))


def on_device(
    block_input,
    cotangent,
    documents,
    attn_weights,
    ffn_weights,
    norm_gains,
    attn_moments,
    ffn_moments,
    gain_moments,
):
    local_rows = block_input.shape[1]
    heads_per_group = QUERY_HEADS // KEY_VALUE_HEADS
    query_width = QUERY_HEADS * HEAD_SIZE
    key_value_width = KEY_VALUE_HEADS * HEAD_SIZE
    score_scale = HEAD_SIZE ** (-0.5)
    grad_factor = float(local_rows * lax.axis_size(("fsdp", "context"))) ** (-0.5)
    attn_full, ffn_full = (
        lax.all_gather(attn_weights.astype(jnp.bfloat16), ("fsdp", "context"), axis=0, tiled=True),
        lax.all_gather(ffn_weights.astype(jnp.bfloat16), ("fsdp", "context"), axis=0, tiled=True),
    )
    w_query, key_weight, value_weight, w_out, w_gate, w_up, w_down = split_weights(
        attn_full, ffn_full
    )
    own_docs = documents[0]
    all_docs = lax.all_gather(own_docs, "context", axis=0, tiled=True)
    query_index = lax.axis_index("context") * local_rows + jnp.arange(local_rows, dtype=jnp.int32)
    doc_starts = jnp.sum((all_docs[None, :] < own_docs[:, None]).astype(jnp.int32), axis=1)
    cosine_lookup, sine_lookup = rope_tables(query_index - doc_starts)

    def block_mask(key_first, key_width):
        key_index = key_first + jnp.arange(key_width, dtype=jnp.int32)
        key_docs = lax.dynamic_slice_in_dim(all_docs, key_first, key_width, 0)
        return (key_index[None, :] <= query_index[:, None]) & (
            key_docs[None, :] == own_docs[:, None]
        )

    residual = block_input[0].astype(jnp.float32)
    scale_one = rms_scale(residual)
    normed_one = residual * scale_one
    first_hidden = (normed_one * (1.0 + norm_gains[0])).astype(jnp.bfloat16)
    query_matrix = rotary_heads(
        product_transposed(first_hidden, w_query).reshape(local_rows, QUERY_HEADS, HEAD_SIZE),
        cosine_lookup,
        sine_lookup,
        1.0,
    ).astype(jnp.bfloat16)
    key_flat = (
        rotary_heads(
            product_transposed(first_hidden, key_weight).reshape(
                local_rows, KEY_VALUE_HEADS, HEAD_SIZE
            ),
            cosine_lookup,
            sine_lookup,
            1.0,
        )
        .astype(jnp.bfloat16)
        .reshape(local_rows, key_value_width)
    )
    value_flat = product_transposed(first_hidden, value_weight).astype(jnp.bfloat16)
    grouped_queries = query_matrix.reshape(local_rows, KEY_VALUE_HEADS, heads_per_group, HEAD_SIZE)
    start_pair = (
        jnp.zeros((KEY_VALUE_HEADS, heads_per_group, local_rows, HEAD_SIZE), jnp.float32),
        jnp.zeros((KEY_VALUE_HEADS, heads_per_group, local_rows), jnp.float32),
    )
    key_piece = lax.all_gather(key_flat, "context", axis=0, tiled=True)
    value_piece = lax.all_gather(value_flat, "context", axis=0, tiled=True)
    piece_rows = key_piece.shape[0]
    inner_rows = math.gcd(piece_rows, 512)

    def sub_block(sub_index, inner_pair):
        out_sum, total_sum = inner_pair
        offset = sub_index * inner_rows
        key_block = lax.dynamic_slice_in_dim(key_piece, offset, inner_rows, 0).reshape(
            inner_rows, KEY_VALUE_HEADS, HEAD_SIZE
        )
        value_block = lax.dynamic_slice_in_dim(value_piece, offset, inner_rows, 0).reshape(
            inner_rows, KEY_VALUE_HEADS, HEAD_SIZE
        )
        allowed = block_mask(offset, inner_rows)
        scores = (
            jnp.einsum(
                "qhgd,khd->hgqk", grouped_queries, key_block, preferred_element_type=jnp.float32
            )
            * score_scale
        )
        exponent = jnp.where(allowed[None, None], jnp.exp(scores), 0.0)
        out_sum = out_sum + jnp.einsum(
            "hgqk,khd->hgqd",
            exponent.astype(jnp.bfloat16),
            value_block,
            preferred_element_type=jnp.float32,
        )
        return (out_sum, total_sum + jnp.sum(exponent, axis=-1))

    out_sum, totals = lax.fori_loop(0, piece_rows // inner_rows, sub_block, start_pair)
    log_totals = jnp.log(totals)
    attended_rows = (
        (out_sum / totals[..., None])
        .transpose(2, 0, 1, 3)
        .reshape(local_rows, query_width)
        .astype(jnp.bfloat16)
    )
    middle = residual + plain_times(attended_rows, w_out)
    scale_two = rms_scale(middle)
    normed_two = middle * scale_two
    hidden_two = (normed_two * (1.0 + norm_gains[1])).astype(jnp.bfloat16)
    gate_pre = product_transposed(hidden_two, w_gate)
    up_pre = product_transposed(hidden_two, w_up)
    sigmoid_gate = jax.nn.sigmoid(gate_pre)
    activated = (gate_pre * sigmoid_gate * up_pre).astype(jnp.bfloat16)
    block_out = middle + plain_times(activated, w_down)
    attn_back, ffn_back = (
        lax.all_gather(attn_weights.astype(jnp.bfloat16), ("fsdp", "context"), axis=0, tiled=True),
        lax.all_gather(ffn_weights.astype(jnp.bfloat16), ("fsdp", "context"), axis=0, tiled=True),
    )
    w_query, key_weight, value_weight, w_out, w_gate, w_up, w_down = split_weights(
        attn_back, ffn_back
    )
    seq_cotangent = cotangent[0]
    grad_act = product_transposed(seq_cotangent, w_down)
    grad_gate = (grad_act * up_pre * sigmoid_gate * (1.0 + gate_pre * (1.0 - sigmoid_gate))).astype(
        jnp.bfloat16
    )
    grad_up = (grad_act * gate_pre * sigmoid_gate).astype(jnp.bfloat16)
    ffn_term = (
        jnp.concatenate(
            [
                transposed_times(grad_gate, hidden_two),
                transposed_times(grad_up, hidden_two),
                transposed_times(activated, seq_cotangent),
            ],
            axis=0,
        )
        * grad_factor
    )
    grad_hidden_two = plain_times(grad_gate, w_gate) + plain_times(grad_up, w_up)
    gain_two = jnp.sum(grad_hidden_two * normed_two, axis=0)
    grad_middle = seq_cotangent.astype(jnp.float32) + norm_backward(
        grad_hidden_two, normed_two, scale_two, norm_gains[1]
    )
    grad_middle_bf = grad_middle.astype(jnp.bfloat16)
    grad_w_out = transposed_times(attended_rows, grad_middle_bf)
    attended_gradient = product_transposed(grad_middle_bf, w_out).astype(jnp.bfloat16)
    group_gradient = attended_gradient.reshape(
        local_rows, KEY_VALUE_HEADS, heads_per_group, HEAD_SIZE
    )
    row_delta = jnp.sum(
        group_gradient.astype(jnp.float32)
        * attended_rows.reshape(local_rows, KEY_VALUE_HEADS, heads_per_group, HEAD_SIZE).astype(
            jnp.float32
        ),
        axis=-1,
    ).transpose(1, 2, 0)
    seq_rows = local_rows * lax.axis_size("context")
    start_three = (
        jnp.zeros((KEY_VALUE_HEADS, heads_per_group, local_rows, HEAD_SIZE), jnp.float32),
        jnp.zeros((seq_rows, key_value_width), jnp.float32),
        jnp.zeros((seq_rows, key_value_width), jnp.float32),
    )
    attend_key_piece = lax.all_gather(key_flat, "context", axis=0, tiled=True)
    attend_value_piece = lax.all_gather(value_flat, "context", axis=0, tiled=True)
    piece_rows = attend_key_piece.shape[0]
    attend_inner_rows = math.gcd(piece_rows, 512)

    def sub_block(sub_index, inner_three):
        grad_query, grad_key_all, grad_value_all = inner_three
        offset = sub_index * attend_inner_rows
        key_block = lax.dynamic_slice_in_dim(
            attend_key_piece, offset, attend_inner_rows, 0
        ).reshape(attend_inner_rows, KEY_VALUE_HEADS, HEAD_SIZE)
        value_block = lax.dynamic_slice_in_dim(
            attend_value_piece, offset, attend_inner_rows, 0
        ).reshape(attend_inner_rows, KEY_VALUE_HEADS, HEAD_SIZE)
        allowed = block_mask(offset, attend_inner_rows)
        scores = (
            jnp.einsum(
                "qhgd,khd->hgqk", grouped_queries, key_block, preferred_element_type=jnp.float32
            )
            * score_scale
        )
        probabilities = jnp.where(allowed[None, None], jnp.exp(scores - log_totals[..., None]), 0.0)
        grad_probs = jnp.einsum(
            "qhgd,khd->hgqk", group_gradient, value_block, preferred_element_type=jnp.float32
        )
        grad_scores = (probabilities * (grad_probs - row_delta[..., None]) * score_scale).astype(
            jnp.bfloat16
        )
        grad_query = grad_query + jnp.einsum(
            "hgqk,khd->hgqd", grad_scores, key_block, preferred_element_type=jnp.float32
        )
        key_part = jnp.einsum(
            "hgqk,qhgd->khd", grad_scores, grouped_queries, preferred_element_type=jnp.float32
        ).reshape(attend_inner_rows, key_value_width)
        value_part = jnp.einsum(
            "hgqk,qhgd->khd",
            probabilities.astype(jnp.bfloat16),
            group_gradient,
            preferred_element_type=jnp.float32,
        ).reshape(attend_inner_rows, key_value_width)
        grad_key_all = lax.dynamic_update_slice_in_dim(grad_key_all, key_part, offset, 0)
        grad_value_all = lax.dynamic_update_slice_in_dim(grad_value_all, value_part, offset, 0)
        return (grad_query, grad_key_all, grad_value_all)

    grad_query_sum, grad_key_all, grad_value_all = lax.fori_loop(
        0, piece_rows // attend_inner_rows, sub_block, start_three
    )
    key_gradient_rows, grad_values = (
        lax.psum_scatter(
            grad_key_all.astype(jnp.bfloat16), "context", scatter_dimension=0, tiled=True
        ).astype(jnp.float32),
        lax.psum_scatter(
            grad_value_all.astype(jnp.bfloat16), "context", scatter_dimension=0, tiled=True
        ).astype(jnp.float32),
    )
    grad_q_bf = (
        rotary_heads(
            grad_query_sum.transpose(2, 0, 1, 3).reshape(local_rows, QUERY_HEADS, HEAD_SIZE),
            cosine_lookup,
            sine_lookup,
            -1.0,
        )
        .reshape(local_rows, query_width)
        .astype(jnp.bfloat16)
    )
    grad_k_bf = (
        rotary_heads(
            key_gradient_rows.reshape(local_rows, KEY_VALUE_HEADS, HEAD_SIZE),
            cosine_lookup,
            sine_lookup,
            -1.0,
        )
        .reshape(local_rows, key_value_width)
        .astype(jnp.bfloat16)
    )
    grad_v_bf = grad_values.astype(jnp.bfloat16)
    attn_term = (
        jnp.concatenate(
            [
                transposed_times(grad_q_bf, first_hidden),
                transposed_times(grad_k_bf, first_hidden),
                transposed_times(grad_v_bf, first_hidden),
                grad_w_out,
            ],
            axis=0,
        )
        * grad_factor
    )
    grad_hidden_one = (
        plain_times(grad_q_bf, w_query)
        + plain_times(grad_k_bf, key_weight)
        + plain_times(grad_v_bf, value_weight)
    )
    gain_one = jnp.sum(grad_hidden_one * normed_one, axis=0)
    grad_input = grad_middle + norm_backward(grad_hidden_one, normed_one, scale_one, norm_gains[0])
    gain_term = jnp.stack([gain_one, gain_two]) * grad_factor
    attn_shard, ffn_shard, gain_shard = (
        lax.psum_scatter(attn_term, ("fsdp", "context"), scatter_dimension=0, tiled=True),
        lax.psum_scatter(ffn_term, ("fsdp", "context"), scatter_dimension=0, tiled=True),
        lax.psum_scatter(gain_term, ("fsdp", "context"), scatter_dimension=1, tiled=True),
    )
    column_count = norm_gains.shape[1] // lax.axis_size(("fsdp", "context"))
    own_gains = lax.dynamic_slice_in_dim(
        norm_gains, lax.axis_index(("fsdp", "context")) * column_count, column_count, 1
    )
    new_attn, attn_states = adamw_update(attn_weights, attn_shard, attn_moments, WEIGHT_DECAY)
    new_ffn, ffn_states = adamw_update(ffn_weights, ffn_shard, ffn_moments, WEIGHT_DECAY)
    new_gains, gain_states = adamw_update(own_gains, gain_shard, gain_moments, 0.0)
    return (
        block_out[None],
        grad_input[None],
        attn_shard,
        ffn_shard,
        gain_shard,
        new_attn,
        new_ffn,
        new_gains,
        attn_states,
        ffn_states,
        gain_states,
    )


def solution(mesh):
    placed = (
        P("fsdp", "context", None),
        P("fsdp", "context", None),
        P("fsdp", "context"),
        P(("fsdp", "context"), None),
        P(("fsdp", "context"), None),
        P(),
        P(None, ("fsdp", "context"), None),
        P(None, ("fsdp", "context"), None),
        P(None, None, ("fsdp", "context")),
    )
    return jax.shard_map(
        on_device,
        mesh=mesh,
        in_specs=placed,
        out_specs=(
            P("fsdp", "context", None),
            P("fsdp", "context", None),
            P(("fsdp", "context"), None),
            P(("fsdp", "context"), None),
            P(None, ("fsdp", "context")),
            P(("fsdp", "context"), None),
            P(("fsdp", "context"), None),
            P(None, ("fsdp", "context")),
            P(None, ("fsdp", "context"), None),
            P(None, ("fsdp", "context"), None),
            P(None, None, ("fsdp", "context")),
        ),
        check_vma=False,
    )
```

profile of v0, /device:TPU:0, one launch (start us, length us, event | category | flops | bytes accessed | tf_op | source)
XLA Modules:
  0.0 1590.1 jit_solution(6565524639662273563)
XLA Ops:
  11.3 105.4 %all-gather.6.cloned.1.call-done = bf16[4608,1536]{1,0:T(8,128)(2,1)} async-done(((bf16[144,1536]{1,0:T(8,128)(2,1)}), bf16[4608,1536]{1,0:T(8,128)(2,1)}) %all-gather.6.cloned.1.call-update) | async-done | bytes 14155792 | tf_op jit(solution)/shard_map/all_gather | solution.py:114
  116.7 3.5 fusion.65
  120.3 8.8 all-gather
  138.1 6.3 all-gather.10.cloned.1.call-done
  147.0 25.7 %all-gather.8.cloned.1.call-done = bf16[1024,768]{0,1:T(8,128)(2,1)} async-done(((bf16[128,768]{0,1:T(8,128)(2,1)}), bf16[1024,768]{0,1:T(8,128)(2,1)}) %all-gather.8.cloned.1.call-update) | async-done | bytes 1572880 | tf_op jit(solution)/shard_map/all_gather | solution.py:161
  172.7 16.3 %while.34 = (s32[]{:T(128)}, f32[8,2,128,96]{2,3,1,0:T(8,128)S(1)}, f32[8,2,128]{2,1,0:T(2,128)S(1)}, s32[1024]{0:T(1024)S(1)}, s32[1,128]{1,0:T(1,128)S(1)}, /*...) while((s32[]{:T(128)}, f32[8,2,128,96]{2,3,1,0:T(8,128)S(1)}, ...), condition=%wide.region_4.5_spmd.clone, body=%wide.region_2.4_spmd.clone.sunk | while | flops 409537152 | bytes 15314638 | solution.py:191
  177.5 3.1 fusion.177
  185.5 3.4 fusion.177
  189.1 3.4 multiply_reduce_fusion.3
  192.6 197.7 %all-gather.12.cloned.1.call-done = bf16[12288,1536]{1,0:T(8,128)(2,1)} async-done(((bf16[384,1536]{1,0:T(8,128)(2,1)}), bf16[12288,1536]{1,0:T(8,128)(2,1)}) %all-gather.12.cloned.1.call-update) | async-done | bytes 37748752 | tf_op jit(solution)/shard_map/all_gather | solution.py:115
  390.4 7.0 fusion.30
  397.4 7.1 fusion.36
  404.5 8.4 multiply_convert_fusion.1
  412.9 6.4 fusion.34
  419.4 6.1 multiply_reduce_fusion
  433.4 28.4 %while.35 = (s32[]{:T(128)}, f32[8,2,128,96]{2,3,1,0:T(8,128)}, bf16[1024,768]{0,1:T(8,128)(2,1)}, bf16[1024,768]{0,1:T(8,128)(2,1)}, s32[1024]{0:T(1024)S(1)}, ...) while((s32[]{:T(128)}, f32[8,2,128,96]{2,3,1,0:T(8,128)}, ...), condition=%wide.region_9.10_spmd.clone, body=%wide.region_8.9_spmd.clone.sunk | while | flops 1018757760 | bytes 91197336 | solution.py:300
  466.5 3.3 fusion.114
  469.8 5.0 fusion.96
  474.8 4.9 fusion.99
  479.7 21.5 %reduce-scatter.16.cloned.1.call-done = bf16[128,768]{1,0:T(8,128)(2,1)} async-done(((bf16[1024,768]{1,0:T(8,128)(2,1)}), bf16[128,768]{1,0:T(8,128)(2,1)}) %reduce-scatter.16.cloned.1.call-update) | async-done | bytes 196624
  507.7 35.7 %reduce-scatter.18.cloned.1.call-done = bf16[128,768]{1,0:T(8,128)(2,1)} async-done(((bf16[1024,768]{1,0:T(8,128)(2,1)}), bf16[128,768]{1,0:T(8,128)(2,1)}) %reduce-scatter.18.cloned.1.call-update) | async-done | bytes 196624
  543.4 3.2 fusion.81
  550.2 17.9 %maximum_multiply_fusion.1 = f32[4608,1536]{1,0:T(8,128)} fusion(f32[1536,1536]{1,0:T(8,128)} %fusion.99, f32[768,1536]{1,0:T(8,128)S(1)} %fusion.103, f32[768,1536]{1,0:T(8,128)S(1)} %copy-done.5, f32[1536,1536]{1,0:T(8,128)} %fusion.96), kind=kLoop, calls=%fused_computation.42 | loop fusion | flops 28311552 | bytes 56623104 | tf_op jit(solution)/shard_map/mul | solution.py:333
  569.1 11.6 fusion.119
  580.7 10.2 fusion.118
  590.9 10.2 fusion.87
  601.1 51.5 %maximum_multiply_fusion = f32[12288,1536]{1,0:T(8,128)} fusion(f32[4096,1536]{1,0:T(8,128)} %fusion.87, f32[4096,1536]{1,0:T(8,128)} %fusion.119, f32[4096,1536]{1,0:T(8,128)} %fusion.118), kind=kLoop, calls=%fused_computation.41 | loop fusion | flops 56623104 | bytes 150994944 | tf_op jit(solution)/shard_map/mul | solution.py:222
  653.7 8.4 fusion.55
  666.0 248.3 %reduce-scatter.12.cloned.1.call-done = f32[144,1536]{1,0:T(8,128)} async-done(((f32[4608,1536]{1,0:T(8,128)}), f32[144,1536]{1,0:T(8,128)}) %reduce-scatter.12.cloned.1.call-update) | async-done | bytes 884752 | tf_op jit(solution)/shard_map/reduce_scatter | solution.py:353
  914.3 3.3 fusion.98
  918.9 655.7 %reduce-scatter.14.cloned.1.call-done = f32[384,1536]{1,0:T(8,128)} async-done(((f32[12288,1536]{1,0:T(8,128)}), f32[384,1536]{1,0:T(8,128)}) %reduce-scatter.14.cloned.1.call-update) | async-done | bytes 2359312 | tf_op jit(solution)/shard_map/reduce_scatter | solution.py:354
  1574.6 6.3 fusion.85
  (198 shorter events, 85.6 us)
Async XLA Ops:
  7.2 113.1 %copy-start.29 = (s32[1,128]{1,0:T(1,128)S(1)}, s32[1,128]{1,0:T(1,128)}, u32[]{:S(2)}) copy-start(s32[1,128]{1,0:T(1,128)} %param.15) | copy-start | bytes 1540
  7.2 109.5 %all-gather.6.cloned.1.call-start = ((), (), s32[]{:S(2)}) async-start(), calls=%async_computation.5 | async-start | bytes 14598144 | tf_op jit(solution)/shard_map/all_gather | solution.py:114
  9.2 135.2 %all-gather.10.cloned.1.call-start = ((), (), s32[]{:S(2)}) async-start(), calls=%async_computation.7 | async-start | bytes 1769472 | tf_op jit(solution)/shard_map/all_gather | solution.py:162
  116.7 12.8 slice-start.4
  116.7 12.8 copy-start.3
  120.3 52.4 %all-gather.8.cloned.1.call-start = ((), (), s32[]{:S(2)}) async-start(), calls=%async_computation.6 | async-start | bytes 1769472 | tf_op jit(solution)/shard_map/all_gather | solution.py:161
  131.1 259.3 %all-gather.12.cloned.1.call-start = ((), (), s32[]{:S(2)}) async-start(), calls=%async_computation.8 | async-start | bytes 38928384 | tf_op jit(solution)/shard_map/all_gather | solution.py:115
  134.0 367.2 %reduce-scatter.16.cloned.1.call-start = ((), (), s32[]{:S(2)}) async-start(), calls=%async_computation.11 | async-start | bytes 1769472
  189.0 201.4 %copy-start.21 = (bf16[1,128,1536]{2,1,0:T(8,128)(2,1)S(1)}, bf16[1,128,1536]{2,1,0:T(8,128)(2,1)}, u32[]{:S(2)}) copy-start(bf16[1,128,1536]{2,1,0:T(8,128)(2,1)} %param.14) | copy-start | bytes 1179652
  192.5 226.9 %copy-start.17 = (f32[128,1536]{1,0:T(8,128)}, f32[128,1536]{1,0:T(8,128)S(1)}, u32[]{:S(2)}) copy-start(f32[128,1536]{1,0:T(8,128)S(1)} %get-tuple-element.633) | copy-start | bytes 2359300
  192.6 211.9 %copy-start.15 = (bf16[128,1536]{1,0:T(8,128)(2,1)}, bf16[128,1536]{1,0:T(8,128)(2,1)S(1)}, u32[]{:S(2)}) copy-start(bf16[128,1536]{1,0:T(8,128)(2,1)S(1)} %multiply_convert_fusion.3) | copy-start | bytes 1179652
  412.9 6.4 copy-start.26
  412.9 6.5 copy-start.24
  412.9 14.0 slice-start
  412.9 14.0 slice-start.1
  419.4 7.6 slice-start.2
  419.4 7.6 slice-start.3
  435.7 4.7 copy-start
  464.6 78.8 %reduce-scatter.18.cloned.1.call-start = ((), (), s32[]{:S(2)}) async-start(), calls=%async_computation.12 | async-start | bytes 1769472
  466.4 196.9 %reduce-scatter.20.cloned.1.call-start = ((), (), s32[]{:S(2)}) async-start(), calls=%async_computation.13 | async-start | bytes 811008
  469.7 5.1 copy-start.8
  469.8 5.1 copy-start.20
  547.8 366.5 %reduce-scatter.12.cloned.1.call-start = ((), (), s32[]{:S(2)}) async-start(), calls=%async_computation.9 | async-start | bytes 29196288 | tf_op jit(solution)/shard_map/reduce_scatter | solution.py:353
  568.2 12.5 copy-start.25
  568.2 1006.4 %reduce-scatter.14.cloned.1.call-start = ((), (), s32[]{:S(2)}) async-start(), calls=%async_computation.10 | async-start | bytes 77856768 | tf_op jit(solution)/shard_map/reduce_scatter | solution.py:354
  580.7 10.2 copy-start.22
  580.7 10.2 copy-start.23
  653.7 8.4 copy-start.27
  653.7 10.4 copy-start.31
  653.7 260.6 %copy-start.14 = (f32[144,1536]{1,0:T(8,128)S(1)}, f32[144,1536]{1,0:T(8,128)}, u32[]{:S(2)}) copy-start(f32[144,1536]{1,0:T(8,128)} %param.16) | copy-start | bytes 2654212
  664.1 254.8 %copy-start.30 = (f32[2,48]{1,0:T(2,128)}, f32[2,48]{1,0:T(2,128)S(1)}, u32[]{:S(2)}) copy-start(f32[2,48]{1,0:T(2,128)S(1)} %copy.64) | copy-start | bytes 1156
  666.0 908.6 %copy-start.6 = (f32[384,1536]{1,0:T(8,128)S(1)}, f32[384,1536]{1,0:T(8,128)}, u32[]{:S(2)}) copy-start(f32[384,1536]{1,0:T(8,128)} %param.17) | copy-start | bytes 7077892
  (21 other events, 55.9 us)
Sparse Core Ops, SparseCore 0:
  11.5 105.2 all-gather.5
  120.4 23.9 all-gather.9
  146.9 25.7 all-gather.7
  176.0 214.3 all-gather.11
  464.7 36.5 reduce-scatter.15
  505.0 38.3 reduce-scatter.17
  549.0 96.1 reduce-scatter.19
  652.3 261.9 reduce-scatter.11
  921.3 653.2 reduce-scatter.13
where the time goes:
time: 1600 us; the launch traced here: 1590 us
  waiting for transfers between devices  1300 us (81%)
  matrix products  138 us (9%)
  other arithmetic  97.8 us (6%)
  local copies, waits for them, and re-layouts  33.7 us (2%)
    reduce_scatter x1, waiting for transfers between devices, on_device(): lax.psum_scatter(ffn_term, ('fsdp', 'context'), scatter_dimension=0, tile...  656 us
    reduce_scatter x1, waiting for transfers between devices, on_device(): lax.psum_scatter(attn_term, ('fsdp', 'context'), scatter_dimension=0, til...  248 us
    all_gather x1, waiting for transfers between devices, on_device(): lax.all_gather(ffn_weights.astype(jnp.bfloat16), ('fsdp', 'context'), axi...  198 us
    all_gather x1, waiting for transfers between devices, on_device(): lax.all_gather(attn_weights.astype(jnp.bfloat16), ('fsdp', 'context'), ax...  105 us
    unnamed x12, waiting for transfers between devices  57.3 us
    mul x1, other arithmetic, on_device(): jnp.concatenate([transposed_times(grad_gate, hidden_two), transposed_time...  51.5 us
    dot_general x7, matrix products, transposed_times(): lax.dot_general(left_matrix, right_matrix, (((0,), (0,)), ((), ())), pref...  45.8 us
    dot_general x7, matrix products, plain_times(): jnp.dot(left_matrix, right_matrix, preferred_element_type=jnp.float32)  32.9 us
  transfers between devices with their start and end apart: 9, of which 8 were waited for; matrix products, arithmetic and copies ran while one was open for 11% of the time, Pallas kernels for 0%

commit v1 on v0

v1 whole, which is shorter than its diff:
```python
import functools

import jax
import jax.numpy as jnp
import numpy as np
from jax import lax
from jax.experimental import pallas as pl
from jax.experimental.pallas import tpu as pltpu
from jax.sharding import PartitionSpec as P

QUERY_HEADS = 16
KEY_VALUE_HEADS = 8
HEAD_SIZE = 96
STEP = 3

NORM_EPS = 1e-05
ROPE_THETA = 100000.0
BETA_ONE = 0.9
BETA_TWO = 0.95
ADAM_EPS = 1e-08
LEARN_RATE = 0.02
WEIGHT_DECAY = 0.1

LANES = 128
TILE = 256
CHUNK = 16
VMEM_LIMIT = 62 * 1024 * 1024
EVERY = ("fsdp", "context")
BF = jnp.bfloat16
F32 = jnp.float32
ID_TYPE = pl.DeviceIdType.MESH


def product_transposed(left_matrix, right_matrix):
    return lax.dot_general(
        left_matrix, right_matrix, (((1,), (1,)), ((), ())), preferred_element_type=F32
    )


def transposed_times(left_matrix, right_matrix):
    return lax.dot_general(
        left_matrix, right_matrix, (((0,), (0,)), ((), ())), preferred_element_type=F32
    )


def plain_times(left_matrix, right_matrix):
    return jnp.dot(left_matrix, right_matrix, preferred_element_type=F32)


def rms_scale(tensor_in):
    return lax.rsqrt(jnp.mean(tensor_in * tensor_in, axis=-1, keepdims=True) + NORM_EPS)


def norm_backward(grad_in, normed, norm_scale, gain_row):
    scaled = grad_in * (1.0 + gain_row)
    return norm_scale * (scaled - normed * jnp.mean(scaled * normed, axis=-1, keepdims=True))


def adamw_update(parameter, gradient, moments, decay_rate):
    first_moment = BETA_ONE * moments[0] + (1.0 - BETA_ONE) * gradient
    second_moment = BETA_TWO * moments[1] + (1.0 - BETA_TWO) * gradient * gradient
    first_hat = first_moment / (1.0 - BETA_ONE**STEP)
    second_hat = second_moment / (1.0 - BETA_TWO**STEP)
    updated = parameter - LEARN_RATE * (
        first_hat / (jnp.sqrt(second_hat) + ADAM_EPS) + decay_rate * parameter
    )
    return (updated, jnp.stack([first_moment, second_moment]))


class UnitPlan:
    def __init__(self, homes, devices):
        waiting = [[] for _ in range(devices)]
        for unit, (device, place) in enumerate(homes):
            waiting[unit // 3].append((unit % 3, device, place))
        self.rounds = []
        for _ in range(3):
            taken = [None] * devices

            def settle(source, seen):
                for piece, device, place in waiting[source]:
                    if device in seen:
                        continue
                    seen.add(device)
                    if taken[device] is None or settle(taken[device][0], seen):
                        taken[device] = (source, piece, place)
                        return True
                return False

            for source in range(devices):
                if not settle(source, set()):
                    raise ValueError("no matching")
            pairs, pieces, places = [], [0] * devices, [0] * devices
            for device, (source, piece, place) in enumerate(taken):
                pairs.append((source, device))
                pieces[source] = piece
                places[device] = place
                waiting[source].remove((piece, device, place))
            self.rounds.append((pairs, np.array(pieces), np.array(places)))

    def _reorder(self, got, columns):
        order = np.argsort(np.stack(columns, axis=1), axis=1).astype(np.int32)
        mine = jnp.asarray(order)[lax.axis_index(EVERY)]
        stacked = jnp.stack(got)
        return jnp.concatenate(
            [lax.dynamic_index_in_dim(stacked, mine[k], 0, keepdims=False) for k in range(3)]
        )

    def spread(self, rows):
        pieces = rows.reshape(3, rows.shape[0] // 3, rows.shape[1])
        me = lax.axis_index(EVERY)
        got = []
        for pairs, piece, _ in self.rounds:
            unit = lax.dynamic_index_in_dim(
                pieces, jnp.asarray(piece, jnp.int32)[me], 0, keepdims=False
            )
            got.append(lax.ppermute(unit, EVERY, pairs))
        return self._reorder(got, [place for _, _, place in self.rounds])

    def collect(self, rows):
        places_of = rows.reshape(3, rows.shape[0] // 3, rows.shape[1])
        me = lax.axis_index(EVERY)
        got = []
        for pairs, _, place in self.rounds:
            unit = lax.dynamic_index_in_dim(
                places_of, jnp.asarray(place, jnp.int32)[me], 0, keepdims=False
            )
            got.append(lax.ppermute(unit, EVERY, [(b, a) for a, b in pairs]))
        return self._reorder(got, [piece for _, piece, _ in self.rounds])


def unit_plans(layers, columns, attn_rows, ffn_rows):
    devices = layers * columns

    def home(column, position):
        return ((position // 3) * columns + column, position % 3)

    homes = []
    for unit in range(3 * devices):
        matrix, rest = divmod(unit, devices)
        stretch, column = divmod(rest, columns)
        homes.append(home(column, matrix * layers + stretch))
    ffn_plan = UnitPlan(homes, devices)
    unit_rows = attn_rows // (3 * devices)
    query_units = QUERY_HEADS * HEAD_SIZE // columns // unit_rows
    share_units = KEY_VALUE_HEADS * HEAD_SIZE // columns // unit_rows
    homes = []
    position = 0
    for count in (query_units, share_units, share_units, query_units):
        for column in range(columns):
            for k in range(count):
                homes.append(home(column, position + k))
        position += count
    return UnitPlan(homes, devices), ffn_plan


def partner(me, step, chips):
    return lax.rem(me // 2 + step, chips) * 2 + lax.rem(me, 2)


def sibling_of(me):
    return me + 1 - 2 * lax.rem(me, 2)


def rows_at(index, rows):
    return pl.ds(pl.multiple_of(index * rows, rows), rows)


def greet(columns, layers=1):
    barrier = pltpu.get_barrier_semaphore()
    me = lax.axis_index("context")
    for step in range(1, columns):
        pl.semaphore_signal(
            barrier, inc=1, device_id={"context": lax.rem(me + step, columns)}, device_id_type=ID_TYPE
        )
    if layers > 1:
        layer = lax.axis_index("fsdp")
        for step in range(1, layers):
            pl.semaphore_signal(
                barrier, inc=1, device_id={"fsdp": lax.rem(layer + step, layers)}, device_id_type=ID_TYPE
            )
    pl.semaphore_wait(barrier, columns - 1 + layers - 1)


def send(source, target, send_sem, recv_sem, device):
    copy = pltpu.make_async_remote_copy(
        src_ref=source,
        dst_ref=target,
        send_sem=send_sem,
        recv_sem=recv_sem,
        device_id=device,
        device_id_type=ID_TYPE,
    )
    copy.start()
    return copy


class Gather:
    @staticmethod
    def scratch(chips):
        return [
            pltpu.SemaphoreType.DMA((chips,)),
            pltpu.SemaphoreType.DMA((chips,)),
            pltpu.SemaphoreType.DMA((chips,)),
            pltpu.SemaphoreType.DMA((chips,)),
            pltpu.SemaphoreType.DMA,
        ]

    def __init__(self, block, full, chips, sems):
        own_send, own_recv, self.on_send, self.on_recv, local_sem = sems
        me = lax.axis_index("context")
        rows = block.shape[0]
        self.block, self.full, self.chips, self.me, self.rows = block, full, chips, me, rows
        mine = full.at[rows_at(me, rows), :]
        self.own = [
            send(block, mine, own_send.at[step], own_recv.at[step], {"context": partner(me, step, chips)})
            for step in range(1, chips)
        ]
        self.own.append(
            send(block, mine, own_send.at[0], own_recv.at[0], {"context": sibling_of(me)})
        )
        self.local = pltpu.make_async_copy(block, mine, local_sem)
        self.local.start()

    def finish(self):
        passed = []
        for step in range(1, self.chips):
            self.own[step - 1].wait_recv()
            source = partner(self.me, self.chips - step, self.chips)
            there = self.full.at[rows_at(source, self.rows), :]
            passed.append(
                send(there, there, self.on_send.at[step], self.on_recv.at[step], {"context": sibling_of(self.me)})
            )
        self.own[-1].wait_recv()
        for copy in passed:
            copy.wait_recv()
        for copy in self.own + passed:
            copy.wait_send()
        self.local.wait()


class Reduce:
    @staticmethod
    def scratch(chips, rows, width):
        return [
            pltpu.VMEM((chips, rows, width), BF),
            pltpu.VMEM((chips, rows, width), BF),
            pltpu.VMEM((chips, rows, width), BF),
            pltpu.SemaphoreType.DMA((chips,)),
            pltpu.SemaphoreType.DMA((chips,)),
            pltpu.SemaphoreType.DMA((chips,)),
            pltpu.SemaphoreType.DMA((chips,)),
        ]

    def __init__(self, part, chips, rows, scratch):
        self.near, self.summed, self.far, near_send, near_recv, self.far_send, self.far_recv = scratch
        me = lax.axis_index("context")
        self.part, self.chips, self.rows, self.me = part, chips, rows, me
        self.near_copies = {}
        for step in [*range(1, chips), 0]:
            block = partner(sibling_of(me), step, chips)
            self.near_copies[step] = send(
                part.at[rows_at(block, rows), :],
                self.near.at[step],
                near_send.at[step],
                near_recv.at[step],
                {"context": sibling_of(me)},
            )
        self.far_copies = []

    def exchange(self):
        for step in range(1, self.chips):
            self.near_copies[step].wait_recv()
            target = partner(self.me, step, self.chips)
            first = pl.multiple_of(target * self.rows, self.rows)

            @pl.loop(0, self.rows // CHUNK)
            def add(k):
                at = pl.ds(pl.multiple_of(k * CHUNK, CHUNK), CHUNK)
                from_part = pl.ds(pl.multiple_of(first + k * CHUNK, CHUNK), CHUNK)
                self.summed[step, at, :] = (
                    self.part[from_part, :].astype(F32) + self.near[step, at, :].astype(F32)
                ).astype(BF)

            self.far_copies.append(
                send(
                    self.summed.at[step],
                    self.far.at[step],
                    self.far_send.at[step],
                    self.far_recv.at[step],
                    {"context": target},
                )
            )

    def arrive(self):
        self.near_copies[0].wait_recv()
        for copy in self.far_copies:
            copy.wait_recv()

    def total(self, k):
        at = pl.ds(pl.multiple_of(k * CHUNK, CHUNK), CHUNK)
        first = pl.multiple_of(self.me * self.rows, self.rows)
        value = self.part[pl.ds(pl.multiple_of(first + k * CHUNK, CHUNK), CHUNK), :].astype(F32)
        value = value + self.near[0, at, :].astype(F32)
        for step in range(1, self.chips):
            value = value + self.far[step, at, :].astype(F32)
        return value

    def drain(self):
        for copy in list(self.near_copies.values()) + self.far_copies:
            copy.wait_send()


def chunk_rows(k):
    return pl.ds(pl.multiple_of(k * CHUNK, CHUNK), CHUNK)


def vmem_specs(count):
    return [pl.BlockSpec(memory_space=pltpu.VMEM)] * count


def comm_params(collective_id):
    return pltpu.CompilerParams(
        collective_id=collective_id, has_side_effects=True, vmem_limit_bytes=VMEM_LIMIT
    )


def gather_kernel(columns, block, docs, full, docs_full, *scratch):
    chips = columns // 2
    docs_send, docs_recv, docs_local = scratch[-3:]
    greet(columns)
    gather = Gather(block, full, chips, scratch[:-3])
    me = lax.axis_index("context")
    mine = docs_full.at[pl.ds(me, 1), :]
    copies = [
        send(docs, mine, docs_send.at[step], docs_recv.at[step], {"context": lax.rem(me + step, columns)})
        for step in range(1, columns)
    ]
    local = pltpu.make_async_copy(docs, mine, docs_local)
    local.start()
    gather.finish()
    for copy in copies:
        copy.wait_recv()
    for copy in copies:
        copy.wait_send()
    local.wait()


def gather_first(block, docs, columns):
    rows, width = block.shape
    return pl.pallas_call(
        functools.partial(gather_kernel, columns),
        out_shape=(
            jax.ShapeDtypeStruct((columns * rows, width), BF),
            jax.ShapeDtypeStruct((columns, docs.shape[1]), jnp.int32),
        ),
        in_specs=vmem_specs(2),
        out_specs=(pl.BlockSpec(memory_space=pl.ANY), pl.BlockSpec(memory_space=pl.ANY)),
        scratch_shapes=[
            *Gather.scratch(columns // 2),
            pltpu.SemaphoreType.DMA((columns,)),
            pltpu.SemaphoreType.DMA((columns,)),
            pltpu.SemaphoreType.DMA,
        ],
        compiler_params=comm_params(1),
        name="gather_first",
        cost_estimate=pl.CostEstimate(flops=0, bytes_accessed=60_000_000, transcendentals=0),
    )(block, docs)


def gather_plain_kernel(columns, block, full, *scratch):
    greet(columns)
    gather = Gather(block, full, columns // 2, scratch)
    gather.finish()


def gather_plain(block, columns):
    rows, width = block.shape
    return pl.pallas_call(
        functools.partial(gather_plain_kernel, columns),
        out_shape=jax.ShapeDtypeStruct((columns * rows, width), BF),
        in_specs=vmem_specs(1),
        out_specs=pl.BlockSpec(memory_space=pl.ANY),
        scratch_shapes=Gather.scratch(columns // 2),
        compiler_params=comm_params(2),
        name="gather_plain",
        cost_estimate=pl.CostEstimate(flops=0, bytes_accessed=60_000_000, transcendentals=0),
    )(block)


def middle_kernel(columns, part, x_ref, gain_ref, middle_ref, full, hidden, *scratch):
    chips = columns // 2
    rows = x_ref.shape[0]
    greet(columns)
    reduce = Reduce(part, chips, rows, scratch[:7])
    reduce.exchange()
    reduce.arrive()

    @pl.loop(0, rows // CHUNK)
    def finish(k):
        at = chunk_rows(k)
        middle = x_ref[at, :].astype(F32) + reduce.total(k)
        middle_ref[at, :] = middle
        hidden[at, :] = (middle * rms_scale(middle) * (1.0 + gain_ref[...])).astype(BF)

    gather = Gather(hidden, full, chips, scratch[7:])
    gather.finish()
    reduce.drain()


def middle_step(part, x_own, gain_row, columns):
    rows, width = x_own.shape
    chips = columns // 2
    return pl.pallas_call(
        functools.partial(middle_kernel, columns),
        out_shape=(
            jax.ShapeDtypeStruct((rows, width), F32),
            jax.ShapeDtypeStruct((columns * rows, width), BF),
        ),
        in_specs=vmem_specs(3),
        out_specs=(pl.BlockSpec(memory_space=pltpu.VMEM), pl.BlockSpec(memory_space=pl.ANY)),
        scratch_shapes=[
            pltpu.VMEM((rows, width), BF),
            *Reduce.scratch(chips, rows, width),
            *Gather.scratch(chips),
        ],
        compiler_params=comm_params(3),
        name="middle_step",
        cost_estimate=pl.CostEstimate(flops=0, bytes_accessed=150_000_000, transcendentals=0),
    )(part, x_own, gain_row)


def turn_kernel(columns, part, middle_ref, dy_ref, gain_ref, grad_ref, sums_ref, full, grad_bf, *scratch):
    chips = columns // 2
    rows = middle_ref.shape[0]
    greet(columns)
    reduce = Reduce(part, chips, rows, scratch[:7])
    sums_ref[...] = jnp.zeros_like(sums_ref)
    reduce.exchange()
    reduce.arrive()

    @pl.loop(0, rows // CHUNK)
    def finish(k):
        at = chunk_rows(k)
        grad_hidden = reduce.total(k)
        middle = middle_ref[at, :]
        scale = rms_scale(middle)
        normed = middle * scale
        sums_ref[0:1, :] += jnp.sum(grad_hidden * normed, axis=0, keepdims=True)
        grad = dy_ref[at, :].astype(F32) + norm_backward(grad_hidden, normed, scale, gain_ref[...])
        grad_ref[at, :] = grad
        grad_bf[at, :] = grad.astype(BF)

    gather = Gather(grad_bf, full, chips, scratch[7:])
    gather.finish()
    reduce.drain()


def turn_step(part, middle, dy_own, gain_row, columns):
    rows, width = middle.shape
    chips = columns // 2
    return pl.pallas_call(
        functools.partial(turn_kernel, columns),
        out_shape=(
            jax.ShapeDtypeStruct((rows, width), F32),
            jax.ShapeDtypeStruct((8, width), F32),
            jax.ShapeDtypeStruct((columns * rows, width), BF),
        ),
        in_specs=vmem_specs(4),
        out_specs=(*vmem_specs(2), pl.BlockSpec(memory_space=pl.ANY)),
        scratch_shapes=[
            pltpu.VMEM((rows, width), BF),
            *Reduce.scratch(chips, rows, width),
            *Gather.scratch(chips),
        ],
        compiler_params=comm_params(4),
        name="turn_step",
        cost_estimate=pl.CostEstimate(flops=0, bytes_accessed=150_000_000, transcendentals=0),
    )(part, middle, dy_own, gain_row)


def last_kernel(
    columns,
    layers,
    part_in,
    part_out,
    x_ref,
    middle_ref,
    grad_ref,
    gain_ref,
    sums_ref,
    input_grad_ref,
    block_out_ref,
    gains_ref,
    own_sums,
    plane_slots,
    plane_sums,
    line_slots,
    plane_send,
    plane_recv,
    line_send,
    line_recv,
    *scratch,
):
    chips = columns // 2
    rows = x_ref.shape[0]
    greet(columns, layers)
    first = Reduce(part_in, chips, rows, scratch[:7])
    second = Reduce(part_out, chips, rows, scratch[7:])
    first.exchange()
    second.exchange()
    own_sums[...] = jnp.zeros_like(own_sums)
    own_sums[1:2, :] = sums_ref[0:1, :]
    first.arrive()

    @pl.loop(0, rows // CHUNK)
    def finish(k):
        at = chunk_rows(k)
        grad_hidden = first.total(k)
        residual = x_ref[at, :].astype(F32)
        scale = rms_scale(residual)
        normed = residual * scale
        own_sums[0:1, :] += jnp.sum(grad_hidden * normed, axis=0, keepdims=True)
        input_grad_ref[at, :] = grad_ref[at, :] + norm_backward(
            grad_hidden, normed, scale, gain_ref[...]
        )

    me = lax.axis_index("context")
    layer = lax.axis_index("fsdp")
    in_plane = [
        send(
            own_sums,
            plane_slots.at[step],
            plane_send.at[step],
            plane_recv.at[step],
            {"context": lax.rem(me + step, columns)},
        )
        for step in range(1, columns)
    ]
    second.arrive()

    @pl.loop(0, rows // CHUNK)
    def finish_out(k):
        at = chunk_rows(k)
        block_out_ref[at, :] = middle_ref[at, :] + second.total(k)

    total = own_sums[...]
    for step, copy in enumerate(in_plane):
        copy.wait_recv()
        total = total + plane_slots[step + 1]
    plane_sums[...] = total
    in_line = [
        send(
            plane_sums,
            line_slots.at[step],
            line_send.at[step],
            line_recv.at[step],
            {"fsdp": lax.rem(layer + step, layers)},
        )
        for step in range(1, layers)
    ]
    for step, copy in enumerate(in_line):
        copy.wait_recv()
        total = total + line_slots[step + 1]
    gains_ref[...] = total
    for copy in in_plane + in_line:
        copy.wait_send()
    first.drain()
    second.drain()


def last_step(part_in, part_out, x_own, middle, grad_middle, gain_row, sums, columns, layers):
    rows, width = x_own.shape
    chips = columns // 2
    return pl.pallas_call(
        functools.partial(last_kernel, columns, layers),
        out_shape=(
            jax.ShapeDtypeStruct((rows, width), F32),
            jax.ShapeDtypeStruct((rows, width), F32),
            jax.ShapeDtypeStruct((8, width), F32),
        ),
        in_specs=vmem_specs(7),
        out_specs=tuple(vmem_specs(3)),
        scratch_shapes=[
            pltpu.VMEM((8, width), F32),
            pltpu.VMEM((columns, 8, width), F32),
            pltpu.VMEM((8, width), F32),
            pltpu.VMEM((layers, 8, width), F32),
            pltpu.SemaphoreType.DMA((columns,)),
            pltpu.SemaphoreType.DMA((columns,)),
            pltpu.SemaphoreType.DMA((layers,)),
            pltpu.SemaphoreType.DMA((layers,)),
            *Reduce.scratch(chips, rows, width),
            *Reduce.scratch(chips, rows, width),
        ],
        compiler_params=comm_params(5),
        name="last_step",
        cost_estimate=pl.CostEstimate(flops=0, bytes_accessed=150_000_000, transcendentals=0),
    )(part_in, part_out, x_own, middle, grad_middle, gain_row, sums)


def turned(heads, low):
    return jnp.where(low, pltpu.roll(heads, LANES - HEAD_SIZE // 2, 1), pltpu.roll(heads, HEAD_SIZE // 2, 1))


def allowed_tile(start_ref, row_first, col_first):
    rows = row_first + lax.broadcasted_iota(jnp.int32, (TILE, TILE), 0)
    cols = col_first + lax.broadcasted_iota(jnp.int32, (TILE, TILE), 1)
    starts = jnp.broadcast_to(start_ref[row_first : row_first + TILE, 0:1], (TILE, TILE))
    return (cols <= rows) & (cols >= starts)


def attend_kernel(
    heads, h_ref, w_ref, cos_ref, sin_ref, start_ref, q_ref, k_ref, v_ref, att_ref, log_ref, part_ref, pad_ref
):
    seq = h_ref.shape[0]
    scale = HEAD_SIZE**-0.5
    for slot in range(2 * heads + 2):
        pad_ref[slot * LANES : slot * LANES + HEAD_SIZE, :] = w_ref[
            slot * HEAD_SIZE : (slot + 1) * HEAD_SIZE, :
        ]
        pad_ref[slot * LANES + HEAD_SIZE : (slot + 1) * LANES, :] = jnp.zeros(
            (LANES - HEAD_SIZE, w_ref.shape[1]), BF
        )
    width = (heads + 2) * LANES

    @pl.loop(0, seq // TILE)
    def project(i):
        at = pl.ds(pl.multiple_of(i * TILE, TILE), TILE)
        low = lax.broadcasted_iota(jnp.int32, (TILE, LANES), 1) < HEAD_SIZE // 2
        projected = product_transposed(h_ref[at, :], pad_ref[0:width, :])
        cosine, sine = cos_ref[at, :], sin_ref[at, :]
        for head in range(heads + 1):
            u = projected[:, head * LANES : (head + 1) * LANES]
            r = (u * cosine + turned(u, low) * sine).astype(BF)
            if head < heads:
                q_ref[at, head * LANES : (head + 1) * LANES] = r
            else:
                k_ref[at, :] = r
        v_ref[at, :] = projected[:, (heads + 1) * LANES :].astype(BF)

    for i in range(seq // TILE):
        rows = slice(i * TILE, (i + 1) * TILE)
        for head in range(heads):
            lanes = slice(head * LANES, (head + 1) * LANES)
            q = q_ref[rows, lanes]
            out = jnp.zeros((TILE, LANES), F32)
            total = jnp.zeros((TILE, 1), F32)
            for j in range(i + 1):
                keys = slice(j * TILE, (j + 1) * TILE)
                s = product_transposed(q, k_ref[keys, :]) * scale
                e = jnp.where(allowed_tile(start_ref, i * TILE, j * TILE), jnp.exp(s), 0.0)
                total = total + jnp.sum(e, axis=1, keepdims=True)
                out = out + plain_times(e.astype(BF), v_ref[keys, :])
            att_ref[rows, lanes] = (out / total).astype(BF)
            log_ref[rows, lanes] = jnp.broadcast_to(jnp.log(total), (TILE, LANES))

    @pl.loop(0, seq // TILE)
    def project_out(i):
        at = pl.ds(pl.multiple_of(i * TILE, TILE), TILE)
        part_ref[at, :] = plain_times(att_ref[at, :], pad_ref[width:, :]).astype(BF)


def attend(h_full, w_col, cosine, sine, starts, heads):
    seq, width = h_full.shape
    return pl.pallas_call(
        functools.partial(attend_kernel, heads),
        out_shape=(
            jax.ShapeDtypeStruct((seq, heads * LANES), BF),
            jax.ShapeDtypeStruct((seq, LANES), BF),
            jax.ShapeDtypeStruct((seq, LANES), BF),
            jax.ShapeDtypeStruct((seq, heads * LANES), BF),
            jax.ShapeDtypeStruct((seq, heads * LANES), F32),
            jax.ShapeDtypeStruct((seq, width), BF),
            jax.ShapeDtypeStruct(((2 * heads + 2) * LANES, width), BF),
        ),
        in_specs=vmem_specs(5),
        out_specs=tuple(vmem_specs(7)),
        compiler_params=pltpu.CompilerParams(vmem_limit_bytes=VMEM_LIMIT),
        name="attend",
        cost_estimate=pl.CostEstimate(flops=6_000_000_000, bytes_accessed=20_000_000, transcendentals=2_000_000),
    )(h_full, w_col, cosine, sine, starts)


def attend_back_kernel(
    heads,
    grad_ref,
    pad_ref,
    cos_ref,
    sin_ref,
    start_ref,
    q_ref,
    k_ref,
    v_ref,
    att_ref,
    log_ref,
    out_ref,
    ga_ref,
    dk_ref,
    dv_ref,
):
    seq = grad_ref.shape[0]
    scale = HEAD_SIZE**-0.5
    width = (heads + 2) * LANES

    @pl.loop(0, seq // TILE)
    def attended_gradient(i):
        at = pl.ds(pl.multiple_of(i * TILE, TILE), TILE)
        ga_ref[at, :] = product_transposed(grad_ref[at, :], pad_ref[width:, :]).astype(BF)

    dk_ref[...] = jnp.zeros_like(dk_ref)
    dv_ref[...] = jnp.zeros_like(dv_ref)
    low = lax.broadcasted_iota(jnp.int32, (TILE, LANES), 1) < HEAD_SIZE // 2

    def turn_back(u, rows):
        return (u * cos_ref[rows, :] - turned(u, low) * sin_ref[rows, :]).astype(BF)

    for i in range(seq // TILE):
        rows = slice(i * TILE, (i + 1) * TILE)
        for head in range(heads):
            lanes = slice(head * LANES, (head + 1) * LANES)
            q = q_ref[rows, lanes]
            ga = ga_ref[rows, lanes]
            delta = jnp.sum(ga.astype(F32) * att_ref[rows, lanes].astype(F32), axis=1, keepdims=True)
            logs = log_ref[rows, head * LANES : head * LANES + 1]
            dq = jnp.zeros((TILE, LANES), F32)
            for j in range(i + 1):
                keys = slice(j * TILE, (j + 1) * TILE)
                s = product_transposed(q, k_ref[keys, :]) * scale
                p = jnp.where(allowed_tile(start_ref, i * TILE, j * TILE), jnp.exp(s - logs), 0.0)
                dp = product_transposed(ga, v_ref[keys, :])
                ds = (p * (dp - delta) * scale).astype(BF)
                dq = dq + plain_times(ds, k_ref[keys, :])
                dk_ref[keys, :] += transposed_times(ds, q)
                dv_ref[keys, :] += transposed_times(p.astype(BF), ga)
            out_ref[rows, lanes] = turn_back(dq, rows)
    for i in range(seq // TILE):
        rows = slice(i * TILE, (i + 1) * TILE)
        out_ref[rows, heads * LANES : (heads + 1) * LANES] = turn_back(dk_ref[rows, :], rows)
        out_ref[rows, (heads + 1) * LANES :] = dv_ref[rows, :].astype(BF)


def attend_back(grad_full, padded, cosine, sine, starts, saved, heads):
    seq = grad_full.shape[0]
    return pl.pallas_call(
        functools.partial(attend_back_kernel, heads),
        out_shape=jax.ShapeDtypeStruct((seq, (heads + 2) * LANES), BF),
        in_specs=vmem_specs(10),
        out_specs=pl.BlockSpec(memory_space=pltpu.VMEM),
        scratch_shapes=[
            pltpu.VMEM((seq, heads * LANES), BF),
            pltpu.VMEM((seq, LANES), F32),
            pltpu.VMEM((seq, LANES), F32),
        ],
        compiler_params=pltpu.CompilerParams(vmem_limit_bytes=VMEM_LIMIT),
        name="attend_back",
        cost_estimate=pl.CostEstimate(flops=8_000_000_000, bytes_accessed=20_000_000, transcendentals=2_000_000),
    )(grad_full, padded, cosine, sine, starts, *saved)


def rope_tables(positions):
    half_width = HEAD_SIZE // 2
    frequency = ROPE_THETA ** (-2.0 * jnp.arange(half_width, dtype=F32) / HEAD_SIZE)
    angles = positions.astype(F32)[:, None] * frequency[None, :]
    cosine, sine = jnp.cos(angles), jnp.sin(angles)
    blank = jnp.zeros((positions.shape[0], LANES - HEAD_SIZE), F32)
    return (
        jnp.concatenate([cosine, cosine, blank], axis=1),
        jnp.concatenate([-sine, sine, blank], axis=1),
    )


def unpadded(rows, count):
    return jnp.concatenate([rows[k * LANES : k * LANES + HEAD_SIZE] for k in range(count)])


def on_device(
    block_input,
    cotangent,
    documents,
    attn_weights,
    ffn_weights,
    norm_gains,
    attn_moments,
    ffn_moments,
    gain_moments,
):
    layers, columns = lax.axis_size("fsdp"), lax.axis_size("context")
    rows, width = block_input.shape[1:]
    seq = rows * columns
    heads = QUERY_HEADS // columns
    sharers = max(1, columns // KEY_VALUE_HEADS)
    share = KEY_VALUE_HEADS * HEAD_SIZE // columns
    hidden = ffn_weights.shape[0] * layers // 3
    grad_factor = float(rows * layers * columns) ** (-0.5)
    attn_plan, ffn_plan = unit_plans(
        layers, columns, attn_weights.shape[0] * layers * columns, ffn_weights.shape[0] * layers * columns
    )
    core = lax.rem(lax.axis_index("context"), 2)
    swap = [(c, c + 1 - 2 * (c % 2)) for c in range(columns)]

    attn_col = lax.all_gather(
        attn_plan.spread(attn_weights.astype(BF)), "fsdp", axis=0, tiled=True
    )
    ffn_col = lax.all_gather(ffn_plan.spread(ffn_weights.astype(BF)), "fsdp", axis=0, tiled=True)
    query_rows = heads * HEAD_SIZE
    if sharers > 1:
        own_part = attn_col[query_rows : query_rows + 2 * share]
        other = lax.ppermute(own_part, "context", swap)

        def whole_head(first):
            mine, theirs = own_part[first : first + share], other[first : first + share]
            return jnp.where(
                core == 0, jnp.concatenate([mine, theirs]), jnp.concatenate([theirs, mine])
            )

        attn_col = jnp.concatenate(
            [
                attn_col[:query_rows],
                whole_head(0),
                whole_head(share),
                attn_col[query_rows + 2 * share :],
            ]
        )
    w_gate, w_up, w_down = ffn_col[:hidden], ffn_col[hidden : 2 * hidden], ffn_col[2 * hidden :]

    x_own = block_input[0]
    residual = x_own.astype(F32)
    first_hidden = (residual * rms_scale(residual) * (1.0 + norm_gains[0])).astype(BF)
    h_full, docs_full = gather_first(first_hidden, documents, columns)
    all_docs = docs_full.reshape(seq)
    starts = jnp.sum((all_docs[None, :] < all_docs[:, None]).astype(jnp.int32), axis=1)
    cosine, sine = rope_tables(jnp.arange(seq, dtype=jnp.int32) - starts)
    start_lanes = jnp.broadcast_to(starts[:, None], (seq, LANES))
    q_all, k_all, v_all, attended, logs, part, padded = attend(
        h_full, attn_col, cosine, sine, start_lanes, heads
    )
    middle, h2_full = middle_step(part, x_own, norm_gains[1:2], columns)
    dy_full = gather_plain(cotangent[0], columns)

    gate_pre = product_transposed(h2_full, w_gate)
    up_pre = product_transposed(h2_full, w_up)
    sigmoid_gate = jax.nn.sigmoid(gate_pre)
    activated = (gate_pre * sigmoid_gate * up_pre).astype(BF)
    grad_act = product_transposed(dy_full, w_down)
    grad_gate = (grad_act * up_pre * sigmoid_gate * (1.0 + gate_pre * (1.0 - sigmoid_gate))).astype(BF)
    grad_up = (grad_act * gate_pre * sigmoid_gate).astype(BF)
    ffn_term = jnp.concatenate(
        [
            (transposed_times(grad_gate, h2_full) * grad_factor).astype(BF),
            (transposed_times(grad_up, h2_full) * grad_factor).astype(BF),
            (transposed_times(activated, dy_full) * grad_factor).astype(BF),
        ]
    )
    ffn_sum = lax.psum_scatter(ffn_term, "fsdp", scatter_dimension=0, tiled=True)
    out_part = plain_times(activated, w_down).astype(BF)
    back_part = (plain_times(grad_gate, w_gate) + plain_times(grad_up, w_up)).astype(BF)
    grad_middle, sums, gm_full = turn_step(back_part, middle, cotangent[0], norm_gains[1:2], columns)

    grads = attend_back(
        gm_full, padded, cosine, sine, start_lanes, (q_all, k_all, v_all, attended, logs), heads
    )
    if sharers > 1:
        shared = grads[:, heads * LANES :]
        shared = (shared.astype(F32) + lax.ppermute(shared, "context", swap).astype(F32)).astype(BF)
        lane = jnp.arange(2 * LANES, dtype=jnp.int32) % LANES // share
        grads = jnp.concatenate(
            [grads[:, : heads * LANES], jnp.where(lane == core, shared, jnp.zeros_like(shared))], axis=1
        )
    term_in = (transposed_times(grads, h_full) * grad_factor).astype(BF)
    term_out = (transposed_times(attended, gm_full) * grad_factor).astype(BF)
    if sharers > 1:
        own_rows = [
            lax.dynamic_slice_in_dim(term_in, (heads + k) * LANES + core * share, share, 0)
            for k in range(2)
        ]
        attn_term = jnp.concatenate(
            [unpadded(term_in, heads), *own_rows, unpadded(term_out, heads)]
        )
    else:
        attn_term = jnp.concatenate([unpadded(term_in, heads + 2), unpadded(term_out, heads)])
    attn_sum = lax.psum_scatter(attn_term, "fsdp", scatter_dimension=0, tiled=True)
    in_part = plain_times(grads, padded[: (heads + 2) * LANES]).astype(BF)
    grad_input, block_out, gain_sums = last_step(
        in_part, out_part, x_own, middle, grad_middle, norm_gains[0:1], sums, columns, layers
    )

    ffn_shard = ffn_plan.collect(ffn_sum).astype(F32)
    attn_shard = attn_plan.collect(attn_sum).astype(F32)
    column_count = width // (layers * columns)
    first_column = lax.axis_index(EVERY) * column_count
    gain_shard = lax.dynamic_slice_in_dim(gain_sums[:2], first_column, column_count, 1) * grad_factor
    own_gains = lax.dynamic_slice_in_dim(norm_gains, first_column, column_count, 1)
    new_ffn, ffn_states = adamw_update(ffn_weights, ffn_shard, ffn_moments, WEIGHT_DECAY)
    new_attn, attn_states = adamw_update(attn_weights, attn_shard, attn_moments, WEIGHT_DECAY)
    new_gains, gain_states = adamw_update(own_gains, gain_shard, gain_moments, 0.0)
    return (
        block_out[None],
        grad_input[None],
        attn_shard,
        ffn_shard,
        gain_shard,
        new_attn,
        new_ffn,
        new_gains,
        attn_states,
        ffn_states,
        gain_states,
    )


def solution(mesh):
    placed = (
        P("fsdp", "context", None),
        P("fsdp", "context", None),
        P("fsdp", "context"),
        P(EVERY, None),
        P(EVERY, None),
        P(),
        P(None, EVERY, None),
        P(None, EVERY, None),
        P(None, None, EVERY),
    )
    return jax.shard_map(
        on_device,
        mesh=mesh,
        in_specs=placed,
        out_specs=(
            P("fsdp", "context", None),
            P("fsdp", "context", None),
            P(EVERY, None),
            P(EVERY, None),
            P(None, EVERY),
            P(EVERY, None),
            P(EVERY, None),
            P(None, EVERY),
            P(None, EVERY, None),
            P(None, EVERY, None),
            P(None, None, EVERY),
        ),
        check_vma=False,
    )
```

time: 1600 us -> 434 us (0.27)
  the two profiles are of different devices: /device:TPU:0 before, /device:TPU:10 now
where the time goes in v1:
time: 434 us; the launch traced here: 429 us
  Pallas kernels  234 us (54%)
  between operations  55.4 us (13%)
  matrix products  40.2 us (9%)
  starting transfers between devices  34.5 us (8%)
  other arithmetic  23.6 us (5%)
  local copies, waits for them, and re-layouts  21.5 us (5%)
  waiting for transfers between devices  19.4 us (4%)
    pallas_call x1, Pallas kernels, last_step(): pl.pallas_call(functools.partial(last_kernel, columns, layers), out_shape...  61.9 us
    pallas_call x1, Pallas kernels, turn_step(): pl.pallas_call(functools.partial(turn_kernel, columns), out_shape=(jax.Sh...  49.1 us
    pallas_call x1, Pallas kernels, middle_step(): pl.pallas_call(functools.partial(middle_kernel, columns), out_shape=(jax....  47.8 us
    pallas_call x1, Pallas kernels, gather_first(): pl.pallas_call(functools.partial(gather_kernel, columns), out_shape=(jax....  23.9 us
    pallas_call x1, Pallas kernels, gather_plain(): pl.pallas_call(functools.partial(gather_plain_kernel, columns), out_shape...  23.7 us
    ppermute x6, starting transfers between devices, collect(): got.append(lax.ppermute(unit, EVERY, [(b, a) for a, b in pairs]))  18.9 us
    ppermute x6, waiting for transfers between devices, collect(): got.append(lax.ppermute(unit, EVERY, [(b, a) for a, b in pairs]))  17.7 us
    dot_general x4, matrix products, plain_times(): return jnp.dot(left_matrix, right_matrix, preferred_element_type=F32)  15.3 us
  transfers between devices with their start and end apart: 16, of which 6 were waited for; matrix products, arithmetic and copies ran while one was open for 10% of the time, Pallas kernels for 40%

profile of v1, /device:TPU:10, one launch (start us, length us, event | category | flops | bytes accessed | tf_op | source)
XLA Modules:
  0.0 428.5 jit_solution(11562552680363812146)
XLA Ops:
  18.2 2.4 collective-permute-start.5
  20.7 3.5 collective-permute-start.4
  24.2 1.9 collective-permute-start.3
  34.5 4.1 collective-permute-start.2
  38.6 3.2 collective-permute-start
  51.3 23.7 %gather_plain.1 = bf16[1024,1536]{1,0:T(8,128)(2,1)} custom-call(bf16[128,1536]{1,0:T(8,128)(2,1)} %bitcast.153), custom_call_target="tpu_custom_call" | custom-call | bytes 60000000 | tf_op jit(solution)/shard_map/gather_plain/pallas_call | solution.py:378
  76.8 23.9 %gather_first.1 = (bf16[1024,1536]{1,0:T(8,128)(2,1)}, s32[8,128]{1,0:T(8,128)}) custom-call(bf16[128,1536]{1,0:T(8,128)(2,1)} %fusion.41.block, s32[1,128]{1,0:T(1,128)} %docs.1), custom_call_target="tpu_custom_call" | custom-call | bytes 60000000 | tf_op jit(solution)/shard_map/gather_first/pallas_call | solution.py:350
  106.3 13.5 %attend.1 = (bf16[1024,256]{1,0:T(8,128)(2,1)}, bf16[1024,128]{1,0:T(8,128)(2,1)}, bf16[1024,128]{1,0:T(8,128)(2,1)}, bf16[1024,256]{1,0:T(8,128)(2,1)}, f32[102...) custom-call(bf16[1024,1536]{1,0:T(8,128)(2,1)} %get-tuple-element.28.h_ref, ...), custom_call_target="tpu_custom_call" | custom-call | flops 6000000000 | bytes 20000000 | tf_op jit(solution)/shard_map/attend/pallas_call | solution.py:665
  119.8 47.8 %middle_step.1 = (f32[128,1536]{1,0:T(8,128)}, bf16[1024,1536]{1,0:T(8,128)(2,1)}) custom-call(bf16[1024,1536]{1,0:T(8,128)(2,1)} %get-tuple-element.30.part, bf16[128,1536]{1,0:T(8,128)(2,1)} %bitcast.147, f32[1,1536]{1,0:T(1,128)} %get-tuple-element.86.gain_ref), custom_call_target="tpu_custom_call" | custom-call | bytes 150000000 | tf_op jit(solution)/shard_map/middle_step/pallas_call | solution.py:413
  167.7 4.3 %fusion.22 = f32[1024,512]{0,1:T(8,128)S(1)} fusion(bf16[1024,1536]{1,0:T(8,128)(2,1)} %get-tuple-element.31, bf16[1536,1536]{1,0:T(8,128)(2,1)} %all-gather.3.cloned.1.call-done), kind=kOutput, calls=%fused_computation.45 | convolution fusion | flops 1610612736 | bytes 6815744 | tf_op jit(solution)/shard_map/dot_general | solution.py:35
  174.3 3.6 multiply_convert_fusion
  179.7 3.7 add_convert_fusion.part
  183.4 49.1 %turn_step.1 = (f32[128,1536]{1,0:T(8,128)}, f32[8,1536]{1,0:T(8,128)}, bf16[1024,1536]{1,0:T(8,128)(2,1)}) custom-call(bf16[1024,1536]{1,0:T(8,128)(2,1)} %add_convert_fusion.part, f32[128,1536]{1,0:T(8,128)} %get-tuple-element.32.middle_ref, bf16[128,1536]{1,0:T(8,128)(2,1)} %bitcast.154, f32[1,1536]{1,0:T(1,128)} %get-tuple-element.86.gain_ref), custom_call_target="tpu_custom_call" | custom-call | bytes 150000000 | tf_op jit(solution)/shard_map/turn_step/pallas_call | solution.py:461
  232.5 3.8 fusion.4
  236.3 13.8 %attend_back.1 = bf16[1024,512]{1,0:T(8,128)(2,1)} custom-call(bf16[1024,1536]{1,0:T(8,128)(2,1)} %get-tuple-element.33.grad_ref, bf16[768,1536]{1,0:T(8,128)(2,1)} %get-tuple-element.34.pad_ref, f32[1024,128]{1,0:T(8,128)} %get-tuple-element.100.cos_ref, f32[1024,128]{1,0:T(8,128)} %get-tuple-element.99.sin_ref, s32[1024,128]{1,0:T(8,128)} %broadcast_in_dim.9.start_ref, ...), custom_call_target="tpu_custom_call" | custom-call | flops 8000000000 | bytes 20000000 | tf_op jit(solution)/shard_map/attend_back/pallas_call | solution.py:744
  250.1 4.0 fusion
  256.9 3.8 fusion.2
  264.7 2.4 pad_maximum_fusion
  296.2 4.9 %convolution_convert_fusion.1.part_in = bf16[1024,1536]{1,0:T(8,128)(2,1)} fusion(bf16[1024,512]{1,0:T(8,128)(2,1)S(1)} %copy-done.24, bf16[768,1536]{1,0:T(8,128)(2,1)} %get-tuple-element.34.pad_ref), kind=kOutput, calls=%fused_computation.5 | convolution fusion | flops 1612185600 | bytes 5767168 | tf_op jit(solution)/shard_map/dot_general | solution.py:47
  301.1 4.9 %convolution_convert_fusion.part_out = bf16[1024,1536]{1,0:T(8,128)(2,1)} fusion(bf16[1024,512]{0,1:T(8,128)(2,1)S(1)} %copy-done.26, bf16[1536,1536]{1,0:T(8,128)(2,1)} %all-gather.3.cloned.1.call-done), kind=kOutput, calls=%fused_computation.4 | convolution fusion | flops 1612185600 | bytes 5767168 | tf_op jit(solution)/shard_map/dot_general | solution.py:47
  306.0 61.9 %last_step.1 = (f32[128,1536]{1,0:T(8,128)}, f32[128,1536]{1,0:T(8,128)}, f32[8,1536]{1,0:T(8,128)}) custom-call(bf16[1024,1536]{1,0:T(8,128)(2,1)} %convolution_convert_fusion.1.part_in, bf16[1024,1536]{1,0:T(8,128)(2,1)} %convolution_convert_fusion.part_out, bf16[128,1536]{1,0:T(8,128)(2,1)} %bitcast.148, f32[128,1536]{1,0:T(8,128)} %get-tuple-element.32.middle_ref, ...), custom_call_target="tpu_custom_call" | custom-call | bytes 150000000 | tf_op jit(solution)/shard_map/last_step/pallas_call | solution.py:574
  370.0 1.9 collective-permute-start.8
  372.0 3.7 collective-permute-start.7
  375.7 1.9 collective-permute-start.6
  378.9 6.5 %collective-permute-done.8 = bf16[48,1536]{1,0:T(8,128)(2,1)S(1)} collective-permute-done((bf16[48,1536]{1,0:T(8,128)(2,1)S(1)}, bf16[48,1536]{1,0:T(8,128)(2,1)S(1)}, u32[]{:S(2)}, u32[]{:S(2)}) %collective-permute-start.8) | collective-permute-done | bytes 147488 | tf_op jit(solution)/shard_map/ppermute | solution.py:127
  385.4 3.3 collective-permute-done.7
  392.0 9.4 %collective-permute-start.11 = (bf16[128,1536]{1,0:T(8,128)(2,1)S(1)}, bf16[128,1536]{1,0:T(8,128)(2,1)S(1)}, u32[]{:S(2)}, u32[]{:S(2)}) collective-permute-start(bf16[128,1536]{1,0:T(8,128)(2,1)S(1)} %get-tuple-element.63), channel_id=1, source_target_pairs={{0,2},{1,5},{2,0},{3,3},{4,6},{5,1},{6,4},{7,7},{8,10},{9,13},{10,... | collective-permute-start | bytes 1179656 | tf_op jit(solution)/shard_map/ppermute | solution.py:127
  401.5 1.9 collective-permute-start.9
  405.0 4.6 %collective-permute-done.11 = bf16[128,1536]{1,0:T(8,128)(2,1)S(1)} collective-permute-done((bf16[128,1536]{1,0:T(8,128)(2,1)S(1)}, bf16[128,1536]{1,0:T(8,128)(2,1)S(1)}, u32[]{:S(2)}, u32[]{:S(2)}) %collective-permute-start.11) | collective-permute-done | bytes 393248 | tf_op jit(solution)/shard_map/ppermute | solution.py:127
  410.4 2.5 collective-permute-done.9
  414.0 2.5 pad_maximum_fusion.1
  416.5 3.3 multiply_subtract_fusion
  (143 shorter events, 47.3 us)
Async XLA Ops:
  7.2 98.1 %all-gather.5.cloned.1.call-start = ((), (), s32[]{:S(2)}) async-start(), calls=%async_computation.3 | async-start | bytes 2211840 | tf_op jit(solution)/shard_map/all_gather | solution.py:801
  14.9 19.4 %copy-start = (f32[384,1536]{1,0:T(8,128)S(1)}, f32[384,1536]{1,0:T(8,128)}, u32[]{:S(2)}) copy-start(f32[384,1536]{1,0:T(8,128)} %param.29) | copy-start | bytes 7077892
  18.2 15.0 %collective-permute-start.5 = (bf16[48,1536]{1,0:T(8,128)(2,1)S(1)}, bf16[48,1536]{1,0:T(8,128)(2,1)S(1)}, u32[]{:S(2)}, u32[]{:S(2)}) collective-permute-start(bf16[48,1536]{1,0:T(8,128)(2,1)S(1)} %get-tuple-element.81), channel_id=1, source_target_pairs={{0,0},{1,1},{2,2},{4,3},{5,4},{6,5},{8,6},{9,7},{10,8},{11,9},{3,1... | collective-permute-start | bytes 442376 | tf_op jit(solution)/shard_map/ppermute | solution.py:116
  20.7 12.6 %collective-permute-start.4 = (bf16[48,1536]{1,0:T(8,128)(2,1)S(1)}, bf16[48,1536]{1,0:T(8,128)(2,1)S(1)}, u32[]{:S(2)}, u32[]{:S(2)}) collective-permute-start(bf16[48,1536]{1,0:T(8,128)(2,1)S(1)} %get-tuple-element.82), channel_id=1, source_target_pairs={{0,0},{2,1},{3,2},{4,3},{6,4},{7,5},{8,6},{10,7},{1,8},{11,9},{12,... | collective-permute-start | bytes 442376 | tf_op jit(solution)/shard_map/ppermute | solution.py:116
  24.2 9.1 %collective-permute-start.3 = (bf16[48,1536]{1,0:T(8,128)(2,1)S(1)}, bf16[48,1536]{1,0:T(8,128)(2,1)S(1)}, u32[]{:S(2)}, u32[]{:S(2)}) collective-permute-start(bf16[48,1536]{1,0:T(8,128)(2,1)S(1)} %get-tuple-element.80), channel_id=1, source_target_pairs={{0,0},{1,1},{3,2},{4,3},{5,4},{7,5},{8,6},{9,7},{11,8},{2,9},{12,1... | collective-permute-start | bytes 442376 | tf_op jit(solution)/shard_map/ppermute | solution.py:116
  34.2 133.5 %all-gather.3.cloned.1.call-start = ((), (), s32[]{:S(2)}) async-start(), calls=%async_computation.2 | async-start | bytes 5898240 | tf_op jit(solution)/shard_map/all_gather | solution.py:804
  34.5 13.8 %collective-permute-start.2 = (bf16[128,1536]{1,0:T(8,128)(2,1)S(1)}, bf16[128,1536]{1,0:T(8,128)(2,1)S(1)}, u32[]{:S(2)}, u32[]{:S(2)}) collective-permute-start(bf16[128,1536]{1,0:T(8,128)(2,1)S(1)} %get-tuple-element.70), channel_id=1, source_target_pairs={{2,0},{5,1},{0,2},{3,3},{6,4},{1,5},{4,6},{7,7},{10,8},{13,9},{8,1... | collective-permute-start | bytes 1179656 | tf_op jit(solution)/shard_map/ppermute | solution.py:116
  38.5 9.7 %collective-permute-start.1 = (bf16[128,1536]{1,0:T(8,128)(2,1)S(1)}, bf16[128,1536]{1,0:T(8,128)(2,1)S(1)}, u32[]{:S(2)}, u32[]{:S(2)}) collective-permute-start(bf16[128,1536]{1,0:T(8,128)(2,1)S(1)} %get-tuple-element.69), channel_id=1, source_target_pairs={{5,0},{0,1},{3,2},{6,3},{1,4},{4,5},{7,6},{2,7},{13,8},{8,9},{11,1... | collective-permute-start | bytes 1179656 | tf_op jit(solution)/shard_map/ppermute | solution.py:116
  38.6 11.3 %collective-permute-start = (bf16[128,1536]{1,0:T(8,128)(2,1)S(1)}, bf16[128,1536]{1,0:T(8,128)(2,1)S(1)}, u32[]{:S(2)}, u32[]{:S(2)}) collective-permute-start(bf16[128,1536]{1,0:T(8,128)(2,1)S(1)} %get-tuple-element.68), channel_id=1, source_target_pairs={{0,0},{3,1},{6,2},{1,3},{4,4},{7,5},{2,6},{5,7},{8,8},{11,9},{14,1... | collective-permute-start | bytes 1179656 | tf_op jit(solution)/shard_map/ppermute | solution.py:116
  51.2 23.8 %copy-start.3 = (bf16[1,128,1536]{2,1,0:T(8,128)(2,1)S(1)}, bf16[1,128,1536]{2,1,0:T(8,128)(2,1)}, u32[]{:S(2)}) copy-start(bf16[1,128,1536]{2,1,0:T(8,128)(2,1)} %param.25) | copy-start | bytes 1179652
  51.2 24.0 %copy-start.12 = (f32[2,1536]{1,0:T(2,128)S(1)}, f32[2,1536]{1,0:T(2,128)}, u32[]{:S(2)}) copy-start(f32[2,1536]{1,0:T(2,128)} %param.30) | copy-start | bytes 36868
  51.3 317.7 %reduce-scatter.3.cloned.1.call-start = ((), (), s32[]{:S(2)}) async-start(), calls=%async_computation.4 | async-start | bytes 2211840 | tf_op jit(solution)/shard_map/reduce_scatter | solution.py:881
  167.7 4.3 %copy-start.5 = (bf16[1024,1536]{1,0:T(8,128)(2,1)S(1)}, bf16[1024,1536]{1,0:T(8,128)(2,1)}, u32[]{:S(2)}) copy-start(bf16[1024,1536]{1,0:T(8,128)(2,1)} %gather_plain.1) | copy-start | bytes 9437188
  167.7 4.7 %copy-start.10 = (bf16[1536,1536]{1,0:T(8,128)(2,1)S(1)}, bf16[1536,1536]{1,0:T(8,128)(2,1)}, u32[]{:S(2)}) copy-start(bf16[1536,1536]{1,0:T(8,128)(2,1)} %all-gather.3.cloned.1.call-done) | copy-start | bytes 14155780
  183.4 49.1 %copy-start.25 = (bf16[1024,256]{1,0:T(8,128)(2,1)S(1)}, bf16[1024,256]{1,0:T(8,128)(2,1)}, u32[]{:S(2)}) copy-start(bf16[1024,256]{1,0:T(8,128)(2,1)} %get-tuple-element.38.att_ref) | copy-start | bytes 1572868
  256.6 134.1 %reduce-scatter.5.cloned.1.call-start = ((), (), s32[]{:S(2)}) async-start(), calls=%async_computation.5 | async-start | bytes 5898240 | tf_op jit(solution)/shard_map/reduce_scatter | solution.py:854
  267.1 4.4 %copy-start.19 = (s32[32]{0:T(128)S(1)}, s32[32]{0:T(128)}, u32[]{:S(2)}) copy-start(s32[32]{0:T(128)} %constant.181.clone) | copy-start | bytes 388
  267.1 11.5 %copy-start.18 = (s32[32]{0:T(128)S(1)}, s32[32]{0:T(128)}, u32[]{:S(2)}) copy-start(s32[32]{0:T(128)} %constant.176.clone) | copy-start | bytes 388
  267.1 13.4 %copy-start.17 = (s32[32]{0:T(128)S(1)}, s32[32]{0:T(128)}, u32[]{:S(2)}) copy-start(s32[32]{0:T(128)} %constant.178.clone) | copy-start | bytes 388
  267.1 15.3 %copy-start.16 = (s32[32]{0:T(128)S(1)}, s32[32]{0:T(128)}, u32[]{:S(2)}) copy-start(s32[32]{0:T(128)} %constant.177.clone) | copy-start | bytes 388
  267.1 29.1 %copy-start.24 = (bf16[1024,512]{1,0:T(8,128)(2,1)S(1)}, bf16[1024,512]{1,0:T(8,128)(2,1)}, u32[]{:S(2)}) copy-start(bf16[1024,512]{1,0:T(8,128)(2,1)} %attend_back.1) | copy-start | bytes 3145732
  306.0 71.6 %copy-start.13 = (f32[2,2,48]{2,1,0:T(2,128)S(1)}, f32[2,2,48]{2,1,0:T(2,128)}, u32[]{:S(2)}) copy-start(f32[2,2,48]{2,1,0:T(2,128)} %param.33) | copy-start | bytes 2308
  368.0 20.9 %copy-start.2 = (f32[2,144,1536]{2,1,0:T(8,128)S(1)}, f32[2,144,1536]{2,1,0:T(8,128)}, u32[]{:S(2)}) copy-start(f32[2,144,1536]{2,1,0:T(8,128)} %param.31) | copy-start | bytes 5308420
  368.0 20.9 %copy-start.4 = (f32[144,1536]{1,0:T(8,128)S(1)}, f32[144,1536]{1,0:T(8,128)}, u32[]{:S(2)}) copy-start(f32[144,1536]{1,0:T(8,128)} %param.28) | copy-start | bytes 2654212
  370.0 15.4 %collective-permute-start.8 = (bf16[48,1536]{1,0:T(8,128)(2,1)S(1)}, bf16[48,1536]{1,0:T(8,128)(2,1)S(1)}, u32[]{:S(2)}, u32[]{:S(2)}) collective-permute-start(bf16[48,1536]{1,0:T(8,128)(2,1)S(1)} %get-tuple-element.75), channel_id=1, source_target_pairs={{0,0},{1,1},{2,2},{3,4},{4,5},{5,6},{6,8},{7,9},{8,10},{9,11},{10,... | collective-permute-start | bytes 442376 | tf_op jit(solution)/shard_map/ppermute | solution.py:127
  372.0 16.8 %collective-permute-start.7 = (bf16[48,1536]{1,0:T(8,128)(2,1)S(1)}, bf16[48,1536]{1,0:T(8,128)(2,1)S(1)}, u32[]{:S(2)}, u32[]{:S(2)}) collective-permute-start(bf16[48,1536]{1,0:T(8,128)(2,1)S(1)} %get-tuple-element.76), channel_id=1, source_target_pairs={{0,0},{1,2},{2,3},{3,4},{4,6},{5,7},{6,8},{7,10},{8,1},{9,11},{10,... | collective-permute-start | bytes 442376 | tf_op jit(solution)/shard_map/ppermute | solution.py:127
  375.7 13.0 %collective-permute-start.6 = (bf16[48,1536]{1,0:T(8,128)(2,1)S(1)}, bf16[48,1536]{1,0:T(8,128)(2,1)S(1)}, u32[]{:S(2)}, u32[]{:S(2)}) collective-permute-start(bf16[48,1536]{1,0:T(8,128)(2,1)S(1)} %get-tuple-element.74), channel_id=1, source_target_pairs={{0,0},{1,1},{2,3},{3,4},{4,5},{5,7},{6,8},{7,9},{8,11},{9,2},{10,1... | collective-permute-start | bytes 442376 | tf_op jit(solution)/shard_map/ppermute | solution.py:127
  392.0 17.6 %collective-permute-start.11 = (bf16[128,1536]{1,0:T(8,128)(2,1)S(1)}, bf16[128,1536]{1,0:T(8,128)(2,1)S(1)}, u32[]{:S(2)}, u32[]{:S(2)}) collective-permute-start(bf16[128,1536]{1,0:T(8,128)(2,1)S(1)} %get-tuple-element.63), channel_id=1, source_target_pairs={{0,2},{1,5},{2,0},{3,3},{4,6},{5,1},{6,4},{7,7},{8,10},{9,13},{10,... | collective-permute-start | bytes 1179656 | tf_op jit(solution)/shard_map/ppermute | solution.py:127
  401.4 9.0 %collective-permute-start.10 = (bf16[128,1536]{1,0:T(8,128)(2,1)S(1)}, bf16[128,1536]{1,0:T(8,128)(2,1)S(1)}, u32[]{:S(2)}, u32[]{:S(2)}) collective-permute-start(bf16[128,1536]{1,0:T(8,128)(2,1)S(1)} %get-tuple-element.64), channel_id=1, source_target_pairs={{0,5},{1,0},{2,3},{3,6},{4,1},{5,4},{6,7},{7,2},{8,13},{9,8},{10,1... | collective-permute-start | bytes 1179656 | tf_op jit(solution)/shard_map/ppermute | solution.py:127
  401.5 11.4 %collective-permute-start.9 = (bf16[128,1536]{1,0:T(8,128)(2,1)S(1)}, bf16[128,1536]{1,0:T(8,128)(2,1)S(1)}, u32[]{:S(2)}, u32[]{:S(2)}) collective-permute-start(bf16[128,1536]{1,0:T(8,128)(2,1)S(1)} %get-tuple-element.62), channel_id=1, source_target_pairs={{0,0},{1,3},{2,6},{3,1},{4,4},{5,7},{6,2},{7,5},{8,8},{9,11},{10,1... | collective-permute-start | bytes 1179656 | tf_op jit(solution)/shard_map/ppermute | solution.py:127
  403.4 9.7 %slice-start = ((s8[4718592]{0:T(1024)(128)(4,1)}), s8[4194304]{0:T(1024)(128)(4,1)S(1)}, s32[]{:S(2)}) async-start(s8[4718592]{0:T(1024)(128)(4,1)} %bitcast.145), calls=%async_computation.6 | async-start | bytes 8388608
  403.7 9.4 %slice-start.1 = ((s8[4718592]{0:T(1024)(128)(4,1)}), s8[524288]{0:T(1024)(128)(4,1)S(1)}, s32[]{:S(2)}) async-start(s8[4718592]{0:T(1024)(128)(4,1)} %bitcast.145), calls=%async_computation.7 | async-start | bytes 1048576
  (13 other events, 31.3 us)
Sparse Core Ops, SparseCore 0:
  34.3 41.5 all-gather.4
  78.1 86.7 all-gather.2
  256.7 38.3 reduce-scatter.2
  297.9 89.6 reduce-scatter.4

commit v2 on v1

--- a/solution.py
+++ b/solution.py
@@ -128,7 +128,7 @@
         return self._reorder(got, [piece for _, piece, _ in self.rounds])
 
 
-def unit_plans(layers, columns, attn_rows, ffn_rows):
+def unit_plans(layers, columns, attn_rows):
     devices = layers * columns
 
     def home(column, position):
@@ -153,6 +153,64 @@
     return UnitPlan(homes, devices), ffn_plan
 
 
+class Homes:
+    def __init__(self, layers, columns, attn_rows):
+        devices = layers * columns
+        unit_rows = attn_rows // (3 * devices)
+        self.layers, self.columns = layers, columns
+        self.counts = [
+            QUERY_HEADS * HEAD_SIZE // columns // unit_rows,
+            KEY_VALUE_HEADS * HEAD_SIZE // columns // unit_rows,
+        ]
+        query, share = self.counts
+        self.first = [0, query, query + share, query + 2 * share]
+        self.sizes = [query, share, share, query]
+
+    def _spot(self, column, position):
+        return position // 3, column, position % 3
+
+    def attn_targets(self):
+        device = lax.axis_index("fsdp") * self.columns + lax.axis_index("context")
+        found = []
+        for piece in range(3):
+            unit = device * 3 + piece
+            column, position = 0, 0
+            for first, size in zip(self.first, self.sizes):
+                inside = unit - first * self.columns
+                begun = inside >= 0
+                column = jnp.where(begun, inside // size, column)
+                position = jnp.where(begun, first + inside % size, position)
+            found.append(self._spot(column, position))
+        return found
+
+    def attn_owners(self):
+        column = lax.axis_index("context")
+        found = []
+        for place in range(3):
+            position = lax.axis_index("fsdp") * 3 + place
+            unit = 0
+            for first, size in zip(self.first, self.sizes):
+                inside = position - first
+                unit = jnp.where(inside >= 0, first * self.columns + column * size + inside, unit)
+            device = unit // 3
+            found.append((device // self.columns, device % self.columns, unit % 3))
+        return found
+
+    def ffn_targets(self):
+        layer, column = lax.axis_index("fsdp"), lax.axis_index("context")
+        return [
+            (layer, (3 * column + piece) % self.columns, (3 * column + piece) // self.columns)
+            for piece in range(3)
+        ]
+
+    def ffn_owners(self):
+        layer, column = lax.axis_index("fsdp"), lax.axis_index("context")
+        return [
+            (layer, (place * self.columns + column) // 3, (place * self.columns + column) % 3)
+            for place in range(3)
+        ]
+
+
 def partner(me, step, chips):
     return lax.rem(me // 2 + step, chips) * 2 + lax.rem(me, 2)
 
@@ -165,9 +223,20 @@
     return pl.ds(pl.multiple_of(index * rows, rows), rows)
 
 
-def greet(columns, layers=1):
+def greet(columns, layers=1, others=()):
     barrier = pltpu.get_barrier_semaphore()
     me = lax.axis_index("context")
+    awaited = columns - 1 + layers - 1
+    for layer, column in others:
+        apart = (layer != lax.axis_index("fsdp")) | (column != me)
+        awaited = awaited + jnp.where(apart, 1, 0)
+
+        @pl.when(apart)
+        def there():
+            pl.semaphore_signal(
+                barrier, inc=1, device_id={"fsdp": layer, "context": column}, device_id_type=ID_TYPE
+            )
+
     for step in range(1, columns):
         pl.semaphore_signal(
             barrier, inc=1, device_id={"context": lax.rem(me + step, columns)}, device_id_type=ID_TYPE
@@ -178,7 +247,7 @@
             pl.semaphore_signal(
                 barrier, inc=1, device_id={"fsdp": lax.rem(layer + step, layers)}, device_id_type=ID_TYPE
             )
-    pl.semaphore_wait(barrier, columns - 1 + layers - 1)
+    pl.semaphore_wait(barrier, awaited)
 
 
 def send(source, target, send_sem, recv_sem, device):
@@ -192,6 +261,220 @@
     )
     copy.start()
     return copy
+
+
+def remote(source, target, send_sem, recv_sem, device):
+    return pltpu.make_async_remote_copy(
+        src_ref=source,
+        dst_ref=target,
+        send_sem=send_sem,
+        recv_sem=recv_sem,
+        device_id=device,
+        device_id_type=ID_TYPE,
+    )
+
+
+class Exchange:
+    @staticmethod
+    def scratch():
+        return [pltpu.SemaphoreType.DMA((3,)), pltpu.SemaphoreType.DMA((3,))]
+
+    def __init__(self, sources, targets, homes, sems):
+        send_sem, recv_sem = sems
+        self.parts = []
+        for i, (layer, column, place) in enumerate(homes):
+            itself = (layer == lax.axis_index("fsdp")) & (column == lax.axis_index("context"))
+            target = targets(layer, place)
+            copy = functools.partial(
+                remote,
+                sources[i],
+                target,
+                send_sem.at[i],
+                recv_sem.at[place],
+                {"fsdp": layer, "context": column},
+            )
+            stay = functools.partial(pltpu.make_async_copy, sources[i], target, recv_sem.at[place])
+
+            @pl.when(itself)
+            def here():
+                stay().start()
+
+            @pl.when(jnp.logical_not(itself))
+            def there():
+                copy().start()
+
+            self.parts.append((itself, copy))
+        self.landing = [
+            functools.partial(pltpu.make_async_copy, sources[k], sources[k], recv_sem.at[k])
+            for k in range(3)
+        ]
+
+    def arrive(self):
+        for landed in self.landing:
+            landed().wait()
+
+    def drain(self):
+        for itself, copy in self.parts:
+
+            @pl.when(jnp.logical_not(itself))
+            def sent():
+                copy().wait_send()
+
+
+class LineGather:
+    @staticmethod
+    def scratch(layers):
+        return [pltpu.SemaphoreType.DMA((layers - 1,))] * 4
+
+    def __init__(self, full, rows, layers, sems, own):
+        self.full, self.rows, self.layers, self.sems, self.own = full, rows, layers, sems, own
+
+    def _moves(self, k):
+        layer = lax.axis_index("fsdp")
+        up_send, up_recv, down_send, down_recv = self.sems
+        top = self.layers - 1
+        for first, last, other, shard, send_sem, recv_sem in (
+            (layer - k >= 0, layer < top, layer + 1, layer - k, up_send, up_recv),
+            (layer + k <= top, layer > 0, layer - 1, layer + k, down_send, down_recv),
+        ):
+            block = self.full.at[rows_at(shard, self.rows), :]
+            yield first & last, functools.partial(
+                remote, self.own if k == 0 else block, block, send_sem.at[k], recv_sem.at[k], {"fsdp": other}
+            )
+
+    def _landed(self, k):
+        layer = lax.axis_index("fsdp")
+        _, up_recv, _, down_recv = self.sems
+        for there, shard, recv_sem in (
+            (layer - 1 - k >= 0, layer - 1 - k, up_recv),
+            (layer + 1 + k <= self.layers - 1, layer + 1 + k, down_recv),
+        ):
+            block = self.full.at[rows_at(shard, self.rows), :]
+            yield there, functools.partial(pltpu.make_async_copy, block, block, recv_sem.at[k])
+
+    def step(self, k):
+        if k > 0:
+            for there, copy in self._landed(k - 1):
+
+                @pl.when(there)
+                def landed():
+                    copy().wait()
+
+        if k < self.layers - 1:
+            for go, copy in self._moves(k):
+
+                @pl.when(go)
+                def start():
+                    copy().start()
+
+    def drain(self):
+        for k in range(self.layers - 1):
+            for go, copy in self._moves(k):
+
+                @pl.when(go)
+                def sent():
+                    copy().wait_send()
+
+
+class LineReduce:
+    @staticmethod
+    def scratch(layers, rows, width):
+        return [
+            pltpu.VMEM((layers - 1, rows, width), BF),
+            pltpu.VMEM((layers - 1, rows, width), BF),
+            *[pltpu.SemaphoreType.DMA((layers - 1,))] * 4,
+        ]
+
+    def __init__(self, term, rows, layers, scratch):
+        self.term, self.rows, self.layers = term, rows, layers
+        self.up_in, self.down_in, *self.sems = scratch
+        layer = lax.axis_index("fsdp")
+        top = layers - 1
+        up_send, up_recv, down_send, down_recv = self.sems
+
+        @pl.when(layer == 0)
+        def bottom():
+            for k in range(top):
+                self._up(k, self.term.at[pl.ds((top - k) * rows, rows), :]).start()
+
+        @pl.when(layer == top)
+        def ceiling():
+            for k in range(top):
+                self._down(k, self.term.at[pl.ds(k * rows, rows), :]).start()
+
+    def _up(self, k, source):
+        up_send, up_recv, _, _ = self.sems
+        other = {"fsdp": lax.axis_index("fsdp") + 1}
+        return remote(source, self.up_in.at[k], up_send.at[k], up_recv.at[k], other)
+
+    def _down(self, k, source):
+        _, _, down_send, down_recv = self.sems
+        other = {"fsdp": lax.axis_index("fsdp") - 1}
+        return remote(source, self.down_in.at[k], down_send.at[k], down_recv.at[k], other)
+
+    def _add(self, sums, k, target):
+        @pl.loop(0, self.rows // CHUNK)
+        def add(c):
+            at = chunk_rows(c)
+            of_term = pl.ds(target * self.rows + pl.multiple_of(c * CHUNK, CHUNK), CHUNK)
+            sums[k, at, :] = (
+                sums[k, at, :].astype(F32) + self.term[of_term, :].astype(F32)
+            ).astype(BF)
+
+    def step(self, k):
+        layer = lax.axis_index("fsdp")
+        top = self.layers - 1
+        _, up_recv, _, down_recv = self.sems
+        target = top - k
+
+        @pl.when((layer > 0) & (layer <= target))
+        def from_below():
+            pltpu.make_async_copy(self.up_in.at[k], self.up_in.at[k], up_recv.at[k]).wait()
+
+        @pl.when((layer > 0) & (layer < target))
+        def pass_up():
+            self._add(self.up_in, k, target)
+            self._up(k, self.up_in.at[k]).start()
+
+        @pl.when((layer < top) & (layer >= k))
+        def from_above():
+            pltpu.make_async_copy(self.down_in.at[k], self.down_in.at[k], down_recv.at[k]).wait()
+
+        @pl.when((layer < top) & (layer > k))
+        def pass_down():
+            self._add(self.down_in, k, k)
+            self._down(k, self.down_in.at[k]).start()
+
+    def finish(self, total):
+        layer = lax.axis_index("fsdp")
+        top = self.layers - 1
+        for own in range(self.layers):
+
+            @pl.when(layer == own)
+            def here():
+                @pl.loop(0, self.rows // CHUNK)
+                def add(c):
+                    at = chunk_rows(c)
+                    of_term = pl.ds(own * self.rows + pl.multiple_of(c * CHUNK, CHUNK), CHUNK)
+                    value = self.term[of_term, :].astype(F32)
+                    if own > 0:
+                        value = value + self.up_in[top - own, at, :].astype(F32)
+                    if own < top:
+                        value = value + self.down_in[own, at, :].astype(F32)
+                    total[at, :] = value.astype(BF)
+
+    def drain(self):
+        layer = lax.axis_index("fsdp")
+        top = self.layers - 1
+        for k in range(top):
+
+            @pl.when(layer < top - k)
+            def up():
+                self._up(k, self.up_in.at[k]).wait_send()
+
+            @pl.when(layer > k)
+            def down():
+                self._down(k, self.down_in.at[k]).wait_send()
 
 
 class Gather:
@@ -324,11 +607,157 @@
     )
 
 
-def gather_kernel(columns, block, docs, full, docs_full, *scratch):
+def spread_kernel(
+    columns,
+    layers,
+    homes,
+    docs,
+    attn_ref,
+    ffn_ref,
+    docs_full,
+    attn_shard,
+    ffn_shard,
+    attn_bf,
+    ffn_bf,
+    docs_send,
+    docs_recv,
+    docs_local,
+    *scratch,
+):
+    attn_rows, ffn_rows = attn_ref.shape[0], ffn_ref.shape[0]
+    me = lax.axis_index("context")
+
+    @pl.loop(0, attn_rows // CHUNK)
+    def cast_attn(k):
+        attn_bf[chunk_rows(k), :] = attn_ref[chunk_rows(k), :].astype(BF)
+
+    @pl.loop(0, ffn_rows // CHUNK)
+    def cast_ffn(k):
+        ffn_bf[chunk_rows(k), :] = ffn_ref[chunk_rows(k), :].astype(BF)
+
+    greet(columns, 1, [spot[:2] for spot in homes.attn_targets() + homes.attn_owners()])
+    exchanges = []
+    for rows, source, target, targets, sems in (
+        (attn_rows, attn_bf, attn_shard, homes.attn_targets(), scratch[0:2]),
+        (ffn_rows, ffn_bf, ffn_shard, homes.ffn_targets(), scratch[2:4]),
+    ):
+        unit = rows // 3
+        exchanges.append(
+            Exchange(
+                [source.at[pl.ds(k * unit, unit), :] for k in range(3)],
+                functools.partial(place_rows, target, unit),
+                targets,
+                sems,
+            )
+        )
+    mine = docs_full.at[pl.ds(me, 1), :]
+    copies = [
+        send(docs, mine, docs_send.at[step], docs_recv.at[step], {"context": lax.rem(me + step, columns)})
+        for step in range(1, columns)
+    ]
+    local = pltpu.make_async_copy(docs, mine, docs_local)
+    local.start()
+    for exchange in exchanges:
+        exchange.arrive()
+    for copy in copies:
+        copy.wait_recv()
+    for copy in copies:
+        copy.wait_send()
+    local.wait()
+    for exchange in exchanges:
+        exchange.drain()
+
+
+def place_rows(ref, unit, layer, place):
+    return ref.at[rows_at(place, unit), :]
+
+
+def spread_step(docs, attn_weights, ffn_weights, columns, layers):
+    attn_rows, width = attn_weights.shape
+    ffn_rows = ffn_weights.shape[0]
+    homes = Homes(layers, columns, attn_rows * layers * columns)
+    return pl.pallas_call(
+        functools.partial(spread_kernel, columns, layers, homes),
+        out_shape=(
+            jax.ShapeDtypeStruct((columns, docs.shape[1]), jnp.int32),
+            jax.ShapeDtypeStruct((attn_rows, width), BF),
+            jax.ShapeDtypeStruct((ffn_rows, width), BF),
+        ),
+        in_specs=vmem_specs(3),
+        out_specs=tuple([pl.BlockSpec(memory_space=pl.ANY)] * 3),
+        scratch_shapes=[
+            pltpu.VMEM((attn_rows, width), BF),
+            pltpu.VMEM((ffn_rows, width), BF),
+            pltpu.SemaphoreType.DMA((columns,)),
+            pltpu.SemaphoreType.DMA((columns,)),
+            pltpu.SemaphoreType.DMA,
+            *Exchange.scratch(),
+            *Exchange.scratch(),
+        ],
+        compiler_params=comm_params(1),
+        name="spread_step",
+        cost_estimate=pl.CostEstimate(flops=0, bytes_accessed=60_000_000, transcendentals=0),
+    )(docs, attn_weights, ffn_weights)
+
+
+def open_kernel(
+    columns, layers, x_ref, gain_ref, dy_ref, shard_ref, h_full, dy_full, attn_col, hidden, shard_local, *scratch
+):
     chips = columns // 2
+    attn_rows = shard_ref.shape[0]
+    layer = lax.axis_index("fsdp")
+    greet(columns, layers)
+    line = LineGather(attn_col, attn_rows, layers, scratch[0:4], shard_ref)
+    line.step(0)
+    own = pltpu.make_async_copy(shard_ref, attn_col.at[rows_at(layer, attn_rows), :], shard_local)
+    own.start()
+
+    @pl.loop(0, x_ref.shape[0] // CHUNK)
+    def norm(k):
+        residual = x_ref[chunk_rows(k), :].astype(F32)
+        hidden[chunk_rows(k), :] = (residual * rms_scale(residual) * (1.0 + gain_ref[...])).astype(BF)
+
+    first = Gather(hidden, h_full, chips, scratch[4:9])
+    second = Gather(dy_ref, dy_full, chips, scratch[9:14])
+    line.step(1)
+    first.finish()
+    for k in range(2, layers - 1):
+        line.step(k)
+    second.finish()
+    line.step(layers - 1)
+    line.drain()
+    own.wait()
+
+
+def open_step(x_own, gain_row, dy_own, attn_shard, columns, layers):
+    rows, width = x_own.shape
+    attn_rows = attn_shard.shape[0]
+    return pl.pallas_call(
+        functools.partial(open_kernel, columns, layers),
+        out_shape=(
+            jax.ShapeDtypeStruct((columns * rows, width), BF),
+            jax.ShapeDtypeStruct((columns * rows, width), BF),
+            jax.ShapeDtypeStruct((layers * attn_rows, width), BF),
+        ),
+        in_specs=vmem_specs(4),
+        out_specs=tuple([pl.BlockSpec(memory_space=pl.ANY)] * 3),
+        scratch_shapes=[
+            pltpu.VMEM((rows, width), BF),
+            pltpu.SemaphoreType.DMA,
+            *LineGather.scratch(layers),
+            *Gather.scratch(columns // 2),
+            *Gather.scratch(columns // 2),
+        ],
+        compiler_params=comm_params(2),
+        name="open_step",
+        cost_estimate=pl.CostEstimate(flops=0, bytes_accessed=150_000_000, transcendentals=0),
+    )(x_own, gain_row, dy_own, attn_shard)
+
+
+def gather_docs_kernel(columns, block, docs, full, docs_full, *scratch):
     docs_send, docs_recv, docs_local = scratch[-3:]
     greet(columns)
-    gather = Gather(block, full, chips, scratch[:-3])
+    gather = Gather(block, full, columns // 2, scratch[:-3])
     me = lax.axis_index("context")
     mine = docs_full.at[pl.ds(me, 1), :]
     copies = [
@@ -345,10 +774,10 @@
     local.wait()
 
 
-def gather_first(block, docs, columns):
+def gather_docs(block, docs, columns):
     rows, width = block.shape
     return pl.pallas_call(
-        functools.partial(gather_kernel, columns),
+        functools.partial(gather_docs_kernel, columns),
         out_shape=(
             jax.ShapeDtypeStruct((columns * rows, width), BF),
             jax.ShapeDtypeStruct((columns, docs.shape[1]), jnp.int32),
@@ -361,8 +790,8 @@
             pltpu.SemaphoreType.DMA((columns,)),
             pltpu.SemaphoreType.DMA,
         ],
-        compiler_params=comm_params(1),
-        name="gather_first",
+        compiler_params=comm_params(6),
+        name="gather_docs",
         cost_estimate=pl.CostEstimate(flops=0, bytes_accessed=60_000_000, transcendentals=0),
     )(block, docs)
 
@@ -381,7 +810,7 @@
         in_specs=vmem_specs(1),
         out_specs=pl.BlockSpec(memory_space=pl.ANY),
         scratch_shapes=Gather.scratch(columns // 2),
-        compiler_params=comm_params(2),
+        compiler_params=comm_params(7),
         name="gather_plain",
         cost_estimate=pl.CostEstimate(flops=0, bytes_accessed=60_000_000, transcendentals=0),
     )(block)
@@ -478,38 +907,50 @@
     )(part, middle, dy_own, gain_row)
 
 
-def last_kernel(
-    columns,
-    layers,
-    part_in,
-    part_out,
-    x_ref,
-    middle_ref,
-    grad_ref,
-    gain_ref,
-    sums_ref,
-    input_grad_ref,
-    block_out_ref,
-    gains_ref,
-    own_sums,
-    plane_slots,
-    plane_sums,
-    line_slots,
-    plane_send,
-    plane_recv,
-    line_send,
-    line_recv,
-    *scratch,
-):
+def last_kernel(columns, layers, homes, *refs):
+    (part_in, x_ref, grad_ref, gain_ref, sums_ref), refs = refs[:5], refs[5:]
+    if homes is not None:
+        (term, ffn_sum), refs = refs[:2], refs[2:]
+    (input_grad_ref, gains_ref), refs = refs[:2], refs[2:]
+    if homes is not None:
+        (attn_back, ffn_back), refs = refs[:2], refs[2:]
+    (own_sums, plane_slots, plane_sums, line_slots), refs = refs[:4], refs[4:]
+    (plane_send, plane_recv, line_send, line_recv), scratch = refs[:4], refs[4:]
     chips = columns // 2
     rows = x_ref.shape[0]
-    greet(columns, layers)
+    if homes is None:
+        greet(columns, layers)
+    else:
+        attn_owners = homes.attn_owners()
+        greet(columns, layers, [spot[:2] for spot in homes.attn_targets() + attn_owners])
     first = Reduce(part_in, chips, rows, scratch[:7])
-    second = Reduce(part_out, chips, rows, scratch[7:])
+    if homes is not None:
+        attn_rows, ffn_rows = term.shape[0] // layers, ffn_sum.shape[0]
+        attn_done = scratch[7]
+        line = LineReduce(term, attn_rows, layers, scratch[8:14])
+        unit_ffn = ffn_rows // 3
+        ffn_owned = Exchange(
+            [ffn_sum.at[pl.ds(k * unit_ffn, unit_ffn), :] for k in range(3)],
+            lambda layer, piece: ffn_back.at[rows_at(piece, unit_ffn), :],
+            homes.ffn_owners(),
+            scratch[14:16],
+        )
     first.exchange()
-    second.exchange()
+    if homes is not None:
+        line.step(0)
     own_sums[...] = jnp.zeros_like(own_sums)
     own_sums[1:2, :] = sums_ref[0:1, :]
+    if homes is not None:
+        for k in range(1, layers - 1):
+            line.step(k)
+        line.finish(attn_done)
+        unit = attn_rows // 3
+        attn_owned = Exchange(
+            [attn_done.at[pl.ds(k * unit, unit), :] for k in range(3)],
+            lambda layer, piece: attn_back.at[rows_at(piece, unit), :],
+            attn_owners,
+            scratch[16:18],
+        )
     first.arrive()
 
     @pl.loop(0, rows // CHUNK)
@@ -536,13 +977,6 @@
         )
         for step in range(1, columns)
     ]
-    second.arrive()
-
-    @pl.loop(0, rows // CHUNK)
-    def finish_out(k):
-        at = chunk_rows(k)
-        block_out_ref[at, :] = middle_ref[at, :] + second.total(k)
-
     total = own_sums[...]
     for step, copy in enumerate(in_plane):
         copy.wait_recv()
@@ -562,24 +996,45 @@
         copy.wait_recv()
         total = total + line_slots[step + 1]
     gains_ref[...] = total
+    if homes is not None:
+        ffn_owned.arrive()
+        attn_owned.arrive()
+        ffn_owned.drain()
+        attn_owned.drain()
+        line.drain()
     for copy in in_plane + in_line:
         copy.wait_send()
     first.drain()
-    second.drain()
-
-
-def last_step(part_in, part_out, x_own, middle, grad_middle, gain_row, sums, columns, layers):
+
+
+def last_step(part_in, x_own, grad_middle, gain_row, sums, columns, layers, weight_sums=()):
     rows, width = x_own.shape
     chips = columns // 2
+    homes = None
+    back_shapes, back_scratch = [], []
+    if weight_sums:
+        term, ffn_sum = weight_sums
+        attn_rows = term.shape[0] // layers
+        homes = Homes(layers, columns, attn_rows * layers * columns)
+        back_shapes = [
+            jax.ShapeDtypeStruct((attn_rows, width), BF),
+            jax.ShapeDtypeStruct(ffn_sum.shape, BF),
+        ]
+        back_scratch = [
+            pltpu.VMEM((attn_rows, width), BF),
+            *LineReduce.scratch(layers, attn_rows, width),
+            *Exchange.scratch(),
+            *Exchange.scratch(),
+        ]
     return pl.pallas_call(
-        functools.partial(last_kernel, columns, layers),
+        functools.partial(last_kernel, columns, layers, homes),
         out_shape=(
             jax.ShapeDtypeStruct((rows, width), F32),
-            jax.ShapeDtypeStruct((rows, width), F32),
             jax.ShapeDtypeStruct((8, width), F32),
+            *back_shapes,
         ),
-        in_specs=vmem_specs(7),
-        out_specs=tuple(vmem_specs(3)),
+        in_specs=vmem_specs(5 + len(weight_sums)),
+        out_specs=tuple(vmem_specs(2) + [pl.BlockSpec(memory_space=pl.ANY)] * len(back_shapes)),
         scratch_shapes=[
             pltpu.VMEM((8, width), F32),
             pltpu.VMEM((columns, 8, width), F32),
@@ -590,12 +1045,12 @@
             pltpu.SemaphoreType.DMA((layers,)),
             pltpu.SemaphoreType.DMA((layers,)),
             *Reduce.scratch(chips, rows, width),
-            *Reduce.scratch(chips, rows, width),
+            *back_scratch,
         ],
         compiler_params=comm_params(5),
         name="last_step",
         cost_estimate=pl.CostEstimate(flops=0, bytes_accessed=150_000_000, transcendentals=0),
-    )(part_in, part_out, x_own, middle, grad_middle, gain_row, sums)
+    )(part_in, x_own, grad_middle, gain_row, sums, *weight_sums)
 
 
 def turned(heads, low):
@@ -682,7 +1137,10 @@
 
 
 def attend_back_kernel(
+    columns,
     heads,
+    part_ref,
+    middle_ref,
     grad_ref,
     pad_ref,
     cos_ref,
@@ -694,11 +1152,16 @@
     att_ref,
     log_ref,
     out_ref,
+    block_out_ref,
     ga_ref,
     dk_ref,
     dv_ref,
+    *scratch,
 ):
     seq = grad_ref.shape[0]
+    own_rows = middle_ref.shape[0]
+    greet(columns)
+    reduce = Reduce(part_ref, columns // 2, own_rows, scratch)
     scale = HEAD_SIZE**-0.5
     width = (heads + 2) * LANES
 
@@ -707,6 +1170,7 @@
         at = pl.ds(pl.multiple_of(i * TILE, TILE), TILE)
         ga_ref[at, :] = product_transposed(grad_ref[at, :], pad_ref[width:, :]).astype(BF)
 
+    reduce.exchange()
     dk_ref[...] = jnp.zeros_like(dk_ref)
     dv_ref[...] = jnp.zeros_like(dv_ref)
     low = lax.broadcasted_iota(jnp.int32, (TILE, LANES), 1) < HEAD_SIZE // 2
@@ -737,24 +1201,75 @@
         rows = slice(i * TILE, (i + 1) * TILE)
         out_ref[rows, heads * LANES : (heads + 1) * LANES] = turn_back(dk_ref[rows, :], rows)
         out_ref[rows, (heads + 1) * LANES :] = dv_ref[rows, :].astype(BF)
-
-
-def attend_back(grad_full, padded, cosine, sine, starts, saved, heads):
-    seq = grad_full.shape[0]
+    reduce.arrive()
+
+    @pl.loop(0, own_rows // CHUNK)
+    def finish_out(k):
+        at = chunk_rows(k)
+        block_out_ref[at, :] = middle_ref[at, :] + reduce.total(k)
+
+    reduce.drain()
+
+
+def attend_back(part_out, middle, grad_full, padded, cosine, sine, starts, saved, heads, columns):
+    seq, width = grad_full.shape
+    rows = seq // columns
     return pl.pallas_call(
-        functools.partial(attend_back_kernel, heads),
-        out_shape=jax.ShapeDtypeStruct((seq, (heads + 2) * LANES), BF),
-        in_specs=vmem_specs(10),
-        out_specs=pl.BlockSpec(memory_space=pltpu.VMEM),
+        functools.partial(attend_back_kernel, columns, heads),
+        out_shape=(
+            jax.ShapeDtypeStruct((seq, (heads + 2) * LANES), BF),
+            jax.ShapeDtypeStruct((rows, width), F32),
+        ),
+        in_specs=vmem_specs(12),
+        out_specs=tuple(vmem_specs(2)),
         scratch_shapes=[
             pltpu.VMEM((seq, heads * LANES), BF),
             pltpu.VMEM((seq, LANES), F32),
             pltpu.VMEM((seq, LANES), F32),
+            *Reduce.scratch(columns // 2, rows, width),
         ],
-        compiler_params=pltpu.CompilerParams(vmem_limit_bytes=VMEM_LIMIT),
+        compiler_params=comm_params(8),
         name="attend_back",
         cost_estimate=pl.CostEstimate(flops=8_000_000_000, bytes_accessed=20_000_000, transcendentals=2_000_000),
-    )(grad_full, padded, cosine, sine, starts, *saved)
+    )(part_out, middle, grad_full, padded, cosine, sine, starts, *saved)
+
+
+def update_kernel(g_ref, p_ref, m_ref, grad_ref, new_p_ref, new_m_ref):
+    gradient = g_ref[...].astype(F32)
+    grad_ref[...] = gradient
+    parameter = p_ref[...]
+    first_moment = BETA_ONE * m_ref[0] + (1.0 - BETA_ONE) * gradient
+    second_moment = BETA_TWO * m_ref[1] + (1.0 - BETA_TWO) * gradient * gradient
+    new_m_ref[0] = first_moment
+    new_m_ref[1] = second_moment
+    first_hat = first_moment / (1.0 - BETA_ONE**STEP)
+    second_hat = second_moment / (1.0 - BETA_TWO**STEP)
+    new_p_ref[...] = parameter - LEARN_RATE * (
+        first_hat / (jnp.sqrt(second_hat) + ADAM_EPS) + WEIGHT_DECAY * parameter
+    )
+
+
+def update(gradient, parameter, moments):
+    rows, width = parameter.shape
+    block = rows // 6 if rows % (6 * CHUNK) == 0 else rows // 3 if rows % (3 * CHUNK) == 0 else rows
+    flat = pl.BlockSpec((block, width), lambda i: (i, 0))
+    pair = pl.BlockSpec((2, block, width), lambda i: (0, i, 0))
+    return pl.pallas_call(
+        update_kernel,
+        grid=(rows // block,),
+        out_shape=(
+            jax.ShapeDtypeStruct((rows, width), F32),
+            jax.ShapeDtypeStruct((rows, width), F32),
+            jax.ShapeDtypeStruct((2, rows, width), F32),
+        ),
+        in_specs=[flat, flat, pair],
+        out_specs=(flat, flat, pair),
+        compiler_params=pltpu.CompilerParams(vmem_limit_bytes=VMEM_LIMIT),
+        name="update",
+        cost_estimate=pl.CostEstimate(
+            flops=20 * rows * width, bytes_accessed=30 * rows * width, transcendentals=rows * width
+        ),
+    )(gradient, parameter, moments)
 
 
 def rope_tables(positions):
@@ -792,16 +1307,30 @@
     share = KEY_VALUE_HEADS * HEAD_SIZE // columns
     hidden = ffn_weights.shape[0] * layers // 3
     grad_factor = float(rows * layers * columns) ** (-0.5)
-    attn_plan, ffn_plan = unit_plans(
-        layers, columns, attn_weights.shape[0] * layers * columns, ffn_weights.shape[0] * layers * columns
-    )
+    attn_plan, ffn_plan = unit_plans(layers, columns, attn_weights.shape[0] * layers * columns)
     core = lax.rem(lax.axis_index("context"), 2)
     swap = [(c, c + 1 - 2 * (c % 2)) for c in range(columns)]
 
-    attn_col = lax.all_gather(
-        attn_plan.spread(attn_weights.astype(BF)), "fsdp", axis=0, tiled=True
-    )
-    ffn_col = lax.all_gather(ffn_plan.spread(ffn_weights.astype(BF)), "fsdp", axis=0, tiled=True)
+    x_own = block_input[0]
+    aligned = attn_weights.shape[0] % (3 * CHUNK) == 0 and layers > 1
+    if aligned:
+        docs_full, attn_shard, ffn_shard = spread_step(
+            documents, attn_weights, ffn_weights, columns, layers
+        )
+        h_full, dy_full, attn_col = open_step(
+            x_own, norm_gains[0:1], cotangent[0], attn_shard, columns, layers
+        )
+    else:
+        residual = x_own.astype(F32)
+        first_hidden = (residual * rms_scale(residual) * (1.0 + norm_gains[0])).astype(BF)
+        h_full, docs_full = gather_docs(first_hidden, documents, columns)
+        dy_full = gather_plain(cotangent[0], columns)
+        attn_col = lax.all_gather(
+            attn_plan.spread(attn_weights.astype(BF)), "fsdp", axis=0, tiled=True
+        )
+        ffn_shard = ffn_plan.spread(ffn_weights.astype(BF))
+    ffn_shard, attn_col = lax.optimization_barrier((ffn_shard, attn_col))
+    ffn_col = lax.all_gather(ffn_shard, "fsdp", axis=0, tiled=True)
     query_rows = heads * HEAD_SIZE
     if sharers > 1:
         own_part = attn_col[query_rows : query_rows + 2 * share]
@@ -823,10 +1352,6 @@
         )
     w_gate, w_up, w_down = ffn_col[:hidden], ffn_col[hidden : 2 * hidden], ffn_col[2 * hidden :]
 
-    x_own = block_input[0]
-    residual = x_own.astype(F32)
-    first_hidden = (residual * rms_scale(residual) * (1.0 + norm_gains[0])).astype(BF)
-    h_full, docs_full = gather_first(first_hidden, documents, columns)
     all_docs = docs_full.reshape(seq)
     starts = jnp.sum((all_docs[None, :] < all_docs[:, None]).astype(jnp.int32), axis=1)
     cosine, sine = rope_tables(jnp.arange(seq, dtype=jnp.int32) - starts)
@@ -835,7 +1360,6 @@
         h_full, attn_col, cosine, sine, start_lanes, heads
     )
     middle, h2_full = middle_step(part, x_own, norm_gains[1:2], columns)
-    dy_full = gather_plain(cotangent[0], columns)
 
     gate_pre = product_transposed(h2_full, w_gate)
     up_pre = product_transposed(h2_full, w_up)
@@ -851,13 +1375,23 @@
             (transposed_times(activated, dy_full) * grad_factor).astype(BF),
         ]
     )
-    ffn_sum = lax.psum_scatter(ffn_term, "fsdp", scatter_dimension=0, tiled=True)
     out_part = plain_times(activated, w_down).astype(BF)
     back_part = (plain_times(grad_gate, w_gate) + plain_times(grad_up, w_up)).astype(BF)
+    back_part, ffn_term = lax.optimization_barrier((back_part, ffn_term))
+    ffn_sum = lax.psum_scatter(ffn_term, "fsdp", scatter_dimension=0, tiled=True)
     grad_middle, sums, gm_full = turn_step(back_part, middle, cotangent[0], norm_gains[1:2], columns)
 
-    grads = attend_back(
-        gm_full, padded, cosine, sine, start_lanes, (q_all, k_all, v_all, attended, logs), heads
+    grads, block_out = attend_back(
+        out_part,
+        middle,
+        gm_full,
+        padded,
+        cosine,
+        sine,
+        start_lanes,
+        (q_all, k_all, v_all, attended, logs),
+        heads,
+        columns,
     )
     if sharers > 1:
         shared = grads[:, heads * LANES :]
@@ -878,20 +1412,22 @@
         )
     else:
         attn_term = jnp.concatenate([unpadded(term_in, heads + 2), unpadded(term_out, heads)])
-    attn_sum = lax.psum_scatter(attn_term, "fsdp", scatter_dimension=0, tiled=True)
     in_part = plain_times(grads, padded[: (heads + 2) * LANES]).astype(BF)
-    grad_input, block_out, gain_sums = last_step(
-        in_part, out_part, x_own, middle, grad_middle, norm_gains[0:1], sums, columns, layers
-    )
-
-    ffn_shard = ffn_plan.collect(ffn_sum).astype(F32)
-    attn_shard = attn_plan.collect(attn_sum).astype(F32)
+    last_args = (in_part, x_own, grad_middle, norm_gains[0:1], sums, columns, layers)
+    if aligned:
+        grad_input, gain_sums, attn_shard, ffn_shard = last_step(*last_args, (attn_term, ffn_sum))
+    else:
+        attn_sum = lax.psum_scatter(attn_term, "fsdp", scatter_dimension=0, tiled=True)
+        grad_input, gain_sums = last_step(*last_args)
+        ffn_shard = ffn_plan.collect(ffn_sum)
+        attn_shard = attn_plan.collect(attn_sum)
+
     column_count = width // (layers * columns)
     first_column = lax.axis_index(EVERY) * column_count
     gain_shard = lax.dynamic_slice_in_dim(gain_sums[:2], first_column, column_count, 1) * grad_factor
     own_gains = lax.dynamic_slice_in_dim(norm_gains, first_column, column_count, 1)
-    new_ffn, ffn_states = adamw_update(ffn_weights, ffn_shard, ffn_moments, WEIGHT_DECAY)
-    new_attn, attn_states = adamw_update(attn_weights, attn_shard, attn_moments, WEIGHT_DECAY)
+    ffn_shard, new_ffn, ffn_states = update(ffn_shard, ffn_weights, ffn_moments)
+    attn_shard, new_attn, attn_states = update(attn_shard, attn_weights, attn_moments)
     new_gains, gain_states = adamw_update(own_gains, gain_shard, gain_moments, 0.0)
     return (
         block_out[None],

time: 434 us -> 383 us (0.88)
  the two profiles are of different devices: /device:TPU:10 before, /device:TPU:0 now
where the time goes in v2:
time: 383 us; the launch traced here: 382 us
  Pallas kernels  296 us (77%)
  matrix products  35.7 us (9%)
  waiting for transfers between devices  20.9 us (5%)
  between operations  14.3 us (4%)
  other arithmetic  8.29 us (2%)
  local copies, waits for them, and re-layouts  6.84 us (2%)
    pallas_call x1, Pallas kernels, last_step(): pl.pallas_call(functools.partial(last_kernel, columns, layers, homes), ou...  71.8 us
    pallas_call x1, Pallas kernels, turn_step(): pl.pallas_call(functools.partial(turn_kernel, columns), out_shape=(jax.Sh...  49.4 us
    pallas_call x1, Pallas kernels, middle_step(): pl.pallas_call(functools.partial(middle_kernel, columns), out_shape=(jax....  49.3 us
    pallas_call x1, Pallas kernels, open_step(): pl.pallas_call(functools.partial(open_kernel, columns, layers), out_shape...  44.4 us
    pallas_call x1, Pallas kernels, attend_back(): pl.pallas_call(functools.partial(attend_back_kernel, columns, heads), out...  29.5 us
    pallas_call x1, Pallas kernels, spread_step(): pl.pallas_call(functools.partial(spread_kernel, columns, layers, homes),...  23.8 us
    all_gather x1, waiting for transfers between devices, on_device(): ffn_col = lax.all_gather(ffn_shard, 'fsdp', axis=0, tiled=True)  20.9 us
    dot_general x4, matrix products, plain_times(): return jnp.dot(left_matrix, right_matrix, preferred_element_type=F32)  16.6 us
  transfers between devices with their start and end apart: 2, of which 1 were waited for; matrix products, arithmetic and copies ran while one was open for 5% of the time, Pallas kernels for 37%

profile of v2, /device:TPU:0, one launch (start us, length us, event | category | flops | bytes accessed | tf_op | source)
XLA Modules:
  0.0 382.1 jit_solution(9033084446113529209)
XLA Ops:
  7.2 1.4 fusion.18
  8.6 23.8 %spread_step.1 = (s32[8,128]{1,0:T(8,128)}, bf16[144,1536]{1,0:T(8,128)(2,1)}, bf16[384,1536]{1,0:T(8,128)(2,1)}) custom-call(s32[1,128]{1,0:T(1,128)} %docs.1, f32[144,1536]{1,0:T(8,128)} %p_ref.2, f32[384,1536]{1,0:T(8,128)} %p_ref.3), custom_call_target="tpu_custom_call" | custom-call | bytes 60000000 | tf_op jit(solution)/shard_map/spread_step/pallas_call | solution.py:679
  32.4 44.4 %open_step.1 = (bf16[1024,1536]{1,0:T(8,128)(2,1)}, bf16[1024,1536]{1,0:T(8,128)(2,1)}, bf16[576,1536]{1,0:T(8,128)(2,1)}) custom-call(bf16[128,1536]{1,0:T(8,128)(2,1)} %bitcast.34, f32[1,1536]{1,0:T(1,128)} %get-tuple-element.87.gain_ref.refs_3_, bf16[128,1536]{1,0:T(8,128)(2,1)} %bitcast.37, bf16[144,1536]{1,0:T(8,128)(2,1)} %get-tuple-element.45.shard_ref), custom_call_target="tpu_custom_call" | custom-call | bytes 150000000 | tf_op jit(solution)/shard_map/open_step/pallas_call | solution.py:735
  77.7 1.9 fusion.16
  79.6 1.3 maximum_maximum_fusion.1
  80.9 1.0 broadcast_in_dim.18.start_ref
  81.9 14.1 %attend.1 = (bf16[1024,256]{1,0:T(8,128)(2,1)}, bf16[1024,128]{1,0:T(8,128)(2,1)}, bf16[1024,128]{1,0:T(8,128)(2,1)}, bf16[1024,256]{1,0:T(8,128)(2,1)}, f32[102...) custom-call(bf16[1024,1536]{1,0:T(8,128)(2,1)} %get-tuple-element.46.h_ref, ...), custom_call_target="tpu_custom_call" | custom-call | flops 6000000000 | bytes 20000000 | tf_op jit(solution)/shard_map/attend/pallas_call | solution.py:1120
  95.9 49.3 %middle_step.1 = (f32[128,1536]{1,0:T(8,128)}, bf16[1024,1536]{1,0:T(8,128)(2,1)}) custom-call(bf16[1024,1536]{1,0:T(8,128)(2,1)} %get-tuple-element.51.part, bf16[128,1536]{1,0:T(8,128)(2,1)} %bitcast.35, f32[1,1536]{1,0:T(1,128)} %get-tuple-element.86.gain_ref), custom_call_target="tpu_custom_call" | custom-call | bytes 150000000 | tf_op jit(solution)/shard_map/middle_step/pallas_call | solution.py:842
  145.3 20.9 %all-gather.2.cloned.1.call-done = bf16[1536,1536]{1,0:T(8,128)(2,1)} async-done(((bf16[384,1536]{1,0:T(8,128)(2,1)}), bf16[1536,1536]{1,0:T(8,128)(2,1)}) %all-gather.2.cloned.1.call-update) | async-done | bytes 4718608 | tf_op jit(solution)/shard_map/all_gather | solution.py:1333
  166.1 4.3 %fusion.10 = f32[1024,512]{1,0:T(8,128)S(1)} fusion(bf16[1024,1536]{1,0:T(8,128)(2,1)} %get-tuple-element.52, bf16[1536,1536]{1,0:T(8,128)(2,1)} %all-gather.2.cloned.1.call-done), kind=kOutput, calls=%fused_computation.24 | convolution fusion | flops 1610612736 | bytes 6815744 | tf_op jit(solution)/shard_map/dot_general | solution.py:35
  170.9 1.8 fusion.14
  172.8 2.6 multiply_convert_fusion
  175.4 1.8 fusion
  177.2 1.8 fusion.1
  179.1 1.8 fusion.2
  180.9 2.6 pad_maximum_fusion
  183.5 3.2 fusion.12
  186.7 5.0 %add_convert_fusion.part = bf16[1024,1536]{1,0:T(8,128)(2,1)} fusion(f32[1024,1536]{1,0:T(8,128)S(1)} %fusion.12, bf16[1024,512]{1,0:T(8,128)(2,1)S(1)} %get-tuple-element.82, bf16[1536,1536]{1,0:T(8,128)(2,1)} %all-gather.2.cloned.1.call-done), kind=kOutput, calls=%fused_computation | convolution fusion | flops 1613758464 | bytes 12058624 | tf_op jit(solution)/shard_map/dot_general | solution.py:47
  191.7 49.4 %turn_step.1 = (f32[128,1536]{1,0:T(8,128)}, f32[8,1536]{1,0:T(8,128)}, bf16[1024,1536]{1,0:T(8,128)(2,1)}) custom-call(bf16[1024,1536]{1,0:T(8,128)(2,1)} %add_convert_fusion.part, f32[128,1536]{1,0:T(8,128)} %get-tuple-element.54.middle_ref, bf16[128,1536]{1,0:T(8,128)(2,1)} %bitcast.38, f32[1,1536]{1,0:T(1,128)} %get-tuple-element.86.gain_ref), custom_call_target="tpu_custom_call" | custom-call | bytes 150000000 | tf_op jit(solution)/shard_map/turn_step/pallas_call | solution.py:890
  241.1 5.0 %convolution_convert_fusion.1.part_ref = bf16[1024,1536]{1,0:T(8,128)(2,1)} fusion(bf16[1024,512]{1,0:T(8,128)(2,1)S(1)} %get-tuple-element.84, bf16[1536,1536]{1,0:T(8,128)(2,1)} %all-gather.2.cloned.1.call-done), kind=kOutput, calls=%fused_computation.4 | convolution fusion | flops 1612185600 | bytes 5767168 | tf_op jit(solution)/shard_map/dot_general | solution.py:47
  246.0 29.5 %attend_back.1 = (bf16[1024,512]{1,0:T(8,128)(2,1)}, f32[128,1536]{1,0:T(8,128)}) custom-call(bf16[1024,1536]{1,0:T(8,128)(2,1)} %convolution_convert_fusion.1.part_ref, f32[128,1536]{1,0:T(8,128)} %get-tuple-element.54.middle_ref, bf16[1024,1536]{1,0:T(8,128)(2,1)} %get-tuple-element.57.grad_ref, bf16[768,1536]{1,0:T(8,128)(2,1)} %get-tuple-element.58.pad_ref, ...), custom_call_target="tpu_custom_call" | custom-call | flops 8000000000 | bytes 20000000 | tf_op jit(solution)/shard_map/attend_back/pallas_call | solution.py:1217
  275.6 3.0 fusion.4
  278.7 3.4 convolution_convert_fusion.refs_0_
  282.1 1.8 fusion.3
  284.1 1.2 copy-done
  285.3 71.8 %last_step.1 = (f32[128,1536]{1,0:T(8,128)}, f32[8,1536]{1,0:T(8,128)}, bf16[144,1536]{1,0:T(8,128)(2,1)}, bf16[384,1536]{1,0:T(8,128)(2,1)}) custom-call(bf16[1024,1536]{1,0:T(8,128)(2,1)} %convolution_convert_fusion.refs_0_, bf16[128,1536]{1,0:T(8,128)(2,1)} %bitcast.36, f32[128,1536]{1,0:T(8,128)} %get-tuple-element.66.refs_2_, ...), custom_call_target="tpu_custom_call" | custom-call | bytes 150000000 | tf_op jit(solution)/shard_map/last_step/pallas_call | solution.py:1029
  357.1 0.8 slice.59
  357.9 1.3 multiply_subtract_fusion
  359.8 8.8 %update.3 = (f32[384,1536]{1,0:T(8,128)}, f32[384,1536]{1,0:T(8,128)}, f32[2,384,1536]{2,1,0:T(8,128)}) custom-call(bf16[384,1536]{1,0:T(8,128)(2,1)} %get-tuple-element.72.g_ref, f32[384,1536]{1,0:T(8,128)} %p_ref.3, f32[2,384,1536]{2,1,0:T(8,128)} %m_ref.3), custom_call_target="tpu_custom_call" | custom-call | flops 11796480 | bytes 17694720 | tf_op jit(solution)/shard_map/update/pallas_call | solution.py:1257
  368.7 4.9 %update.2 = (f32[144,1536]{1,0:T(8,128)}, f32[144,1536]{1,0:T(8,128)}, f32[2,144,1536]{2,1,0:T(8,128)}) custom-call(bf16[144,1536]{1,0:T(8,128)(2,1)} %get-tuple-element.70.g_ref, f32[144,1536]{1,0:T(8,128)} %p_ref.2, f32[2,144,1536]{2,1,0:T(8,128)} %m_ref.2), custom_call_target="tpu_custom_call" | custom-call | flops 4423680 | bytes 6635520 | tf_op jit(solution)/shard_map/update/pallas_call | solution.py:1257
  373.5 0.9 copy.27
  374.4 0.9 copy.28
  (40 shorter events, 2.0 us)
Async XLA Ops:
  7.2 159.0 %all-gather.2.cloned.1.call-start = ((), (), s32[]{:S(2)}) async-start(), calls=%async_computation.1 | async-start | bytes 5898240 | tf_op jit(solution)/shard_map/all_gather | solution.py:1333
  32.4 44.6 %copy-start.4 = (s32[8,128]{1,0:T(8,128)S(1)}, s32[8,128]{1,0:T(8,128)}, u32[]{:S(2)}) copy-start(s32[8,128]{1,0:T(8,128)} %get-tuple-element.50) | copy-start | bytes 12292
  76.9 207.2 %reduce-scatter.2.cloned.1.call-start = ((), (), s32[]{:S(2)}) async-start(), calls=%async_computation.2 | async-start | bytes 5898240 | tf_op jit(solution)/shard_map/reduce_scatter | solution.py:1381
  166.1 4.3 %copy-start.3 = (bf16[1536,1536]{1,0:T(8,128)(2,1)S(1)}, bf16[1536,1536]{1,0:T(8,128)(2,1)}, u32[]{:S(2)}) copy-start(bf16[1536,1536]{1,0:T(8,128)(2,1)} %all-gather.2.cloned.1.call-done) | copy-start | bytes 14155780
  166.1 4.7 %copy-start.8 = (bf16[1024,1536]{1,0:T(8,128)(2,1)S(1)}, bf16[1024,1536]{1,0:T(8,128)(2,1)}, u32[]{:S(2)}) copy-start(bf16[1024,1536]{1,0:T(8,128)(2,1)} %get-tuple-element.52) | copy-start | bytes 9437188
  170.9 1.9 copy-start.7
  246.0 29.5 %copy-start.10 = (bf16[1024,256]{1,0:T(8,128)(2,1)S(1)}, bf16[1024,256]{1,0:T(8,128)(2,1)}, u32[]{:S(2)}) copy-start(bf16[1024,256]{1,0:T(8,128)(2,1)} %get-tuple-element.62.att_ref) | copy-start | bytes 1572868
  275.6 3.1 copy-start.9
  275.6 3.1 copy-start.11
  278.6 3.4 copy-start.6
  284.1 1.2 copy-start
  285.3 72.6 %copy-start.5 = (f32[2,2,48]{2,1,0:T(2,128)S(1)}, f32[2,2,48]{2,1,0:T(2,128)}, u32[]{:S(2)}) copy-start(f32[2,2,48]{2,1,0:T(2,128)} %param.17) | copy-start | bytes 2308
  368.7 4.9 %copy-start.1 = (f32[128,1536]{1,0:T(8,128)S(1)}, f32[128,1536]{1,0:T(8,128)}, u32[]{:S(2)}) copy-start(f32[128,1536]{1,0:T(8,128)} %get-tuple-element.64) | copy-start | bytes 2359300
  368.7 5.7 %copy-start.2 = (f32[128,1536]{1,0:T(8,128)S(1)}, f32[128,1536]{1,0:T(8,128)}, u32[]{:S(2)}) copy-start(f32[128,1536]{1,0:T(8,128)} %get-tuple-element.69) | copy-start | bytes 2359300
Sparse Core Ops, SparseCore 0:
  77.0 89.0 all-gather.1
  191.8 83.6 reduce-scatter.1

commit v3 on v2

--- a/solution.py
+++ b/solution.py
@@ -64,7 +64,7 @@
     updated = parameter - LEARN_RATE * (
         first_hat / (jnp.sqrt(second_hat) + ADAM_EPS) + decay_rate * parameter
     )
-    return (updated, jnp.stack([first_moment, second_moment]))
+    return (updated, (first_moment, second_moment))
 
 
 class UnitPlan:
@@ -169,6 +169,13 @@
     def _spot(self, column, position):
         return position // 3, column, position % 3
 
+    def _column(self, group):
+        half = self.columns // 2
+        return group % half * 2 + group // half
+
+    def _group(self, column):
+        return column % 2 * (self.columns // 2) + column // 2
+
     def attn_targets(self):
         device = lax.axis_index("fsdp") * self.columns + lax.axis_index("context")
         found = []
@@ -178,20 +185,20 @@
             for first, size in zip(self.first, self.sizes):
                 inside = unit - first * self.columns
                 begun = inside >= 0
-                column = jnp.where(begun, inside // size, column)
+                column = jnp.where(begun, self._column(inside // size), column)
                 position = jnp.where(begun, first + inside % size, position)
             found.append(self._spot(column, position))
         return found
 
     def attn_owners(self):
-        column = lax.axis_index("context")
+        group = self._group(lax.axis_index("context"))
         found = []
         for place in range(3):
             position = lax.axis_index("fsdp") * 3 + place
             unit = 0
             for first, size in zip(self.first, self.sizes):
                 inside = position - first
-                unit = jnp.where(inside >= 0, first * self.columns + column * size + inside, unit)
+                unit = jnp.where(inside >= 0, first * self.columns + group * size + inside, unit)
             device = unit // 3
             found.append((device // self.columns, device % self.columns, unit % 3))
         return found
@@ -323,13 +330,29 @@
 
 class LineGather:
     @staticmethod
-    def scratch(layers):
-        return [pltpu.SemaphoreType.DMA((layers - 1,))] * 4
-
-    def __init__(self, full, rows, layers, sems, own):
-        self.full, self.rows, self.layers, self.sems, self.own = full, rows, layers, sems, own
-
-    def _moves(self, k):
+    def scratch(layers, pieces):
+        return [*[pltpu.SemaphoreType.DMA(((layers - 1) * pieces,))] * 4, pltpu.SemaphoreType.DMA]
+
+    def __init__(self, full, own, layers, pieces, sems):
+        self.full, self.own, self.layers, self.pieces = full, own, layers, pieces
+        *self.sems, local_sem = sems
+        self.rows = own.shape[0]
+        self.size = self.rows // pieces
+        self.count = (layers - 1) * pieces
+        self.local = pltpu.make_async_copy(
+            own, full.at[rows_at(lax.axis_index("fsdp"), self.rows), :], local_sem
+        )
+        for m in range(pieces):
+            self._send(m)
+        self.local.start()
+        self.next = pieces
+
+    def _block(self, shard, piece):
+        first = pl.multiple_of(shard * self.rows + piece * self.size, self.size)
+        return self.full.at[pl.ds(first, self.size), :]
+
+    def _moves(self, m):
+        k, piece = divmod(m, self.pieces)
         layer = lax.axis_index("fsdp")
         up_send, up_recv, down_send, down_recv = self.sems
         top = self.layers - 1
@@ -337,144 +360,186 @@
             (layer - k >= 0, layer < top, layer + 1, layer - k, up_send, up_recv),
             (layer + k <= top, layer > 0, layer - 1, layer + k, down_send, down_recv),
         ):
-            block = self.full.at[rows_at(shard, self.rows), :]
+            block = self._block(shard, piece)
+            source = self.own.at[pl.ds(piece * self.size, self.size), :] if k == 0 else block
             yield first & last, functools.partial(
-                remote, self.own if k == 0 else block, block, send_sem.at[k], recv_sem.at[k], {"fsdp": other}
+                remote, source, block, send_sem.at[m], recv_sem.at[m], {"fsdp": other}
             )
 
-    def _landed(self, k):
+    def _send(self, m):
+        for go, copy in self._moves(m):
+
+            @pl.when(go)
+            def start():
+                copy().start()
+
+    def _land(self, m):
+        k, piece = divmod(m, self.pieces)
         layer = lax.axis_index("fsdp")
         _, up_recv, _, down_recv = self.sems
         for there, shard, recv_sem in (
             (layer - 1 - k >= 0, layer - 1 - k, up_recv),
             (layer + 1 + k <= self.layers - 1, layer + 1 + k, down_recv),
         ):
-            block = self.full.at[rows_at(shard, self.rows), :]
-            yield there, functools.partial(pltpu.make_async_copy, block, block, recv_sem.at[k])
-
-    def step(self, k):
-        if k > 0:
-            for there, copy in self._landed(k - 1):
-
-                @pl.when(there)
-                def landed():
-                    copy().wait()
-
-        if k < self.layers - 1:
-            for go, copy in self._moves(k):
-
-                @pl.when(go)
-                def start():
-                    copy().start()
-
-    def drain(self):
-        for k in range(self.layers - 1):
-            for go, copy in self._moves(k):
+            block = self._block(shard, piece)
+            copy = functools.partial(pltpu.make_async_copy, block, block, recv_sem.at[m])
+
+            @pl.when(there)
+            def landed():
+                copy().wait()
+
+    def relay(self, count=None):
+        stop = self.count if count is None else min(self.count, self.next + count)
+        for m in range(self.next, stop):
+            self._land(m - self.pieces)
+            self._send(m)
+        self.next = stop
+
+    def finish(self):
+        self.relay()
+        for m in range(self.count - self.pieces, self.count):
+            self._land(m)
+        for m in range(self.count):
+            for go, copy in self._moves(m):
 
                 @pl.when(go)
                 def sent():
                     copy().wait_send()
 
+        self.local.wait()
+
 
 class LineReduce:
     @staticmethod
-    def scratch(layers, rows, width):
+    def scratch(layers, pieces, rows, width):
+        count = (layers - 1) * pieces
         return [
-            pltpu.VMEM((layers - 1, rows, width), BF),
-            pltpu.VMEM((layers - 1, rows, width), BF),
-            *[pltpu.SemaphoreType.DMA((layers - 1,))] * 4,
-        ]
-
-    def __init__(self, term, rows, layers, scratch):
-        self.term, self.rows, self.layers = term, rows, layers
+            pltpu.VMEM((count, rows // pieces, width), BF),
+            pltpu.VMEM((count, rows // pieces, width), BF),
+            *[pltpu.SemaphoreType.DMA((count,))] * 4,
+        ]
+
+    def __init__(self, term, layers, pieces, scratch):
+        self.term, self.layers, self.pieces = term, layers, pieces
+        self.rows = term.shape[0] // layers
+        self.size = self.rows // pieces
         self.up_in, self.down_in, *self.sems = scratch
+        self.count = (layers - 1) * pieces
+        self.slots = self.count + layers - 1
+        self.next = 1
         layer = lax.axis_index("fsdp")
         top = layers - 1
-        up_send, up_recv, down_send, down_recv = self.sems
 
         @pl.when(layer == 0)
         def bottom():
-            for k in range(top):
-                self._up(k, self.term.at[pl.ds((top - k) * rows, rows), :]).start()
+            for m in range(self.count):
+                self._up(m, self._block(top - m // pieces, m % pieces)).start()
 
         @pl.when(layer == top)
         def ceiling():
-            for k in range(top):
-                self._down(k, self.term.at[pl.ds(k * rows, rows), :]).start()
-
-    def _up(self, k, source):
+            for m in range(self.count):
+                self._down(m, self._block(m // pieces, m % pieces)).start()
+
+    def _block(self, target, piece):
+        return self.term.at[pl.ds(target * self.rows + piece * self.size, self.size), :]
+
+    def _up(self, m, source):
         up_send, up_recv, _, _ = self.sems
         other = {"fsdp": lax.axis_index("fsdp") + 1}
-        return remote(source, self.up_in.at[k], up_send.at[k], up_recv.at[k], other)
-
-    def _down(self, k, source):
+        return remote(source, self.up_in.at[m], up_send.at[m], up_recv.at[m], other)
+
+    def _down(self, m, source):
         _, _, down_send, down_recv = self.sems
         other = {"fsdp": lax.axis_index("fsdp") - 1}
-        return remote(source, self.down_in.at[k], down_send.at[k], down_recv.at[k], other)
-
-    def _add(self, sums, k, target):
-        @pl.loop(0, self.rows // CHUNK)
+        return remote(source, self.down_in.at[m], down_send.at[m], down_recv.at[m], other)
+
+    def _add(self, sums, m, target):
+        first = pl.multiple_of(target * self.rows + m % self.pieces * self.size, CHUNK)
+
+        @pl.loop(0, self.size // CHUNK)
         def add(c):
             at = chunk_rows(c)
-            of_term = pl.ds(target * self.rows + pl.multiple_of(c * CHUNK, CHUNK), CHUNK)
-            sums[k, at, :] = (
-                sums[k, at, :].astype(F32) + self.term[of_term, :].astype(F32)
+            of_term = pl.ds(pl.multiple_of(first + c * CHUNK, CHUNK), CHUNK)
+            sums[m, at, :] = (
+                sums[m, at, :].astype(F32) + self.term[of_term, :].astype(F32)
             ).astype(BF)
 
-    def step(self, k):
+    def _slot(self, slot):
         layer = lax.axis_index("fsdp")
         top = self.layers - 1
         _, up_recv, _, down_recv = self.sems
-        target = top - k
-
-        @pl.when((layer > 0) & (layer <= target))
+        m = slot - layer
+        target = top - m // self.pieces
+
+        @pl.when((layer > 0) & (m >= 0) & (m < self.count) & (layer <= target))
         def from_below():
-            pltpu.make_async_copy(self.up_in.at[k], self.up_in.at[k], up_recv.at[k]).wait()
-
-        @pl.when((layer > 0) & (layer < target))
-        def pass_up():
-            self._add(self.up_in, k, target)
-            self._up(k, self.up_in.at[k]).start()
-
-        @pl.when((layer < top) & (layer >= k))
+            pltpu.make_async_copy(self.up_in.at[m], self.up_in.at[m], up_recv.at[m]).wait()
+
+            @pl.when(layer < target)
+            def pass_up():
+                self._add(self.up_in, m, target)
+                self._up(m, self.up_in.at[m]).start()
+
+        n = slot - (top - layer)
+        goal = n // self.pieces
+
+        @pl.when((layer < top) & (n >= 0) & (n < self.count) & (layer >= goal))
         def from_above():
-            pltpu.make_async_copy(self.down_in.at[k], self.down_in.at[k], down_recv.at[k]).wait()
-
-        @pl.when((layer < top) & (layer > k))
-        def pass_down():
-            self._add(self.down_in, k, k)
-            self._down(k, self.down_in.at[k]).start()
+            pltpu.make_async_copy(self.down_in.at[n], self.down_in.at[n], down_recv.at[n]).wait()
+
+            @pl.when(layer > goal)
+            def pass_down():
+                self._add(self.down_in, n, goal)
+                self._down(n, self.down_in.at[n]).start()
+
+    def relay(self, count=None):
+        stop = self.slots if count is None else min(self.slots, self.next + count)
+        if stop > self.next:
+
+            @pl.loop(self.next, stop)
+            def slots(slot):
+                self._slot(slot)
+
+        self.next = stop
 
     def finish(self, total):
+        self.relay()
         layer = lax.axis_index("fsdp")
         top = self.layers - 1
         for own in range(self.layers):
 
             @pl.when(layer == own)
             def here():
-                @pl.loop(0, self.rows // CHUNK)
-                def add(c):
-                    at = chunk_rows(c)
-                    of_term = pl.ds(own * self.rows + pl.multiple_of(c * CHUNK, CHUNK), CHUNK)
-                    value = self.term[of_term, :].astype(F32)
-                    if own > 0:
-                        value = value + self.up_in[top - own, at, :].astype(F32)
-                    if own < top:
-                        value = value + self.down_in[own, at, :].astype(F32)
-                    total[at, :] = value.astype(BF)
+                for piece in range(self.pieces):
+
+                    @pl.loop(0, self.size // CHUNK)
+                    def add(c):
+                        start = pl.multiple_of(c * CHUNK, CHUNK)
+                        at = pl.ds(start, CHUNK)
+                        value = self.term[
+                            pl.ds(own * self.rows + piece * self.size + start, CHUNK), :
+                        ].astype(F32)
+                        if own > 0:
+                            m = (top - own) * self.pieces + piece
+                            value = value + self.up_in[m, at, :].astype(F32)
+                        if own < top:
+                            m = own * self.pieces + piece
+                            value = value + self.down_in[m, at, :].astype(F32)
+                        total[pl.ds(piece * self.size + start, CHUNK), :] = value.astype(BF)
 
     def drain(self):
         layer = lax.axis_index("fsdp")
         top = self.layers - 1
-        for k in range(top):
+        for m in range(self.count):
+            k = m // self.pieces
 
             @pl.when(layer < top - k)
             def up():
-                self._up(k, self.up_in.at[k]).wait_send()
+                self._up(m, self.up_in.at[m]).wait_send()
 
             @pl.when(layer > k)
             def down():
-                self._down(k, self.down_in.at[k]).wait_send()
+                self._down(m, self.down_in.at[m]).wait_send()
 
 
 class Gather:
@@ -504,19 +569,24 @@
         self.local = pltpu.make_async_copy(block, mine, local_sem)
         self.local.start()
 
-    def finish(self):
-        passed = []
+        self.passed = []
+
+    def pass_on(self):
         for step in range(1, self.chips):
             self.own[step - 1].wait_recv()
             source = partner(self.me, self.chips - step, self.chips)
             there = self.full.at[rows_at(source, self.rows), :]
-            passed.append(
+            self.passed.append(
                 send(there, there, self.on_send.at[step], self.on_recv.at[step], {"context": sibling_of(self.me)})
             )
+
+    def finish(self):
+        if not self.passed:
+            self.pass_on()
         self.own[-1].wait_recv()
-        for copy in passed:
+        for copy in self.passed:
             copy.wait_recv()
-        for copy in self.own + passed:
+        for copy in self.own + self.passed:
             copy.wait_send()
         self.local.wait()
 
@@ -607,171 +677,142 @@
     )
 
 
-def spread_kernel(
+def place_rows(ref, unit, layer, place):
+    return ref.at[rows_at(place, unit), :]
+
+
+class Docs:
+    @staticmethod
+    def scratch(columns):
+        return [
+            pltpu.SemaphoreType.DMA((columns,)),
+            pltpu.SemaphoreType.DMA((columns,)),
+            pltpu.SemaphoreType.DMA,
+        ]
+
+    def __init__(self, docs, docs_full, columns, sems):
+        docs_send, docs_recv, docs_local = sems
+        me = lax.axis_index("context")
+        mine = docs_full.at[pl.ds(me, 1), :]
+        self.copies = [
+            send(docs, mine, docs_send.at[step], docs_recv.at[step], {"context": lax.rem(me + step, columns)})
+            for step in range(1, columns)
+        ]
+        self.local = pltpu.make_async_copy(docs, mine, docs_local)
+        self.local.start()
+
+    def finish(self):
+        for copy in self.copies:
+            copy.wait_recv()
+        for copy in self.copies:
+            copy.wait_send()
+        self.local.wait()
+
+
+def open_kernel(
     columns,
     layers,
     homes,
+    x_ref,
+    gain_ref,
     docs,
     attn_ref,
     ffn_ref,
+    h_full,
     docs_full,
-    attn_shard,
+    attn_col,
     ffn_shard,
+    hidden,
     attn_bf,
     ffn_bf,
-    docs_send,
-    docs_recv,
-    docs_local,
+    attn_shard,
     *scratch,
 ):
     attn_rows, ffn_rows = attn_ref.shape[0], ffn_ref.shape[0]
-    me = lax.axis_index("context")
 
     @pl.loop(0, attn_rows // CHUNK)
     def cast_attn(k):
         attn_bf[chunk_rows(k), :] = attn_ref[chunk_rows(k), :].astype(BF)
 
-    @pl.loop(0, ffn_rows // CHUNK)
-    def cast_ffn(k):
-        ffn_bf[chunk_rows(k), :] = ffn_ref[chunk_rows(k), :].astype(BF)
-
-    greet(columns, 1, [spot[:2] for spot in homes.attn_targets() + homes.attn_owners()])
-    exchanges = []
-    for rows, source, target, targets, sems in (
-        (attn_rows, attn_bf, attn_shard, homes.attn_targets(), scratch[0:2]),
-        (ffn_rows, ffn_bf, ffn_shard, homes.ffn_targets(), scratch[2:4]),
-    ):
-        unit = rows // 3
-        exchanges.append(
-            Exchange(
-                [source.at[pl.ds(k * unit, unit), :] for k in range(3)],
-                functools.partial(place_rows, target, unit),
-                targets,
-                sems,
-            )
-        )
-    mine = docs_full.at[pl.ds(me, 1), :]
-    copies = [
-        send(docs, mine, docs_send.at[step], docs_recv.at[step], {"context": lax.rem(me + step, columns)})
-        for step in range(1, columns)
-    ]
-    local = pltpu.make_async_copy(docs, mine, docs_local)
-    local.start()
-    for exchange in exchanges:
-        exchange.arrive()
-    for copy in copies:
-        copy.wait_recv()
-    for copy in copies:
-        copy.wait_send()
-    local.wait()
-    for exchange in exchanges:
-        exchange.drain()
-
-
-def place_rows(ref, unit, layer, place):
-    return ref.at[rows_at(place, unit), :]
-
-
-def spread_step(docs, attn_weights, ffn_weights, columns, layers):
-    attn_rows, width = attn_weights.shape
-    ffn_rows = ffn_weights.shape[0]
-    homes = Homes(layers, columns, attn_rows * layers * columns)
-    return pl.pallas_call(
-        functools.partial(spread_kernel, columns, layers, homes),
-        out_shape=(
-            jax.ShapeDtypeStruct((columns, docs.shape[1]), jnp.int32),
-            jax.ShapeDtypeStruct((attn_rows, width), BF),
-            jax.ShapeDtypeStruct((ffn_rows, width), BF),
-        ),
-        in_specs=vmem_specs(3),
-        out_specs=tuple([pl.BlockSpec(memory_space=pl.ANY)] * 3),
-        scratch_shapes=[
-            pltpu.VMEM((attn_rows, width), BF),
-            pltpu.VMEM((ffn_rows, width), BF),
-            pltpu.SemaphoreType.DMA((columns,)),
-            pltpu.SemaphoreType.DMA((columns,)),
-            pltpu.SemaphoreType.DMA,
-            *Exchange.scratch(),
-            *Exchange.scratch(),
-        ],
-        compiler_params=comm_params(1),
-        name="spread_step",
-        cost_estimate=pl.CostEstimate(flops=0, bytes_accessed=60_000_000, transcendentals=0),
-    )(docs, attn_weights, ffn_weights)
-
-
-def open_kernel(
-    columns, layers, x_ref, gain_ref, dy_ref, shard_ref, h_full, dy_full, attn_col, hidden, shard_local, *scratch
-):
-    chips = columns // 2
-    attn_rows = shard_ref.shape[0]
-    layer = lax.axis_index("fsdp")
-    greet(columns, layers)
-    line = LineGather(attn_col, attn_rows, layers, scratch[0:4], shard_ref)
-    line.step(0)
-    own = pltpu.make_async_copy(shard_ref, attn_col.at[rows_at(layer, attn_rows), :], shard_local)
-    own.start()
+    targets = homes.attn_targets()
+    greet(columns, layers, [spot[:2] for spot in targets + homes.attn_owners()])
+    unit = attn_rows // 3
+    attn_spread = Exchange(
+        [attn_bf.at[pl.ds(k * unit, unit), :] for k in range(3)],
+        functools.partial(place_rows, attn_shard, unit),
+        targets,
+        scratch[0:2],
+    )
 
     @pl.loop(0, x_ref.shape[0] // CHUNK)
     def norm(k):
         residual = x_ref[chunk_rows(k), :].astype(F32)
         hidden[chunk_rows(k), :] = (residual * rms_scale(residual) * (1.0 + gain_ref[...])).astype(BF)
 
-    first = Gather(hidden, h_full, chips, scratch[4:9])
-    second = Gather(dy_ref, dy_full, chips, scratch[9:14])
-    line.step(1)
-    first.finish()
-    for k in range(2, layers - 1):
-        line.step(k)
-    second.finish()
-    line.step(layers - 1)
-    line.drain()
-    own.wait()
-
-
-def open_step(x_own, gain_row, dy_own, attn_shard, columns, layers):
+    documents = Docs(docs, docs_full, columns, scratch[2:5])
+    gather = Gather(hidden, h_full, columns // 2, scratch[5:10])
+
+    @pl.loop(0, ffn_rows // CHUNK)
+    def cast_ffn(k):
+        ffn_bf[chunk_rows(k), :] = ffn_ref[chunk_rows(k), :].astype(BF)
+
+    attn_spread.arrive()
+    line = LineGather(attn_col, attn_shard, layers, 1, scratch[10:15])
+    unit = ffn_rows // 3
+    ffn_spread = Exchange(
+        [ffn_bf.at[pl.ds(k * unit, unit), :] for k in range(3)],
+        functools.partial(place_rows, ffn_shard, unit),
+        homes.ffn_targets(),
+        scratch[15:17],
+    )
+    line.relay(1)
+    gather.pass_on()
+    line.relay()
+    documents.finish()
+    gather.finish()
+    ffn_spread.arrive()
+    line.finish()
+    attn_spread.drain()
+    ffn_spread.drain()
+
+
+def open_step(x_own, gain_row, docs, attn_weights, ffn_weights, columns, layers):
     rows, width = x_own.shape
-    attn_rows = attn_shard.shape[0]
+    attn_rows, ffn_rows = attn_weights.shape[0], ffn_weights.shape[0]
+    homes = Homes(layers, columns, attn_rows * layers * columns)
     return pl.pallas_call(
-        functools.partial(open_kernel, columns, layers),
+        functools.partial(open_kernel, columns, layers, homes),
         out_shape=(
             jax.ShapeDtypeStruct((columns * rows, width), BF),
-            jax.ShapeDtypeStruct((columns * rows, width), BF),
+            jax.ShapeDtypeStruct((columns, docs.shape[1]), jnp.int32),
             jax.ShapeDtypeStruct((layers * attn_rows, width), BF),
+            jax.ShapeDtypeStruct((ffn_rows, width), BF),
         ),
-        in_specs=vmem_specs(4),
-        out_specs=tuple([pl.BlockSpec(memory_space=pl.ANY)] * 3),
+        in_specs=vmem_specs(5),
+        out_specs=tuple([pl.BlockSpec(memory_space=pl.ANY)] * 4),
         scratch_shapes=[
             pltpu.VMEM((rows, width), BF),
-            pltpu.SemaphoreType.DMA,
-            *LineGather.scratch(layers),
+            pltpu.VMEM((attn_rows, width), BF),
+            pltpu.VMEM((ffn_rows, width), BF),
+            pltpu.VMEM((attn_rows, width), BF),
+            *Exchange.scratch(),
+            *Docs.scratch(columns),
             *Gather.scratch(columns // 2),
-            *Gather.scratch(columns // 2),
+            *LineGather.scratch(layers, 1),
+            *Exchange.scratch(),
         ],
-        compiler_params=comm_params(2),
+        compiler_params=comm_params(1),
         name="open_step",
         cost_estimate=pl.CostEstimate(flops=0, bytes_accessed=150_000_000, transcendentals=0),
-    )(x_own, gain_row, dy_own, attn_shard)
+    )(x_own, gain_row, docs, attn_weights, ffn_weights)
 
 
 def gather_docs_kernel(columns, block, docs, full, docs_full, *scratch):
-    docs_send, docs_recv, docs_local = scratch[-3:]
     greet(columns)
-    gather = Gather(block, full, columns // 2, scratch[:-3])
-    me = lax.axis_index("context")
-    mine = docs_full.at[pl.ds(me, 1), :]
-    copies = [
-        send(docs, mine, docs_send.at[step], docs_recv.at[step], {"context": lax.rem(me + step, columns)})
-        for step in range(1, columns)
-    ]
-    local = pltpu.make_async_copy(docs, mine, docs_local)
-    local.start()
+    gather = Gather(block, full, columns // 2, scratch[:5])
+    documents = Docs(docs, docs_full, columns, scratch[5:])
     gather.finish()
-    for copy in copies:
-        copy.wait_recv()
-    for copy in copies:
-        copy.wait_send()
-    local.wait()
+    documents.finish()
 
 
 def gather_docs(block, docs, columns):
@@ -784,127 +825,11 @@
         ),
         in_specs=vmem_specs(2),
         out_specs=(pl.BlockSpec(memory_space=pl.ANY), pl.BlockSpec(memory_space=pl.ANY)),
-        scratch_shapes=[
-            *Gather.scratch(columns // 2),
-            pltpu.SemaphoreType.DMA((columns,)),
-            pltpu.SemaphoreType.DMA((columns,)),
-            pltpu.SemaphoreType.DMA,
-        ],
-        compiler_params=comm_params(6),
+        scratch_shapes=[*Gather.scratch(columns // 2), *Docs.scratch(columns)],
+        compiler_params=comm_params(2),
         name="gather_docs",
         cost_estimate=pl.CostEstimate(flops=0, bytes_accessed=60_000_000, transcendentals=0),
     )(block, docs)
-
-
-def gather_plain_kernel(columns, block, full, *scratch):
-    greet(columns)
-    gather = Gather(block, full, columns // 2, scratch)
-    gather.finish()
-
-
-def gather_plain(block, columns):
-    rows, width = block.shape
-    return pl.pallas_call(
-        functools.partial(gather_plain_kernel, columns),
-        out_shape=jax.ShapeDtypeStruct((columns * rows, width), BF),
-        in_specs=vmem_specs(1),
-        out_specs=pl.BlockSpec(memory_space=pl.ANY),
-        scratch_shapes=Gather.scratch(columns // 2),
-        compiler_params=comm_params(7),
-        name="gather_plain",
-        cost_estimate=pl.CostEstimate(flops=0, bytes_accessed=60_000_000, transcendentals=0),
-    )(block)
-
-
-def middle_kernel(columns, part, x_ref, gain_ref, middle_ref, full, hidden, *scratch):
-    chips = columns // 2
-    rows = x_ref.shape[0]
-    greet(columns)
-    reduce = Reduce(part, chips, rows, scratch[:7])
-    reduce.exchange()
-    reduce.arrive()
-
-    @pl.loop(0, rows // CHUNK)
-    def finish(k):
-        at = chunk_rows(k)
-        middle = x_ref[at, :].astype(F32) + reduce.total(k)
-        middle_ref[at, :] = middle
-        hidden[at, :] = (middle * rms_scale(middle) * (1.0 + gain_ref[...])).astype(BF)
-
-    gather = Gather(hidden, full, chips, scratch[7:])
-    gather.finish()
-    reduce.drain()
-
-
-def middle_step(part, x_own, gain_row, columns):
-    rows, width = x_own.shape
-    chips = columns // 2
-    return pl.pallas_call(
-        functools.partial(middle_kernel, columns),
-        out_shape=(
-            jax.ShapeDtypeStruct((rows, width), F32),
-            jax.ShapeDtypeStruct((columns * rows, width), BF),
-        ),
-        in_specs=vmem_specs(3),
-        out_specs=(pl.BlockSpec(memory_space=pltpu.VMEM), pl.BlockSpec(memory_space=pl.ANY)),
-        scratch_shapes=[
-            pltpu.VMEM((rows, width), BF),
-            *Reduce.scratch(chips, rows, width),
-            *Gather.scratch(chips),
-        ],
-        compiler_params=comm_params(3),
-        name="middle_step",
-        cost_estimate=pl.CostEstimate(flops=0, bytes_accessed=150_000_000, transcendentals=0),
-    )(part, x_own, gain_row)
-
-
-def turn_kernel(columns, part, middle_ref, dy_ref, gain_ref, grad_ref, sums_ref, full, grad_bf, *scratch):
-    chips = columns // 2
-    rows = middle_ref.shape[0]
-    greet(columns)
-    reduce = Reduce(part, chips, rows, scratch[:7])
-    sums_ref[...] = jnp.zeros_like(sums_ref)
-    reduce.exchange()
-    reduce.arrive()
-
-    @pl.loop(0, rows // CHUNK)
-    def finish(k):
-        at = chunk_rows(k)
-        grad_hidden = reduce.total(k)
-        middle = middle_ref[at, :]
-        scale = rms_scale(middle)
-        normed = middle * scale
-        sums_ref[0:1, :] += jnp.sum(grad_hidden * normed, axis=0, keepdims=True)
-        grad = dy_ref[at, :].astype(F32) + norm_backward(grad_hidden, normed, scale, gain_ref[...])
-        grad_ref[at, :] = grad
-        grad_bf[at, :] = grad.astype(BF)
-
-    gather = Gather(grad_bf, full, chips, scratch[7:])
-    gather.finish()
-    reduce.drain()
-
-
-def turn_step(part, middle, dy_own, gain_row, columns):
-    rows, width = middle.shape
-    chips = columns // 2
-    return pl.pallas_call(
-        functools.partial(turn_kernel, columns),
-        out_shape=(
-            jax.ShapeDtypeStruct((rows, width), F32),
-            jax.ShapeDtypeStruct((8, width), F32),
-            jax.ShapeDtypeStruct((columns * rows, width), BF),
-        ),
-        in_specs=vmem_specs(4),
-        out_specs=(*vmem_specs(2), pl.BlockSpec(memory_space=pl.ANY)),
-        scratch_shapes=[
-            pltpu.VMEM((rows, width), BF),
-            *Reduce.scratch(chips, rows, width),
-            *Gather.scratch(chips),
-        ],
-        compiler_params=comm_params(4),
-        name="turn_step",
-        cost_estimate=pl.CostEstimate(flops=0, bytes_accessed=150_000_000, transcendentals=0),
-    )(part, middle, dy_own, gain_row)
 
 
 def last_kernel(columns, layers, homes, *refs):
@@ -927,30 +852,21 @@
     if homes is not None:
         attn_rows, ffn_rows = term.shape[0] // layers, ffn_sum.shape[0]
         attn_done = scratch[7]
-        line = LineReduce(term, attn_rows, layers, scratch[8:14])
+        line = LineReduce(term, layers, 3, scratch[8:14])
         unit_ffn = ffn_rows // 3
+    first.exchange()
+    if homes is not None:
         ffn_owned = Exchange(
             [ffn_sum.at[pl.ds(k * unit_ffn, unit_ffn), :] for k in range(3)],
-            lambda layer, piece: ffn_back.at[rows_at(piece, unit_ffn), :],
+            functools.partial(place_rows, ffn_back, unit_ffn),
             homes.ffn_owners(),
             scratch[14:16],
         )
-    first.exchange()
-    if homes is not None:
-        line.step(0)
+        line.relay(3)
     own_sums[...] = jnp.zeros_like(own_sums)
     own_sums[1:2, :] = sums_ref[0:1, :]
     if homes is not None:
-        for k in range(1, layers - 1):
-            line.step(k)
-        line.finish(attn_done)
-        unit = attn_rows // 3
-        attn_owned = Exchange(
-            [attn_done.at[pl.ds(k * unit, unit), :] for k in range(3)],
-            lambda layer, piece: attn_back.at[rows_at(piece, unit), :],
-            attn_owners,
-            scratch[16:18],
-        )
+        line.relay(3)
     first.arrive()
 
     @pl.loop(0, rows // CHUNK)
@@ -977,6 +893,15 @@
         )
         for step in range(1, columns)
     ]
+    if homes is not None:
+        line.finish(attn_done)
+        unit = attn_rows // 3
+        attn_owned = Exchange(
+            [attn_done.at[pl.ds(k * unit, unit), :] for k in range(3)],
+            functools.partial(place_rows, attn_back, unit),
+            attn_owners,
+            scratch[16:18],
+        )
     total = own_sums[...]
     for step, copy in enumerate(in_plane):
         copy.wait_recv()
@@ -1022,7 +947,7 @@
         ]
         back_scratch = [
             pltpu.VMEM((attn_rows, width), BF),
-            *LineReduce.scratch(layers, attn_rows, width),
+            *LineReduce.scratch(layers, 3, attn_rows, width),
             *Exchange.scratch(),
             *Exchange.scratch(),
         ]
@@ -1064,10 +989,14 @@
     return (cols <= rows) & (cols >= starts)
 
 
-def attend_kernel(
-    heads, h_ref, w_ref, cos_ref, sin_ref, start_ref, q_ref, k_ref, v_ref, att_ref, log_ref, part_ref, pad_ref
-):
-    seq = h_ref.shape[0]
+def forward_kernel(columns, layers, heads, *refs):
+    (h_ref, w_ref, cos_ref, sin_ref, start_ref, x_ref, gain_ref, dy_ref, ffn_shard), refs = refs[:9], refs[9:]
+    (q_ref, k_ref, v_ref, att_ref, log_ref, pad_ref, middle_ref), refs = refs[:7], refs[7:]
+    (h2_full, dy_full, ffn_col), (part_ref, hidden, *scratch) = refs[:3], refs[3:]
+    seq, own_rows, chips = h_ref.shape[0], x_ref.shape[0], columns // 2
+    greet(columns, layers)
+    line = LineGather(ffn_col, ffn_shard, layers, 3, scratch[0:5])
+    dy_gather = Gather(dy_ref, dy_full, chips, scratch[5:10])
     scale = HEAD_SIZE**-0.5
     for slot in range(2 * heads + 2):
         pad_ref[slot * LANES : slot * LANES + HEAD_SIZE, :] = w_ref[
@@ -1114,63 +1043,108 @@
         at = pl.ds(pl.multiple_of(i * TILE, TILE), TILE)
         part_ref[at, :] = plain_times(att_ref[at, :], pad_ref[width:, :]).astype(BF)
 
-
-def attend(h_full, w_col, cosine, sine, starts, heads):
+    reduce = Reduce(part_ref, chips, own_rows, scratch[10:17])
+    line.relay(1)
+    reduce.exchange()
+    line.relay(1)
+    dy_gather.pass_on()
+    line.relay(1)
+    reduce.arrive()
+
+    @pl.loop(0, own_rows // CHUNK)
+    def finish(k):
+        at = chunk_rows(k)
+        middle = x_ref[at, :].astype(F32) + reduce.total(k)
+        middle_ref[at, :] = middle
+        hidden[at, :] = (middle * rms_scale(middle) * (1.0 + gain_ref[...])).astype(BF)
+
+    gather = Gather(hidden, h2_full, chips, scratch[17:22])
+    line.relay(2)
+    gather.pass_on()
+    line.relay()
+    gather.finish()
+    dy_gather.finish()
+    reduce.drain()
+    line.finish()
+
+
+def forward_step(h_full, w_col, cosine, sine, starts, x_own, gain_row, dy_own, ffn_shard, heads, columns, layers):
     seq, width = h_full.shape
+    rows = x_own.shape[0]
+    chips = columns // 2
     return pl.pallas_call(
-        functools.partial(attend_kernel, heads),
+        functools.partial(forward_kernel, columns, layers, heads),
         out_shape=(
             jax.ShapeDtypeStruct((seq, heads * LANES), BF),
             jax.ShapeDtypeStruct((seq, LANES), BF),
             jax.ShapeDtypeStruct((seq, LANES), BF),
             jax.ShapeDtypeStruct((seq, heads * LANES), BF),
             jax.ShapeDtypeStruct((seq, heads * LANES), F32),
+            jax.ShapeDtypeStruct(((2 * heads + 2) * LANES, width), BF),
+            jax.ShapeDtypeStruct((rows, width), F32),
             jax.ShapeDtypeStruct((seq, width), BF),
-            jax.ShapeDtypeStruct(((2 * heads + 2) * LANES, width), BF),
+            jax.ShapeDtypeStruct((seq, width), BF),
+            jax.ShapeDtypeStruct((layers * ffn_shard.shape[0], width), BF),
         ),
-        in_specs=vmem_specs(5),
-        out_specs=tuple(vmem_specs(7)),
-        compiler_params=pltpu.CompilerParams(vmem_limit_bytes=VMEM_LIMIT),
-        name="attend",
-        cost_estimate=pl.CostEstimate(flops=6_000_000_000, bytes_accessed=20_000_000, transcendentals=2_000_000),
-    )(h_full, w_col, cosine, sine, starts)
-
-
-def attend_back_kernel(
-    columns,
-    heads,
-    part_ref,
-    middle_ref,
-    grad_ref,
-    pad_ref,
-    cos_ref,
-    sin_ref,
-    start_ref,
-    q_ref,
-    k_ref,
-    v_ref,
-    att_ref,
-    log_ref,
-    out_ref,
-    block_out_ref,
-    ga_ref,
-    dk_ref,
-    dv_ref,
-    *scratch,
-):
-    seq = grad_ref.shape[0]
-    own_rows = middle_ref.shape[0]
-    greet(columns)
-    reduce = Reduce(part_ref, columns // 2, own_rows, scratch)
+        in_specs=vmem_specs(9),
+        out_specs=tuple(vmem_specs(7) + [pl.BlockSpec(memory_space=pl.ANY)] * 3),
+        scratch_shapes=[
+            pltpu.VMEM((seq, width), BF),
+            pltpu.VMEM((rows, width), BF),
+            *LineGather.scratch(layers, 3),
+            *Gather.scratch(chips),
+            *Reduce.scratch(chips, rows, width),
+            *Gather.scratch(chips),
+        ],
+        compiler_params=comm_params(3),
+        name="forward_step",
+        cost_estimate=pl.CostEstimate(flops=6_000_000_000, bytes_accessed=150_000_000, transcendentals=2_000_000),
+    )(h_full, w_col, cosine, sine, starts, x_own, gain_row, dy_own, ffn_shard)
+
+
+def backward_kernel(columns, layers, heads, *refs):
+    (part_back, part_out, term, middle_ref, dy_ref, gain_ref, pad_ref), refs = refs[:7], refs[7:]
+    (cos_ref, sin_ref, start_ref, q_ref, k_ref, v_ref, att_ref, log_ref), refs = refs[:8], refs[8:]
+    (out_ref, block_out_ref, grad_ref, sums_ref, gm_full, ffn_sum), refs = refs[:6], refs[6:]
+    (grad_bf, ga_ref, dk_ref, dv_ref), scratch = refs[:4], refs[4:]
+    seq, own_rows, chips = gm_full.shape[0], middle_ref.shape[0], columns // 2
+    greet(columns, layers)
+    back = Reduce(part_back, chips, own_rows, scratch[0:7])
+    line = LineReduce(term, layers, 3, scratch[7:13])
+    sums_ref[...] = jnp.zeros_like(sums_ref)
+    back.exchange()
+    out = Reduce(part_out, chips, own_rows, scratch[13:20])
+    line.relay(1)
+    back.arrive()
+
+    @pl.loop(0, own_rows // CHUNK)
+    def turn(k):
+        at = chunk_rows(k)
+        grad_hidden = back.total(k)
+        middle = middle_ref[at, :]
+        scale = rms_scale(middle)
+        normed = middle * scale
+        sums_ref[0:1, :] += jnp.sum(grad_hidden * normed, axis=0, keepdims=True)
+        grad = dy_ref[at, :].astype(F32) + norm_backward(grad_hidden, normed, scale, gain_ref[...])
+        grad_ref[at, :] = grad
+        grad_bf[at, :] = grad.astype(BF)
+
+    gather = Gather(grad_bf, gm_full, chips, scratch[20:25])
+    line.relay(2)
+    out.exchange()
+    gather.pass_on()
+    line.relay(1)
+    gather.finish()
+    line.relay(1)
+
     scale = HEAD_SIZE**-0.5
     width = (heads + 2) * LANES
 
     @pl.loop(0, seq // TILE)
     def attended_gradient(i):
         at = pl.ds(pl.multiple_of(i * TILE, TILE), TILE)
-        ga_ref[at, :] = product_transposed(grad_ref[at, :], pad_ref[width:, :]).astype(BF)
-
-    reduce.exchange()
+        ga_ref[at, :] = product_transposed(gm_full[at, :], pad_ref[width:, :]).astype(BF)
+
     dk_ref[...] = jnp.zeros_like(dk_ref)
     dv_ref[...] = jnp.zeros_like(dv_ref)
     low = lax.broadcasted_iota(jnp.int32, (TILE, LANES), 1) < HEAD_SIZE // 2
@@ -1201,40 +1175,56 @@
         rows = slice(i * TILE, (i + 1) * TILE)
         out_ref[rows, heads * LANES : (heads + 1) * LANES] = turn_back(dk_ref[rows, :], rows)
         out_ref[rows, (heads + 1) * LANES :] = dv_ref[rows, :].astype(BF)
-    reduce.arrive()
+    line.relay(2)
+    out.arrive()
 
     @pl.loop(0, own_rows // CHUNK)
     def finish_out(k):
         at = chunk_rows(k)
-        block_out_ref[at, :] = middle_ref[at, :] + reduce.total(k)
-
-    reduce.drain()
-
-
-def attend_back(part_out, middle, grad_full, padded, cosine, sine, starts, saved, heads, columns):
-    seq, width = grad_full.shape
+        block_out_ref[at, :] = middle_ref[at, :] + out.total(k)
+
+    line.finish(ffn_sum)
+    line.drain()
+    back.drain()
+    out.drain()
+
+
+def backward_step(
+    part_back, part_out, term, middle, dy_own, gain_row, padded, tables, saved, heads, columns, layers
+):
+    seq, width = part_back.shape
     rows = seq // columns
+    chips = columns // 2
+    ffn_rows = term.shape[0] // layers
     return pl.pallas_call(
-        functools.partial(attend_back_kernel, columns, heads),
+        functools.partial(backward_kernel, columns, layers, heads),
         out_shape=(
             jax.ShapeDtypeStruct((seq, (heads + 2) * LANES), BF),
             jax.ShapeDtypeStruct((rows, width), F32),
+            jax.ShapeDtypeStruct((rows, width), F32),
+            jax.ShapeDtypeStruct((8, width), F32),
+            jax.ShapeDtypeStruct((seq, width), BF),
+            jax.ShapeDtypeStruct((ffn_rows, width), BF),
         ),
-        in_specs=vmem_specs(12),
-        out_specs=tuple(vmem_specs(2)),
+        in_specs=vmem_specs(15),
+        out_specs=tuple(vmem_specs(6)),
         scratch_shapes=[
+            pltpu.VMEM((rows, width), BF),
             pltpu.VMEM((seq, heads * LANES), BF),
             pltpu.VMEM((seq, LANES), F32),
             pltpu.VMEM((seq, LANES), F32),
-            *Reduce.scratch(columns // 2, rows, width),
+            *Reduce.scratch(chips, rows, width),
+            *LineReduce.scratch(layers, 3, ffn_rows, width),
+            *Reduce.scratch(chips, rows, width),
+            *Gather.scratch(chips),
         ],
-        compiler_params=comm_params(8),
-        name="attend_back",
-        cost_estimate=pl.CostEstimate(flops=8_000_000_000, bytes_accessed=20_000_000, transcendentals=2_000_000),
-    )(part_out, middle, grad_full, padded, cosine, sine, starts, *saved)
-
-
-def update_kernel(g_ref, p_ref, m_ref, grad_ref, new_p_ref, new_m_ref):
+        compiler_params=comm_params(4),
+        name="backward_step",
+        cost_estimate=pl.CostEstimate(flops=8_000_000_000, bytes_accessed=150_000_000, transcendentals=2_000_000),
+    )(part_back, part_out, term, middle, dy_own, gain_row, padded, *tables, *saved)
+
+
+def update_rows(g_ref, p_ref, m_ref, grad_ref, new_p_ref, new_m_ref):
     gradient = g_ref[...].astype(F32)
     grad_ref[...] = gradient
     parameter = p_ref[...]
@@ -1242,34 +1232,56 @@
     second_moment = BETA_TWO * m_ref[1] + (1.0 - BETA_TWO) * gradient * gradient
     new_m_ref[0] = first_moment
     new_m_ref[1] = second_moment
-    first_hat = first_moment / (1.0 - BETA_ONE**STEP)
-    second_hat = second_moment / (1.0 - BETA_TWO**STEP)
-    new_p_ref[...] = parameter - LEARN_RATE * (
-        first_hat / (jnp.sqrt(second_hat) + ADAM_EPS) + WEIGHT_DECAY * parameter
-    )
-
-
-def update(gradient, parameter, moments):
-    rows, width = parameter.shape
-    block = rows // 6 if rows % (6 * CHUNK) == 0 else rows // 3 if rows % (3 * CHUNK) == 0 else rows
-    flat = pl.BlockSpec((block, width), lambda i: (i, 0))
-    pair = pl.BlockSpec((2, block, width), lambda i: (0, i, 0))
-    return pl.pallas_call(
-        update_kernel,
-        grid=(rows // block,),
-        out_shape=(
+    below = jnp.sqrt(second_moment * (1.0 / (1.0 - BETA_TWO**STEP))) + ADAM_EPS
+    step = first_moment * (LEARN_RATE / (1.0 - BETA_ONE**STEP)) / below
+    new_p_ref[...] = parameter * (1.0 - LEARN_RATE * WEIGHT_DECAY) - step
+
+
+def update_kernel(steps, *refs):
+    first = pl.program_id(0) < steps
+
+    @pl.when(first)
+    def one():
+        update_rows(*refs[0:3], *refs[6:9])
+
+    @pl.when(jnp.logical_not(first))
+    def other():
+        update_rows(*refs[3:6], *refs[9:12])
+
+
+def update_all(first, second):
+    specs, shapes = [], []
+    blocks = []
+    for gradient, parameter, _ in (first, second):
+        rows = parameter.shape[0]
+        whole = [n for n in (48, 32) if rows % n == 0]
+        blocks.append(whole[0] if whole else rows)
+    steps = first[1].shape[0] // blocks[0]
+    rest = second[1].shape[0] // blocks[1]
+    for block, place, (_, parameter, _) in (
+        (blocks[0], lambda i: jnp.minimum(i, steps - 1), first),
+        (blocks[1], lambda i: jnp.maximum(i - steps, 0), second),
+    ):
+        rows, width = parameter.shape
+        flat = pl.BlockSpec((block, width), lambda i, place=place: (place(i), 0))
+        pair = pl.BlockSpec((2, block, width), lambda i, place=place: (0, place(i), 0))
+        specs.append([flat, flat, pair])
+        shapes += [
             jax.ShapeDtypeStruct((rows, width), F32),
             jax.ShapeDtypeStruct((rows, width), F32),
             jax.ShapeDtypeStruct((2, rows, width), F32),
-        ),
-        in_specs=[flat, flat, pair],
-        out_specs=(flat, flat, pair),
+        ]
+    out = pl.pallas_call(
+        functools.partial(update_kernel, steps),
+        grid=(steps + rest,),
+        out_shape=tuple(shapes),
+        in_specs=specs[0] + specs[1],
+        out_specs=tuple(specs[0] + specs[1]),
         compiler_params=pltpu.CompilerParams(vmem_limit_bytes=VMEM_LIMIT),
-        name="update",
-        cost_estimate=pl.CostEstimate(
-            flops=20 * rows * width, bytes_accessed=30 * rows * width, transcendentals=rows * width
-        ),
-    )(gradient, parameter, moments)
+        name="update_all",
+        cost_estimate=pl.CostEstimate(flops=20_000_000, bytes_accessed=25_000_000, transcendentals=1_000_000),
+    )(*first, *second)
+    return out[:3], out[3:]
 
 
 def rope_tables(positions):
@@ -1311,26 +1323,20 @@
     core = lax.rem(lax.axis_index("context"), 2)
     swap = [(c, c + 1 - 2 * (c % 2)) for c in range(columns)]
 
-    x_own = block_input[0]
+    x_own, dy_own = block_input[0], cotangent[0]
     aligned = attn_weights.shape[0] % (3 * CHUNK) == 0 and layers > 1
     if aligned:
-        docs_full, attn_shard, ffn_shard = spread_step(
-            documents, attn_weights, ffn_weights, columns, layers
-        )
-        h_full, dy_full, attn_col = open_step(
-            x_own, norm_gains[0:1], cotangent[0], attn_shard, columns, layers
+        h_full, docs_full, attn_col, ffn_shard = open_step(
+            x_own, norm_gains[0:1], documents, attn_weights, ffn_weights, columns, layers
         )
     else:
         residual = x_own.astype(F32)
         first_hidden = (residual * rms_scale(residual) * (1.0 + norm_gains[0])).astype(BF)
         h_full, docs_full = gather_docs(first_hidden, documents, columns)
-        dy_full = gather_plain(cotangent[0], columns)
         attn_col = lax.all_gather(
             attn_plan.spread(attn_weights.astype(BF)), "fsdp", axis=0, tiled=True
         )
         ffn_shard = ffn_plan.spread(ffn_weights.astype(BF))
-    ffn_shard, attn_col = lax.optimization_barrier((ffn_shard, attn_col))
-    ffn_col = lax.all_gather(ffn_shard, "fsdp", axis=0, tiled=True)
     query_rows = heads * HEAD_SIZE
     if sharers > 1:
         own_part = attn_col[query_rows : query_rows + 2 * share]
@@ -1350,16 +1356,17 @@
                 attn_col[query_rows + 2 * share :],
             ]
         )
-    w_gate, w_up, w_down = ffn_col[:hidden], ffn_col[hidden : 2 * hidden], ffn_col[2 * hidden :]
 
     all_docs = docs_full.reshape(seq)
     starts = jnp.sum((all_docs[None, :] < all_docs[:, None]).astype(jnp.int32), axis=1)
     cosine, sine = rope_tables(jnp.arange(seq, dtype=jnp.int32) - starts)
     start_lanes = jnp.broadcast_to(starts[:, None], (seq, LANES))
-    q_all, k_all, v_all, attended, logs, part, padded = attend(
-        h_full, attn_col, cosine, sine, start_lanes, heads
-    )
-    middle, h2_full = middle_step(part, x_own, norm_gains[1:2], columns)
+    tables = (cosine, sine, start_lanes)
+    *saved, padded, middle, h2_full, dy_full, ffn_col = forward_step(
+        h_full, attn_col, *tables, x_own, norm_gains[1:2], dy_own, ffn_shard, heads, columns, layers
+    )
+    attended = saved[3]
+    w_gate, w_up, w_down = ffn_col[:hidden], ffn_col[hidden : 2 * hidden], ffn_col[2 * hidden :]
 
     gate_pre = product_transposed(h2_full, w_gate)
     up_pre = product_transposed(h2_full, w_up)
@@ -1377,21 +1384,20 @@
     )
     out_part = plain_times(activated, w_down).astype(BF)
     back_part = (plain_times(grad_gate, w_gate) + plain_times(grad_up, w_up)).astype(BF)
-    back_part, ffn_term = lax.optimization_barrier((back_part, ffn_term))
-    ffn_sum = lax.psum_scatter(ffn_term, "fsdp", scatter_dimension=0, tiled=True)
-    grad_middle, sums, gm_full = turn_step(back_part, middle, cotangent[0], norm_gains[1:2], columns)
-
-    grads, block_out = attend_back(
+
+    grads, block_out, grad_middle, sums, gm_full, ffn_sum = backward_step(
+        back_part,
         out_part,
+        ffn_term,
         middle,
-        gm_full,
+        dy_own,
+        norm_gains[1:2],
         padded,
-        cosine,
-        sine,
-        start_lanes,
-        (q_all, k_all, v_all, attended, logs),
+        tables,
+        saved,
         heads,
         columns,
+        layers,
     )
     if sharers > 1:
         shared = grads[:, heads * LANES :]
@@ -1426,8 +1432,9 @@
     first_column = lax.axis_index(EVERY) * column_count
     gain_shard = lax.dynamic_slice_in_dim(gain_sums[:2], first_column, column_count, 1) * grad_factor
     own_gains = lax.dynamic_slice_in_dim(norm_gains, first_column, column_count, 1)
-    ffn_shard, new_ffn, ffn_states = update(ffn_shard, ffn_weights, ffn_moments)
-    attn_shard, new_attn, attn_states = update(attn_shard, attn_weights, attn_moments)
+    (ffn_shard, new_ffn, ffn_states), (attn_shard, new_attn, attn_states) = update_all(
+        (ffn_shard, ffn_weights, ffn_moments), (attn_shard, attn_weights, attn_moments)
+    )
     new_gains, gain_states = adamw_update(own_gains, gain_shard, gain_moments, 0.0)
     return (
         block_out[None],
@@ -1440,7 +1447,7 @@
         new_gains,
         attn_states,
         ffn_states,
-        gain_states,
+        jnp.stack(gain_states),
     )
 
 

time: 383 us -> 341 us (0.89)
  waiting for transfers between devices: 20.9 us -> 0 us
  between operations: 14.3 us -> 0.89 us
  matrix products: 35.7 us -> 31.6 us
  Pallas kernels: 296 us -> 292 us
    all_gather x1 -> x0, waiting for transfers between devices: 20.9 us -> none  [on_device(): ffn_col = lax.all_gather(ffn_shard, 'fsdp', axis=0, tiled=True)]
    pallas_call x1, Pallas kernels: 71.8 us -> 52.6 us  [last_step(): pl.pallas_call(functools.partial(last_kernel, columns, layers, homes), ou...]
    pallas_call x8 -> x4, Pallas kernels: 224 us -> 239 us  [the longest x1 87.9 us: backward_step(): pl.pallas_call(functools.partial(backward_kernel, columns, layers, heads)...]
    dot_general x4, matrix products: 16.6 us -> 12.4 us  [plain_times(): return jnp.dot(left_matrix, right_matrix, preferred_element_type=F32)]
  transfers between devices with their start and end apart: 2 -> 0, of which waited for: 1 -> 0; matrix products, arithmetic and copies ran while one was open for 5% -> 0% of each run, Pallas kernels for 37% -> 0%
where the time goes in v3:
time: 341 us; the launch traced here: 340 us
  Pallas kernels  292 us (86%)
  matrix products  31.6 us (9%)
  other arithmetic  8.81 us (3%)
  local copies, waits for them, and re-layouts  7.14 us (2%)
    pallas_call x1, Pallas kernels, backward_step(): pl.pallas_call(functools.partial(backward_kernel, columns, layers, heads)...  87.9 us
    pallas_call x1, Pallas kernels, forward_step(): pl.pallas_call(functools.partial(forward_kernel, columns, layers, heads),...  85.1 us
    pallas_call x1, Pallas kernels, last_step(): pl.pallas_call(functools.partial(last_kernel, columns, layers, homes), ou...  52.6 us
    pallas_call x1, Pallas kernels, open_step(): pl.pallas_call(functools.partial(open_kernel, columns, layers, homes), ou...  52.3 us
    pallas_call x1, Pallas kernels, update_all(): pl.pallas_call(functools.partial(update_kernel, steps), grid=(steps + res...  13.9 us
    dot_general x4, matrix products, plain_times(): return jnp.dot(left_matrix, right_matrix, preferred_element_type=F32)  12.4 us
    dot_general x5, matrix products, transposed_times(): lax.dot_general(left_matrix, right_matrix, (((0,), (0,)), ((), ())), pref...  10.4 us
    dot_general x3, matrix products, product_transposed(): lax.dot_general(left_matrix, right_matrix, (((1,), (1,)), ((), ())), pref...  8.79 us

profile of v3, /device:TPU:0, one launch (start us, length us, event | category | flops | bytes accessed | tf_op | source)
XLA Modules:
  0.0 340.3 jit_solution(7342592436262586913)
XLA Ops:
  0.6 1.4 fusion.18
  2.0 52.3 %open_step.1 = (bf16[1024,1536]{1,0:T(8,128)(2,1)}, s32[8,128]{1,0:T(8,128)}, bf16[576,1536]{1,0:T(8,128)(2,1)}, bf16[384,1536]{1,0:T(8,128)(2,1)}) custom-call(bf16[128,1536]{1,0:T(8,128)(2,1)} %bitcast.34, f32[1,1536]{1,0:T(1,128)} %get-tuple-element.79.gain_ref.refs_3_, s32[1,128]{1,0:T(1,128)} %docs.1, f32[144,1536]{1,0:T(8,128)} %refs_4_.1, ...), custom_call_target="tpu_custom_call" | custom-call | bytes 150000000 | tf_op jit(solution)/shard_map/open_step/pallas_call | solution.py:783
  54.3 1.3 convert_reduce_fusion
  55.6 1.9 fusion.16
  57.6 0.1 pad.10.clone
  57.6 1.3 maximum_maximum_fusion.1
  58.9 1.0 broadcast_in_dim.18.refs_4_.refs_9_
  59.9 85.1 %forward_step.1 = (bf16[1024,256]{1,0:T(8,128)(2,1)}, bf16[1024,128]{1,0:T(8,128)(2,1)}, bf16[1024,128]{1,0:T(8,128)(2,1)}, bf16[1024,256]{1,0:T(8,128)(2,1)}, f...) custom-call(bf16[1024,1536]{1,0:T(8,128)(2,1)} %get-tuple-element.41, ...), custom_call_target="tpu_custom_call" | custom-call | flops 6000000000 | bytes 150000000 | tf_op jit(solution)/shard_map/forward_step/pallas_call | solution.py:1075
  145.1 4.3 %fusion.14 = f32[1024,512]{1,0:T(8,128)S(1)} fusion(bf16[1024,1536]{1,0:T(8,128)(2,1)} %get-tuple-element.45, bf16[1536,1536]{1,0:T(8,128)(2,1)} %get-tuple-element.46), kind=kOutput, calls=%fused_computation.28 | convolution fusion | flops 1610612736 | bytes 6815744 | tf_op jit(solution)/shard_map/dot_general | solution.py:35
  149.5 0.4 copy-done.7
  149.8 1.8 fusion.8
  151.7 2.7 multiply_convert_fusion
  154.3 1.9 fusion
  156.2 1.8 fusion.1
  158.1 1.8 fusion.2
  159.9 2.4 pad_maximum_fusion.refs_2_
  162.3 3.6 %convolution_convert_fusion.1.refs_1_ = bf16[1024,1536]{1,0:T(8,128)(2,1)} fusion(bf16[1024,512]{1,0:T(8,128)(2,1)S(1)} %get-tuple-element.74, bf16[1536,1536]{1,0:T(8,128)(2,1)S(1)} %copy-done.3), kind=kOutput, calls=%fused_computation.4 | convolution fusion | flops 1612185600 | bytes 5767168 | tf_op jit(solution)/shard_map/dot_general | solution.py:47
  165.9 1.8 fusion.6
  167.7 3.6 %add_convert_fusion.refs_0_ = bf16[1024,1536]{1,0:T(8,128)(2,1)} fusion(f32[1024,1536]{1,0:T(8,128)S(1)} %fusion.6, bf16[1024,512]{1,0:T(8,128)(2,1)S(1)} %get-tuple-element.76, bf16[1536,1536]{1,0:T(8,128)(2,1)S(1)} %copy-done.3), kind=kOutput, calls=%fused_computation | convolution fusion | flops 1613758464 | bytes 12058624 | tf_op jit(solution)/shard_map/dot_general | solution.py:47
  171.2 87.9 %backward_step.1 = (bf16[1024,512]{1,0:T(8,128)(2,1)}, f32[128,1536]{1,0:T(8,128)}, f32[128,1536]{1,0:T(8,128)}, f32[8,1536]{1,0:T(8,128)}, bf16[1024,1536]{1,0:T(8,128)(2,1)}, /*index=5*/bf16[384,1536]{1,0:T(8,128)(2,1)}) custom-call(bf16[1024,1536]{1,0:T(8,128)(2,1)} %add_convert_fusion.refs_0_, bf16[1024,1536]{1,0:T(8,128)(2,1)} %convolution_convert_fusion.1.refs_1_, ...), custom_call_target="tpu_custom_call" | custom-call | flops 8000000000 | bytes 150000000 | tf_op jit(solution)/shard_map/backward_step/pallas_call | solution.py:1199
  259.1 3.0 fusion.4
  262.2 0.0 copy-done.8
  262.2 1.8 fusion.3
  264.2 1.5 copy-done.10
  265.7 3.5 %convolution_convert_fusion.refs_0_ = bf16[1024,1536]{1,0:T(8,128)(2,1)} fusion(bf16[1024,512]{1,0:T(8,128)(2,1)S(1)} %copy-done.8, bf16[768,1536]{1,0:T(8,128)(2,1)S(1)} %copy-done.10), kind=kOutput, calls=%fused_computation.3 | convolution fusion | flops 1612185600 | bytes 5767168 | tf_op jit(solution)/shard_map/dot_general | solution.py:47
  269.2 52.6 %last_step.1 = (f32[128,1536]{1,0:T(8,128)}, f32[8,1536]{1,0:T(8,128)}, bf16[144,1536]{1,0:T(8,128)(2,1)}, bf16[384,1536]{1,0:T(8,128)(2,1)}) custom-call(bf16[1024,1536]{1,0:T(8,128)(2,1)} %convolution_convert_fusion.refs_0_, bf16[128,1536]{1,0:T(8,128)(2,1)} %bitcast.36, f32[128,1536]{1,0:T(8,128)} %get-tuple-element.57.refs_2_, ...), custom_call_target="tpu_custom_call" | custom-call | bytes 150000000 | tf_op jit(solution)/shard_map/last_step/pallas_call | solution.py:954
  321.8 0.8 slice.59
  322.6 1.3 multiply_subtract_fusion
  324.0 0.6 pad_maximum_fusion.1
  324.6 13.9 %update_all.1 = (f32[384,1536]{1,0:T(8,128)}, f32[384,1536]{1,0:T(8,128)}, f32[2,384,1536]{2,1,0:T(8,128)}, f32[144,1536]{1,0:T(8,128)}, f32[144,1536]{1,0:T(8,128)}, /*index=5*/f32[2,144,1536]{2,1,0:T(8,128)}) custom-call(bf16[384,1536]{1,0:T(8,128)(2,1)} %get-tuple-element.62.refs_0_, f32[384,1536]{1,0:T(8,128)} %refs_1_.1, f32[2,384,1536]{2,1,0:T(8,128)} %refs_2_.1, ...), custom_call_target="tpu_custom_call" | custom-call | flops 20000000 | bytes 25000000 | tf_op jit(solution)/shard_map/update_all/pallas_call | solution.py:1274
  338.5 0.9 copy.27
  339.4 0.9 copy.28
  (28 shorter events, 0.2 us)
Async XLA Ops:
  145.1 4.3 %copy-start.3 = (bf16[1536,1536]{1,0:T(8,128)(2,1)S(1)}, bf16[1536,1536]{1,0:T(8,128)(2,1)}, u32[]{:S(2)}) copy-start(bf16[1536,1536]{1,0:T(8,128)(2,1)} %get-tuple-element.46) | copy-start | bytes 14155780
  145.1 4.7 %copy-start.7 = (bf16[1024,1536]{1,0:T(8,128)(2,1)S(1)}, bf16[1024,1536]{1,0:T(8,128)(2,1)}, u32[]{:S(2)}) copy-start(bf16[1024,1536]{1,0:T(8,128)(2,1)} %get-tuple-element.47) | copy-start | bytes 9437188
  156.2 1.9 copy-start.6
  171.2 87.9 %copy-start.9 = (bf16[1024,256]{1,0:T(8,128)(2,1)S(1)}, bf16[1024,256]{1,0:T(8,128)(2,1)}, u32[]{:S(2)}) copy-start(bf16[1024,256]{1,0:T(8,128)(2,1)} %get-tuple-element.53.refs_13_) | copy-start | bytes 1572868
  259.1 3.1 copy-start.5
  259.1 3.1 copy-start.8
  264.1 1.7 copy-start.10
  265.7 3.5 %copy-start = (bf16[576,1536]{1,0:T(8,128)(2,1)}, bf16[576,1536]{1,0:T(8,128)(2,1)S(1)}, u32[]{:S(2)}) copy-start(bf16[576,1536]{1,0:T(8,128)(2,1)S(1)} %slice_dynamic-update-slice_fusion.refs_5_) | copy-start | bytes 5308420
  269.2 53.5 %copy-start.4 = (f32[2,2,48]{2,1,0:T(2,128)S(1)}, f32[2,2,48]{2,1,0:T(2,128)}, u32[]{:S(2)}) copy-start(f32[2,2,48]{2,1,0:T(2,128)} %param.17) | copy-start | bytes 2308
  324.6 13.9 %copy-start.1 = (f32[128,1536]{1,0:T(8,128)S(1)}, f32[128,1536]{1,0:T(8,128)}, u32[]{:S(2)}) copy-start(f32[128,1536]{1,0:T(8,128)} %get-tuple-element.55) | copy-start | bytes 2359300
  324.6 14.8 %copy-start.2 = (f32[128,1536]{1,0:T(8,128)S(1)}, f32[128,1536]{1,0:T(8,128)}, u32[]{:S(2)}) copy-start(f32[128,1536]{1,0:T(8,128)} %get-tuple-element.61) | copy-start | bytes 2359300

commit v4 on v3

--- a/solution.py
+++ b/solution.py
@@ -24,7 +24,7 @@
 LANES = 128
 TILE = 256
 CHUNK = 16
-VMEM_LIMIT = 62 * 1024 * 1024
+VMEM_LIMIT = 67_000_000
 EVERY = ("fsdp", "context")
 BF = jnp.bfloat16
 F32 = jnp.float32
@@ -593,19 +593,16 @@
 
 class Reduce:
     @staticmethod
-    def scratch(chips, rows, width):
-        return [
-            pltpu.VMEM((chips, rows, width), BF),
-            pltpu.VMEM((chips, rows, width), BF),
-            pltpu.VMEM((chips, rows, width), BF),
-            pltpu.SemaphoreType.DMA((chips,)),
-            pltpu.SemaphoreType.DMA((chips,)),
-            pltpu.SemaphoreType.DMA((chips,)),
-            pltpu.SemaphoreType.DMA((chips,)),
-        ]
-
-    def __init__(self, part, chips, rows, scratch):
-        self.near, self.summed, self.far, near_send, near_recv, self.far_send, self.far_recv = scratch
+    def buffers(chips, rows, width):
+        return [pltpu.VMEM((chips, rows, width), BF), pltpu.VMEM((chips - 1, rows, width), BF)]
+
+    @staticmethod
+    def semaphores(chips):
+        return [pltpu.SemaphoreType.DMA((chips,))] * 4
+
+    def __init__(self, part, chips, rows, buffers, semaphores):
+        self.near, self.far = buffers
+        near_send, near_recv, self.far_send, self.far_recv = semaphores
         me = lax.axis_index("context")
         self.part, self.chips, self.rows, self.me = part, chips, rows, me
         self.near_copies = {}
@@ -628,16 +625,16 @@
 
             @pl.loop(0, self.rows // CHUNK)
             def add(k):
-                at = pl.ds(pl.multiple_of(k * CHUNK, CHUNK), CHUNK)
+                at = chunk_rows(k)
                 from_part = pl.ds(pl.multiple_of(first + k * CHUNK, CHUNK), CHUNK)
-                self.summed[step, at, :] = (
+                self.near[step, at, :] = (
                     self.part[from_part, :].astype(F32) + self.near[step, at, :].astype(F32)
                 ).astype(BF)
 
             self.far_copies.append(
                 send(
-                    self.summed.at[step],
-                    self.far.at[step],
+                    self.near.at[step],
+                    self.far.at[step - 1],
                     self.far_send.at[step],
                     self.far_recv.at[step],
                     {"context": target},
@@ -650,12 +647,12 @@
             copy.wait_recv()
 
     def total(self, k):
-        at = pl.ds(pl.multiple_of(k * CHUNK, CHUNK), CHUNK)
+        at = chunk_rows(k)
         first = pl.multiple_of(self.me * self.rows, self.rows)
         value = self.part[pl.ds(pl.multiple_of(first + k * CHUNK, CHUNK), CHUNK), :].astype(F32)
         value = value + self.near[0, at, :].astype(F32)
         for step in range(1, self.chips):
-            value = value + self.far[step, at, :].astype(F32)
+            value = value + self.far[step - 1, at, :].astype(F32)
         return value
 
     def drain(self):
@@ -848,11 +845,11 @@
     else:
         attn_owners = homes.attn_owners()
         greet(columns, layers, [spot[:2] for spot in homes.attn_targets() + attn_owners])
-    first = Reduce(part_in, chips, rows, scratch[:7])
+    first = Reduce(part_in, chips, rows, scratch[0:2], scratch[2:6])
     if homes is not None:
         attn_rows, ffn_rows = term.shape[0] // layers, ffn_sum.shape[0]
-        attn_done = scratch[7]
-        line = LineReduce(term, layers, 3, scratch[8:14])
+        attn_done = scratch[6]
+        line = LineReduce(term, layers, 3, scratch[7:13])
         unit_ffn = ffn_rows // 3
     first.exchange()
     if homes is not None:
@@ -860,7 +857,7 @@
             [ffn_sum.at[pl.ds(k * unit_ffn, unit_ffn), :] for k in range(3)],
             functools.partial(place_rows, ffn_back, unit_ffn),
             homes.ffn_owners(),
-            scratch[14:16],
+            scratch[13:15],
         )
         line.relay(3)
     own_sums[...] = jnp.zeros_like(own_sums)
@@ -900,7 +897,7 @@
             [attn_done.at[pl.ds(k * unit, unit), :] for k in range(3)],
             functools.partial(place_rows, attn_back, unit),
             attn_owners,
-            scratch[16:18],
+            scratch[15:17],
         )
     total = own_sums[...]
     for step, copy in enumerate(in_plane):
@@ -969,7 +966,8 @@
             pltpu.SemaphoreType.DMA((columns,)),
             pltpu.SemaphoreType.DMA((layers,)),
             pltpu.SemaphoreType.DMA((layers,)),
-            *Reduce.scratch(chips, rows, width),
+            *Reduce.buffers(chips, rows, width),
+            *Reduce.semaphores(chips),
             *back_scratch,
         ],
         compiler_params=comm_params(5),
@@ -1043,7 +1041,7 @@
         at = pl.ds(pl.multiple_of(i * TILE, TILE), TILE)
         part_ref[at, :] = plain_times(att_ref[at, :], pad_ref[width:, :]).astype(BF)
 
-    reduce = Reduce(part_ref, chips, own_rows, scratch[10:17])
+    reduce = Reduce(part_ref, chips, own_rows, scratch[10:12], scratch[12:16])
     line.relay(1)
     reduce.exchange()
     line.relay(1)
@@ -1058,7 +1056,7 @@
         middle_ref[at, :] = middle
         hidden[at, :] = (middle * rms_scale(middle) * (1.0 + gain_ref[...])).astype(BF)
 
-    gather = Gather(hidden, h2_full, chips, scratch[17:22])
+    gather = Gather(hidden, h2_full, chips, scratch[16:21])
     line.relay(2)
     gather.pass_on()
     line.relay()
@@ -1093,7 +1091,8 @@
             pltpu.VMEM((rows, width), BF),
             *LineGather.scratch(layers, 3),
             *Gather.scratch(chips),
-            *Reduce.scratch(chips, rows, width),
+            *Reduce.buffers(chips, rows, width),
+            *Reduce.semaphores(chips),
             *Gather.scratch(chips),
         ],
         compiler_params=comm_params(3),
@@ -1102,20 +1101,112 @@
     )(h_full, w_col, cosine, sine, starts, x_own, gain_row, dy_own, ffn_shard)
 
 
-def backward_kernel(columns, layers, heads, *refs):
-    (part_back, part_out, term, middle_ref, dy_ref, gain_ref, pad_ref), refs = refs[:7], refs[7:]
-    (cos_ref, sin_ref, start_ref, q_ref, k_ref, v_ref, att_ref, log_ref), refs = refs[:8], refs[8:]
-    (out_ref, block_out_ref, grad_ref, sums_ref, gm_full, ffn_sum), refs = refs[:6], refs[6:]
-    (grad_bf, ga_ref, dk_ref, dv_ref), scratch = refs[:4], refs[4:]
+class Load:
+    def __init__(self, source, target, sems, blocks=1):
+        size = source.shape[0] // blocks
+        self.copies = []
+        for k in range(blocks):
+            at = pl.ds(k * size, size)
+            copy = pltpu.make_async_copy(source.at[at, :], target.at[at, :], sems.at[k])
+            copy.start()
+            self.copies.append(copy)
+        self.next = 0
+
+    def wait(self, count=None):
+        stop = len(self.copies) if count is None else self.next + count
+        for copy in self.copies[self.next : stop]:
+            copy.wait()
+        self.next = stop
+
+
+def columns_of(width, most=512):
+    return most, width // most
+
+
+def backward_kernel(columns, layers, heads, sharers, factor, *refs):
+    (h2_hbm, dy_hbm, w_hbm, h_hbm, pad_hbm), refs = refs[:5], refs[5:]
+    (cos_hbm, sin_hbm, start_hbm, q_hbm, k_hbm, v_hbm, att_hbm, log_hbm), refs = refs[:8], refs[8:]
+    (middle_ref, dy_ref, gain_ref), refs = refs[:3], refs[3:]
+    (block_out_ref, grad_ref, sums_ref, ffn_sum, term_in, in_part), refs = refs[:6], refs[6:]
+    (x_ref, y_ref, w_ref, pad_ref, cos_ref, sin_ref, start_ref), refs = refs[:7], refs[7:]
+    (q_ref, k_ref, v_ref, att_ref, log_ref), refs = refs[:5], refs[5:]
+    (act_ref, gg_ref, gu_ref, act_t, gg_t, gu_t, term, part_ref), refs = refs[:8], refs[8:]
+    (gm_full, grad_bf, dk_ref, dv_ref, out_ref, out_t), refs = refs[:6], refs[6:]
+    ga_ref, shared_ref = gg_ref.at[:, 0 : heads * LANES], act_ref.at[:, 0 : 2 * LANES]
+    load_sems, store_sem, shared_send, shared_recv, *scratch = refs
     seq, own_rows, chips = gm_full.shape[0], middle_ref.shape[0], columns // 2
+    hidden = w_ref.shape[0] // 3
+    tiles = seq // TILE
+    block, blocks = columns_of(w_ref.shape[1])
+    w_load = Load(w_hbm, w_ref, load_sems.at[pl.ds(0, 3)], 3)
+    h2_load = Load(h2_hbm, x_ref, load_sems.at[pl.ds(3, 1)])
+    dy_load = Load(dy_hbm, y_ref, load_sems.at[pl.ds(4, 1)])
+    later = [
+        Load(source, target, load_sems.at[pl.ds(5 + k, 1)])
+        for k, (source, target) in enumerate(
+            (
+                (pad_hbm, pad_ref),
+                (cos_hbm, cos_ref),
+                (sin_hbm, sin_ref),
+                (start_hbm, start_ref),
+                (q_hbm, q_ref),
+                (k_hbm, k_ref),
+                (v_hbm, v_ref),
+                (att_hbm, att_ref),
+                (log_hbm, log_ref),
+            )
+        )
+    ]
     greet(columns, layers)
-    back = Reduce(part_back, chips, own_rows, scratch[0:7])
-    line = LineReduce(term, layers, 3, scratch[7:13])
+    w_gate, w_up, w_down = (pl.ds(k * hidden, hidden) for k in range(3))
+
+    w_load.wait()
+    h2_load.wait()
+    dy_load.wait()
+
+    @pl.loop(0, tiles)
+    def feed_forward(i):
+        at = pl.ds(pl.multiple_of(i * TILE, TILE), TILE)
+        gate = product_transposed(x_ref[at, :], w_ref[w_gate, :])
+        up = product_transposed(x_ref[at, :], w_ref[w_up, :])
+        grad_act = product_transposed(y_ref[at, :], w_ref[w_down, :])
+        sigmoid = 1.0 / (1.0 + jnp.exp(-gate))
+        swish = gate * sigmoid
+        act_ref[at, :] = (swish * up).astype(BF)
+        gg_ref[at, :] = (grad_act * up * sigmoid * (1.0 + gate * (1.0 - sigmoid))).astype(BF)
+        gu_ref[at, :] = (grad_act * swish).astype(BF)
+        act_t[:, at] = jnp.transpose(act_ref[at, :])
+        gg_t[:, at] = jnp.transpose(gg_ref[at, :])
+        gu_t[:, at] = jnp.transpose(gu_ref[at, :])
+
+    @pl.loop(0, blocks)
+    def weight_gradients(j):
+        at = pl.ds(pl.multiple_of(j * block, block), block)
+        for rows, left, right in ((w_gate, gg_t, x_ref), (w_up, gu_t, x_ref), (w_down, act_t, y_ref)):
+            term[rows, at] = (plain_times(left[...], right[:, at]) * factor).astype(BF)
+
+    line = LineReduce(term, layers, 3, scratch[0:6])
+    h_load = Load(h_hbm, x_ref, load_sems.at[pl.ds(14, 1)])
+
+    @pl.loop(0, tiles)
+    def back_part(i):
+        at = pl.ds(pl.multiple_of(i * TILE, TILE), TILE)
+        part_ref[at, :] = (
+            plain_times(gg_ref[at, :], w_ref[w_gate, :]) + plain_times(gu_ref[at, :], w_ref[w_up, :])
+        ).astype(BF)
+
+    back = Reduce(part_ref, chips, own_rows, scratch[6:8], scratch[8:12])
     sums_ref[...] = jnp.zeros_like(sums_ref)
+
+    @pl.loop(0, tiles)
+    def out_part(i):
+        at = pl.ds(pl.multiple_of(i * TILE, TILE), TILE)
+        y_ref[at, :] = plain_times(act_ref[at, :], w_ref[w_down, :]).astype(BF)
+
     back.exchange()
-    out = Reduce(part_out, chips, own_rows, scratch[13:20])
-    line.relay(1)
+    line.relay(2)
     back.arrive()
+    back.drain()
 
     @pl.loop(0, own_rows // CHUNK)
     def turn(k):
@@ -1129,22 +1220,24 @@
         grad_ref[at, :] = grad
         grad_bf[at, :] = grad.astype(BF)
 
-    gather = Gather(grad_bf, gm_full, chips, scratch[20:25])
+    gather = Gather(grad_bf, gm_full, chips, scratch[12:17])
+    line.relay(1)
+    gather.pass_on()
     line.relay(2)
-    out.exchange()
-    gather.pass_on()
-    line.relay(1)
     gather.finish()
-    line.relay(1)
+    out = Reduce(y_ref, chips, own_rows, scratch[6:8], scratch[17:21])
+    for load in later:
+        load.wait()
 
     scale = HEAD_SIZE**-0.5
     width = (heads + 2) * LANES
 
-    @pl.loop(0, seq // TILE)
+    @pl.loop(0, tiles)
     def attended_gradient(i):
         at = pl.ds(pl.multiple_of(i * TILE, TILE), TILE)
         ga_ref[at, :] = product_transposed(gm_full[at, :], pad_ref[width:, :]).astype(BF)
 
+    out.exchange()
     dk_ref[...] = jnp.zeros_like(dk_ref)
     dv_ref[...] = jnp.zeros_like(dv_ref)
     low = lax.broadcasted_iota(jnp.int32, (TILE, LANES), 1) < HEAD_SIZE // 2
@@ -1152,7 +1245,7 @@
     def turn_back(u, rows):
         return (u * cos_ref[rows, :] - turned(u, low) * sin_ref[rows, :]).astype(BF)
 
-    for i in range(seq // TILE):
+    for i in range(tiles):
         rows = slice(i * TILE, (i + 1) * TILE)
         for head in range(heads):
             lanes = slice(head * LANES, (head + 1) * LANES)
@@ -1171,11 +1264,54 @@
                 dk_ref[keys, :] += transposed_times(ds, q)
                 dv_ref[keys, :] += transposed_times(p.astype(BF), ga)
             out_ref[rows, lanes] = turn_back(dq, rows)
-    for i in range(seq // TILE):
+        if i == tiles // 2:
+            line.relay(1)
+    line.relay(1)
+    for i in range(tiles):
         rows = slice(i * TILE, (i + 1) * TILE)
         out_ref[rows, heads * LANES : (heads + 1) * LANES] = turn_back(dk_ref[rows, :], rows)
         out_ref[rows, (heads + 1) * LANES :] = dv_ref[rows, :].astype(BF)
-    line.relay(2)
+    if sharers > 1:
+        me = lax.axis_index("context")
+        both = pl.ds(heads * LANES, 2 * LANES)
+        copy = send(
+            out_ref.at[:, both], shared_ref, shared_send, shared_recv, {"context": sibling_of(me)}
+        )
+        copy.wait()
+        lane = lax.broadcasted_iota(jnp.int32, (TILE, 2 * LANES), 1) % LANES
+        kept = lane // (HEAD_SIZE // sharers) == lax.rem(me, 2)
+        for i in range(tiles):
+            rows = slice(i * TILE, (i + 1) * TILE)
+            value = out_ref[rows, both].astype(F32) + shared_ref[rows, :].astype(F32)
+            out_ref[rows, both] = jnp.where(kept, value, 0.0).astype(BF)
+    for i in range(tiles):
+        rows = slice(i * TILE, (i + 1) * TILE)
+        out_t[0:width, rows] = jnp.transpose(out_ref[rows, :])
+        out_t[width:, rows] = jnp.transpose(att_ref[rows, :])
+
+    @pl.loop(0, tiles)
+    def input_part(i):
+        at = pl.ds(pl.multiple_of(i * TILE, TILE), TILE)
+        part_ref[at, :] = plain_times(out_ref[at, :], pad_ref[0:width, :]).astype(BF)
+
+    store = pltpu.make_async_copy(part_ref, in_part, store_sem)
+    store.start()
+    h_load.wait()
+
+    @pl.loop(0, blocks)
+    def attention_gradients(j):
+        at = pl.ds(pl.multiple_of(j * block, block), block)
+        inner = (plain_times(out_t[0:width, :], x_ref[:, at]) * factor).astype(BF)
+        outer = (plain_times(out_t[width:, :], gm_full[:, at]) * factor).astype(BF)
+        for value, first, count in ((inner, 0, heads + 2), (outer, heads + 2, heads)):
+            for k in range(count):
+                if sharers > 1:
+                    term_in[pl.ds((first + k) * LANES, LANES), at] = value[k * LANES : (k + 1) * LANES, :]
+                else:
+                    term_in[pl.ds((first + k) * HEAD_SIZE, HEAD_SIZE), at] = value[
+                        k * LANES : k * LANES + HEAD_SIZE, :
+                    ]
+
     out.arrive()
 
     @pl.loop(0, own_rows // CHUNK)
@@ -1184,44 +1320,63 @@
         block_out_ref[at, :] = middle_ref[at, :] + out.total(k)
 
     line.finish(ffn_sum)
+    store.wait()
     line.drain()
-    back.drain()
     out.drain()
 
 
 def backward_step(
-    part_back, part_out, term, middle, dy_own, gain_row, padded, tables, saved, heads, columns, layers
+    h2_full, dy_full, ffn_col, h_full, padded, tables, saved, middle, dy_own, gain_row, heads, columns, layers, sharers
 ):
-    seq, width = part_back.shape
+    seq, width = h2_full.shape
     rows = seq // columns
     chips = columns // 2
-    ffn_rows = term.shape[0] // layers
+    hidden = ffn_col.shape[0] // 3
+    ffn_rows = ffn_col.shape[0] // layers
+    each = HEAD_SIZE if sharers == 1 else LANES
+    loaded = [ffn_col, padded, *tables, *saved]
     return pl.pallas_call(
-        functools.partial(backward_kernel, columns, layers, heads),
+        functools.partial(
+            backward_kernel, columns, layers, heads, sharers, float(seq * layers) ** (-0.5)
+        ),
         out_shape=(
-            jax.ShapeDtypeStruct((seq, (heads + 2) * LANES), BF),
             jax.ShapeDtypeStruct((rows, width), F32),
             jax.ShapeDtypeStruct((rows, width), F32),
             jax.ShapeDtypeStruct((8, width), F32),
+            jax.ShapeDtypeStruct((ffn_rows, width), BF),
+            jax.ShapeDtypeStruct(((2 * heads + 2) * each, width), BF),
             jax.ShapeDtypeStruct((seq, width), BF),
-            jax.ShapeDtypeStruct((ffn_rows, width), BF),
         ),
-        in_specs=vmem_specs(15),
-        out_specs=tuple(vmem_specs(6)),
+        in_specs=[pl.BlockSpec(memory_space=pl.ANY)] * 13 + vmem_specs(3),
+        out_specs=tuple(vmem_specs(5) + [pl.BlockSpec(memory_space=pl.ANY)]),
         scratch_shapes=[
+            pltpu.VMEM((seq, width), BF),
+            pltpu.VMEM((seq, width), BF),
+            *[pltpu.VMEM(array.shape, array.dtype) for array in loaded],
+            *[pltpu.VMEM((seq, hidden), BF)] * 3,
+            *[pltpu.VMEM((hidden, seq), BF)] * 3,
+            pltpu.VMEM(ffn_col.shape, BF),
+            pltpu.VMEM((seq, width), BF),
+            pltpu.VMEM((seq, width), BF),
             pltpu.VMEM((rows, width), BF),
-            pltpu.VMEM((seq, heads * LANES), BF),
             pltpu.VMEM((seq, LANES), F32),
             pltpu.VMEM((seq, LANES), F32),
-            *Reduce.scratch(chips, rows, width),
+            pltpu.VMEM((seq, (heads + 2) * LANES), BF),
+            pltpu.VMEM(((2 * heads + 2) * LANES, seq), BF),
+            pltpu.SemaphoreType.DMA((15,)),
+            pltpu.SemaphoreType.DMA,
+            pltpu.SemaphoreType.DMA,
+            pltpu.SemaphoreType.DMA,
             *LineReduce.scratch(layers, 3, ffn_rows, width),
-            *Reduce.scratch(chips, rows, width),
+            *Reduce.buffers(chips, rows, width),
+            *Reduce.semaphores(chips),
             *Gather.scratch(chips),
+            *Reduce.semaphores(chips),
         ],
         compiler_params=comm_params(4),
         name="backward_step",
-        cost_estimate=pl.CostEstimate(flops=8_000_000_000, bytes_accessed=150_000_000, transcendentals=2_000_000),
-    )(part_back, part_out, term, middle, dy_own, gain_row, padded, *tables, *saved)
+        cost_estimate=pl.CostEstimate(flops=28_000_000_000, bytes_accessed=150_000_000, transcendentals=4_000_000),
+    )(h2_full, dy_full, ffn_col, h_full, padded, *tables, *saved, middle, dy_own, gain_row)
 
 
 def update_rows(g_ref, p_ref, m_ref, grad_ref, new_p_ref, new_m_ref):
@@ -1317,7 +1472,6 @@
     heads = QUERY_HEADS // columns
     sharers = max(1, columns // KEY_VALUE_HEADS)
     share = KEY_VALUE_HEADS * HEAD_SIZE // columns
-    hidden = ffn_weights.shape[0] * layers // 3
     grad_factor = float(rows * layers * columns) ** (-0.5)
     attn_plan, ffn_plan = unit_plans(layers, columns, attn_weights.shape[0] * layers * columns)
     core = lax.rem(lax.axis_index("context"), 2)
@@ -1365,60 +1519,35 @@
     *saved, padded, middle, h2_full, dy_full, ffn_col = forward_step(
         h_full, attn_col, *tables, x_own, norm_gains[1:2], dy_own, ffn_shard, heads, columns, layers
     )
-    attended = saved[3]
-    w_gate, w_up, w_down = ffn_col[:hidden], ffn_col[hidden : 2 * hidden], ffn_col[2 * hidden :]
-
-    gate_pre = product_transposed(h2_full, w_gate)
-    up_pre = product_transposed(h2_full, w_up)
-    sigmoid_gate = jax.nn.sigmoid(gate_pre)
-    activated = (gate_pre * sigmoid_gate * up_pre).astype(BF)
-    grad_act = product_transposed(dy_full, w_down)
-    grad_gate = (grad_act * up_pre * sigmoid_gate * (1.0 + gate_pre * (1.0 - sigmoid_gate))).astype(BF)
-    grad_up = (grad_act * gate_pre * sigmoid_gate).astype(BF)
-    ffn_term = jnp.concatenate(
-        [
-            (transposed_times(grad_gate, h2_full) * grad_factor).astype(BF),
-            (transposed_times(grad_up, h2_full) * grad_factor).astype(BF),
-            (transposed_times(activated, dy_full) * grad_factor).astype(BF),
-        ]
-    )
-    out_part = plain_times(activated, w_down).astype(BF)
-    back_part = (plain_times(grad_gate, w_gate) + plain_times(grad_up, w_up)).astype(BF)
-
-    grads, block_out, grad_middle, sums, gm_full, ffn_sum = backward_step(
-        back_part,
-        out_part,
-        ffn_term,
+
+    block_out, grad_middle, sums, ffn_sum, attn_term, in_part = backward_step(
+        h2_full,
+        dy_full,
+        ffn_col,
+        h_full,
+        padded,
+        tables,
+        saved,
         middle,
         dy_own,
         norm_gains[1:2],
-        padded,
-        tables,
-        saved,
         heads,
         columns,
         layers,
+        sharers,
     )
     if sharers > 1:
-        shared = grads[:, heads * LANES :]
-        shared = (shared.astype(F32) + lax.ppermute(shared, "context", swap).astype(F32)).astype(BF)
-        lane = jnp.arange(2 * LANES, dtype=jnp.int32) % LANES // share
-        grads = jnp.concatenate(
-            [grads[:, : heads * LANES], jnp.where(lane == core, shared, jnp.zeros_like(shared))], axis=1
-        )
-    term_in = (transposed_times(grads, h_full) * grad_factor).astype(BF)
-    term_out = (transposed_times(attended, gm_full) * grad_factor).astype(BF)
-    if sharers > 1:
         own_rows = [
-            lax.dynamic_slice_in_dim(term_in, (heads + k) * LANES + core * share, share, 0)
+            lax.dynamic_slice_in_dim(attn_term, (heads + k) * LANES + core * share, share, 0)
             for k in range(2)
         ]
         attn_term = jnp.concatenate(
-            [unpadded(term_in, heads), *own_rows, unpadded(term_out, heads)]
+            [
+                unpadded(attn_term, heads),
+                *own_rows,
+                unpadded(attn_term[(heads + 2) * LANES :], heads),
+            ]
         )
-    else:
-        attn_term = jnp.concatenate([unpadded(term_in, heads + 2), unpadded(term_out, heads)])
-    in_part = plain_times(grads, padded[: (heads + 2) * LANES]).astype(BF)
     last_args = (in_part, x_own, grad_middle, norm_gains[0:1], sums, columns, layers)
     if aligned:
         grad_input, gain_sums, attn_shard, ffn_shard = last_step(*last_args, (attn_term, ffn_sum))

time: 341 us -> 317 us (0.930)
  matrix products: 31.6 us -> 0 us
  Pallas kernels: 292 us -> 302 us
    dot_general x12 -> x0, matrix products: 31.6 us -> none  [the longest x4 12.4 us: plain_times(): return jnp.dot(left_matrix, right_matrix, preferred_element_type=F32)]
    pallas_call x1, Pallas kernels: 87.9 us -> 95.8 us  [backward_step(): pl.pallas_call(functools.partial(backward_kernel, columns, layers, heads,...]
where the time goes in v4:
time: 317 us; the launch traced here: 316 us
  Pallas kernels  302 us (95%)
  local copies, waits for them, and re-layouts  7.41 us (2%)
  other arithmetic  6.45 us (2%)
    pallas_call x1, Pallas kernels, backward_step(): pl.pallas_call(functools.partial(backward_kernel, columns, layers, heads,...  95.8 us
    pallas_call x1, Pallas kernels, forward_step(): pl.pallas_call(functools.partial(forward_kernel, columns, layers, heads),...  85.1 us
    pallas_call x1, Pallas kernels, last_step(): pl.pallas_call(functools.partial(last_kernel, columns, layers, homes), ou...  54.7 us
    pallas_call x1, Pallas kernels, open_step(): pl.pallas_call(functools.partial(open_kernel, columns, layers, homes), ou...  52.3 us
    pallas_call x1, Pallas kernels, update_all(): pl.pallas_call(functools.partial(update_kernel, steps), grid=(steps + res...  13.8 us

profile of v4, /device:TPU:0, one launch (start us, length us, event | category | flops | bytes accessed | tf_op | source)
XLA Modules:
  0.0 316.3 jit_solution(9674384559517954195)
XLA Ops:
  0.6 1.4 fusion.2
  2.0 52.3 %open_step.1 = (bf16[1024,1536]{1,0:T(8,128)(2,1)}, s32[8,128]{1,0:T(8,128)}, bf16[576,1536]{1,0:T(8,128)(2,1)}, bf16[384,1536]{1,0:T(8,128)(2,1)}) custom-call(bf16[128,1536]{1,0:T(8,128)(2,1)} %bitcast.17, f32[1,1536]{1,0:T(1,128)} %get-tuple-element.76.gain_ref.refs_3_, s32[1,128]{1,0:T(1,128)} %docs.1, f32[144,1536]{1,0:T(8,128)} %refs_4_.1, ...), custom_call_target="tpu_custom_call" | custom-call | bytes 150000000 | tf_op jit(solution)/shard_map/open_step/pallas_call | solution.py:780
  54.3 1.3 convert_reduce_fusion
  55.6 1.9 fusion
  57.6 0.1 pad.7.clone
  57.6 1.3 maximum_maximum_fusion.1
  58.9 1.0 broadcast_in_dim.18.refs_4_.refs_7_
  59.9 85.1 %forward_step.1 = (bf16[1024,256]{1,0:T(8,128)(2,1)}, bf16[1024,128]{1,0:T(8,128)(2,1)}, bf16[1024,128]{1,0:T(8,128)(2,1)}, bf16[1024,256]{1,0:T(8,128)(2,1)}, f...) custom-call(bf16[1024,1536]{1,0:T(8,128)(2,1)} %get-tuple-element.41, ...), custom_call_target="tpu_custom_call" | custom-call | flops 6000000000 | bytes 150000000 | tf_op jit(solution)/shard_map/forward_step/pallas_call | solution.py:1073
  145.1 95.8 %backward_step.1 = (f32[128,1536]{1,0:T(8,128)}, f32[128,1536]{1,0:T(8,128)}, f32[8,1536]{1,0:T(8,128)}, bf16[384,1536]{1,0:T(8,128)(2,1)}, bf16[576,1536]{1,0:T(8,128)(2,1)}, /*index=5*/bf16[1024,1536]{1,0:T(8,128)(2,1)}) custom-call(bf16[1024,1536]{1,0:T(8,128)(2,1)} %get-tuple-element.45.refs_0_, bf16[1024,1536]{1,0:T(8,128)(2,1)} %get-tuple-element.46.refs_1_, ...), custom_call_target="tpu_custom_call" | custom-call | flops 28000000000 | bytes 150000000 | tf_op jit(solution)/shard_map/backward_step/pallas_call | solution.py:1338
  240.8 0.0 copy-start
  240.9 54.7 %last_step.1 = (f32[128,1536]{1,0:T(8,128)}, f32[8,1536]{1,0:T(8,128)}, bf16[144,1536]{1,0:T(8,128)(2,1)}, bf16[384,1536]{1,0:T(8,128)(2,1)}) custom-call(bf16[1024,1536]{1,0:T(8,128)(2,1)} %get-tuple-element.56.refs_0_, bf16[128,1536]{1,0:T(8,128)(2,1)} %bitcast.19, f32[128,1536]{1,0:T(8,128)} %get-tuple-element.57.refs_2_, ...), custom_call_target="tpu_custom_call" | custom-call | bytes 150000000 | tf_op jit(solution)/shard_map/last_step/pallas_call | solution.py:951
  295.6 0.8 slice.19
  296.4 0.0 copy-done
  296.4 1.3 multiply_subtract_fusion
  297.7 0.6 pad_maximum_fusion
  298.3 13.8 %update_all.1 = (f32[384,1536]{1,0:T(8,128)}, f32[384,1536]{1,0:T(8,128)}, f32[2,384,1536]{2,1,0:T(8,128)}, f32[144,1536]{1,0:T(8,128)}, f32[144,1536]{1,0:T(8,128)}, /*index=5*/f32[2,144,1536]{2,1,0:T(8,128)}) custom-call(bf16[384,1536]{1,0:T(8,128)(2,1)} %get-tuple-element.62.refs_0_, f32[384,1536]{1,0:T(8,128)} %refs_1_.1, f32[2,384,1536]{2,1,0:T(8,128)} %refs_2_.1, ...), custom_call_target="tpu_custom_call" | custom-call | flops 20000000 | bytes 25000000 | tf_op jit(solution)/shard_map/update_all/pallas_call | solution.py:1429
  312.1 2.1 copy.22
  314.2 2.1 copy.23
  (3 shorter events, 0.0 us)
Async XLA Ops:
  240.8 55.6 %copy-start = (f32[2,2,48]{2,1,0:T(2,128)S(1)}, f32[2,2,48]{2,1,0:T(2,128)}, u32[]{:S(2)}) copy-start(f32[2,2,48]{2,1,0:T(2,128)} %param.17) | copy-start | bytes 2308

commit v5 on v4

--- a/solution.py
+++ b/solution.py
@@ -704,129 +704,6 @@
         for copy in self.copies:
             copy.wait_send()
         self.local.wait()
-
-
-def open_kernel(
-    columns,
-    layers,
-    homes,
-    x_ref,
-    gain_ref,
-    docs,
-    attn_ref,
-    ffn_ref,
-    h_full,
-    docs_full,
-    attn_col,
-    ffn_shard,
-    hidden,
-    attn_bf,
-    ffn_bf,
-    attn_shard,
-    *scratch,
-):
-    attn_rows, ffn_rows = attn_ref.shape[0], ffn_ref.shape[0]
-
-    @pl.loop(0, attn_rows // CHUNK)
-    def cast_attn(k):
-        attn_bf[chunk_rows(k), :] = attn_ref[chunk_rows(k), :].astype(BF)
-
-    targets = homes.attn_targets()
-    greet(columns, layers, [spot[:2] for spot in targets + homes.attn_owners()])
-    unit = attn_rows // 3
-    attn_spread = Exchange(
-        [attn_bf.at[pl.ds(k * unit, unit), :] for k in range(3)],
-        functools.partial(place_rows, attn_shard, unit),
-        targets,
-        scratch[0:2],
-    )
-
-    @pl.loop(0, x_ref.shape[0] // CHUNK)
-    def norm(k):
-        residual = x_ref[chunk_rows(k), :].astype(F32)
-        hidden[chunk_rows(k), :] = (residual * rms_scale(residual) * (1.0 + gain_ref[...])).astype(BF)
-
-    documents = Docs(docs, docs_full, columns, scratch[2:5])
-    gather = Gather(hidden, h_full, columns // 2, scratch[5:10])
-
-    @pl.loop(0, ffn_rows // CHUNK)
-    def cast_ffn(k):
-        ffn_bf[chunk_rows(k), :] = ffn_ref[chunk_rows(k), :].astype(BF)
-
-    attn_spread.arrive()
-    line = LineGather(attn_col, attn_shard, layers, 1, scratch[10:15])
-    unit = ffn_rows // 3
-    ffn_spread = Exchange(
-        [ffn_bf.at[pl.ds(k * unit, unit), :] for k in range(3)],
-        functools.partial(place_rows, ffn_shard, unit),
-        homes.ffn_targets(),
-        scratch[15:17],
-    )
-    line.relay(1)
-    gather.pass_on()
-    line.relay()
-    documents.finish()
-    gather.finish()
-    ffn_spread.arrive()
-    line.finish()
-    attn_spread.drain()
-    ffn_spread.drain()
-
-
-def open_step(x_own, gain_row, docs, attn_weights, ffn_weights, columns, layers):
-    rows, width = x_own.shape
-    attn_rows, ffn_rows = attn_weights.shape[0], ffn_weights.shape[0]
-    homes = Homes(layers, columns, attn_rows * layers * columns)
-    return pl.pallas_call(
-        functools.partial(open_kernel, columns, layers, homes),
-        out_shape=(
-            jax.ShapeDtypeStruct((columns * rows, width), BF),
-            jax.ShapeDtypeStruct((columns, docs.shape[1]), jnp.int32),
-            jax.ShapeDtypeStruct((layers * attn_rows, width), BF),
-            jax.ShapeDtypeStruct((ffn_rows, width), BF),
-        ),
-        in_specs=vmem_specs(5),
-        out_specs=tuple([pl.BlockSpec(memory_space=pl.ANY)] * 4),
-        scratch_shapes=[
-            pltpu.VMEM((rows, width), BF),
-            pltpu.VMEM((attn_rows, width), BF),
-            pltpu.VMEM((ffn_rows, width), BF),
-            pltpu.VMEM((attn_rows, width), BF),
-            *Exchange.scratch(),
-            *Docs.scratch(columns),
-            *Gather.scratch(columns // 2),
-            *LineGather.scratch(layers, 1),
-            *Exchange.scratch(),
-        ],
-        compiler_params=comm_params(1),
-        name="open_step",
-        cost_estimate=pl.CostEstimate(flops=0, bytes_accessed=150_000_000, transcendentals=0),
-    )(x_own, gain_row, docs, attn_weights, ffn_weights)
-
-
-def gather_docs_kernel(columns, block, docs, full, docs_full, *scratch):
-    greet(columns)
-    gather = Gather(block, full, columns // 2, scratch[:5])
-    documents = Docs(docs, docs_full, columns, scratch[5:])
-    gather.finish()
-    documents.finish()
-
-
-def gather_docs(block, docs, columns):
-    rows, width = block.shape
-    return pl.pallas_call(
-        functools.partial(gather_docs_kernel, columns),
-        out_shape=(
-            jax.ShapeDtypeStruct((columns * rows, width), BF),
-            jax.ShapeDtypeStruct((columns, docs.shape[1]), jnp.int32),
-        ),
-        in_specs=vmem_specs(2),
-        out_specs=(pl.BlockSpec(memory_space=pl.ANY), pl.BlockSpec(memory_space=pl.ANY)),
-        scratch_shapes=[*Gather.scratch(columns // 2), *Docs.scratch(columns)],
-        compiler_params=comm_params(2),
-        name="gather_docs",
-        cost_estimate=pl.CostEstimate(flops=0, bytes_accessed=60_000_000, transcendentals=0),
-    )(block, docs)
 
 
 def last_kernel(columns, layers, homes, *refs):
@@ -987,14 +864,100 @@
     return (cols <= rows) & (cols >= starts)
 
 
-def forward_kernel(columns, layers, heads, *refs):
-    (h_ref, w_ref, cos_ref, sin_ref, start_ref, x_ref, gain_ref, dy_ref, ffn_shard), refs = refs[:9], refs[9:]
+def place_tables(docs_ref, freq_ref, cos_ref, sin_ref, start_ref):
+    blocks = docs_ref.shape[0]
+
+    @pl.loop(0, blocks)
+    def one_block(r):
+        at = pl.ds(pl.multiple_of(r * LANES, LANES), LANES)
+        mine = jnp.transpose(
+            jnp.broadcast_to(docs_ref[pl.ds(r, 1), :].astype(F32), (LANES, LANES))
+        )
+        earlier = jnp.zeros((LANES, LANES), F32)
+        for other in range(blocks):
+            theirs = docs_ref[other : other + 1, :].astype(F32)
+            earlier = earlier + jnp.where(theirs < mine, 1.0, 0.0)
+        starts = jnp.broadcast_to(jnp.sum(earlier, axis=1, keepdims=True), (LANES, LANES))
+        start_ref[at, :] = starts.astype(jnp.int32)
+        token = r * LANES + lax.broadcasted_iota(jnp.int32, (LANES, LANES), 0)
+        angles = (token.astype(F32) - starts) * freq_ref[...]
+        lane = lax.broadcasted_iota(jnp.int32, (LANES, LANES), 1)
+        sine = jnp.sin(angles)
+        cos_ref[at, :] = jnp.where(lane < HEAD_SIZE, jnp.cos(angles), 0.0)
+        sin_ref[at, :] = jnp.where(
+            lane < HEAD_SIZE // 2, -sine, jnp.where(lane < HEAD_SIZE, sine, 0.0)
+        )
+
+
+def forward_kernel(columns, layers, heads, homes, aligned, *refs):
+    (x_ref, gains_ref, docs_ref, freq_ref, dy_ref, attn_ref, ffn_ref), refs = refs[:7], refs[7:]
     (q_ref, k_ref, v_ref, att_ref, log_ref, pad_ref, middle_ref), refs = refs[:7], refs[7:]
-    (h2_full, dy_full, ffn_col), (part_ref, hidden, *scratch) = refs[:3], refs[3:]
+    (cos_ref, sin_ref, start_ref, h_ref), refs = refs[:4], refs[4:]
+    (h2_full, dy_full, ffn_col), refs = refs[:3], refs[3:]
+    (part_ref, hidden, hidden_two, docs_full, ffn_bf, ffn_shard), refs = refs[:6], refs[6:]
+    if aligned:
+        (attn_bf, attn_shard, attn_col, *attn_scratch), refs = refs[:10], refs[10:]
+    scratch = refs
     seq, own_rows, chips = h_ref.shape[0], x_ref.shape[0], columns // 2
-    greet(columns, layers)
-    line = LineGather(ffn_col, ffn_shard, layers, 3, scratch[0:5])
-    dy_gather = Gather(dy_ref, dy_full, chips, scratch[5:10])
+    ffn_rows = ffn_ref.shape[0]
+    if aligned:
+        attn_rows = attn_ref.shape[0]
+
+        @pl.loop(0, attn_rows // CHUNK)
+        def cast_attn(k):
+            attn_bf[chunk_rows(k), :] = attn_ref[chunk_rows(k), :].astype(BF)
+
+        targets = homes.attn_targets()
+        greet(columns, layers, [spot[:2] for spot in targets + homes.attn_owners()])
+        unit = attn_rows // 3
+        attn_spread = Exchange(
+            [attn_bf.at[pl.ds(k * unit, unit), :] for k in range(3)],
+            functools.partial(place_rows, attn_shard, unit),
+            targets,
+            attn_scratch[0:2],
+        )
+    else:
+        greet(columns, layers)
+    documents = Docs(docs_ref, docs_full, columns, scratch[0:3])
+
+    @pl.loop(0, own_rows // CHUNK)
+    def norm(k):
+        residual = x_ref[chunk_rows(k), :].astype(F32)
+        gain = 1.0 + gains_ref[0:1, :]
+        hidden[chunk_rows(k), :] = (residual * rms_scale(residual) * gain).astype(BF)
+
+    h_gather = Gather(hidden, h_ref, chips, scratch[3:8])
+
+    @pl.loop(0, ffn_rows // CHUNK)
+    def cast_ffn(k):
+        ffn_bf[chunk_rows(k), :] = ffn_ref[chunk_rows(k), :].astype(BF)
+
+    unit_ffn = ffn_rows // 3
+    if aligned:
+        attn_spread.arrive()
+        attn_line = LineGather(attn_col, attn_shard, layers, 1, attn_scratch[2:7])
+    ffn_spread = Exchange(
+        [ffn_bf.at[pl.ds(k * unit_ffn, unit_ffn), :] for k in range(3)],
+        functools.partial(place_rows, ffn_shard, unit_ffn),
+        homes.ffn_targets(),
+        scratch[8:10],
+    )
+    documents.finish()
+    place_tables(docs_full, freq_ref, cos_ref, sin_ref, start_ref)
+    if aligned:
+        attn_line.relay(1)
+    h_gather.pass_on()
+    if aligned:
+        attn_line.relay()
+    ffn_spread.arrive()
+    line = LineGather(ffn_col, ffn_shard, layers, 3, scratch[10:15])
+    h_gather.finish()
+    dy_gather = Gather(dy_ref, dy_full, chips, scratch[15:20])
+    if aligned:
+        attn_line.finish()
+        w_ref = attn_col
+    else:
+        w_ref = attn_ref
     scale = HEAD_SIZE**-0.5
     for slot in range(2 * heads + 2):
         pad_ref[slot * LANES : slot * LANES + HEAD_SIZE, :] = w_ref[
@@ -1041,7 +1004,7 @@
         at = pl.ds(pl.multiple_of(i * TILE, TILE), TILE)
         part_ref[at, :] = plain_times(att_ref[at, :], pad_ref[width:, :]).astype(BF)
 
-    reduce = Reduce(part_ref, chips, own_rows, scratch[10:12], scratch[12:16])
+    reduce = Reduce(part_ref, chips, own_rows, scratch[20:22], scratch[22:26])
     line.relay(1)
     reduce.exchange()
     line.relay(1)
@@ -1054,24 +1017,43 @@
         at = chunk_rows(k)
         middle = x_ref[at, :].astype(F32) + reduce.total(k)
         middle_ref[at, :] = middle
-        hidden[at, :] = (middle * rms_scale(middle) * (1.0 + gain_ref[...])).astype(BF)
-
-    gather = Gather(hidden, h2_full, chips, scratch[16:21])
-    line.relay(2)
+        hidden_two[at, :] = (middle * rms_scale(middle) * (1.0 + gains_ref[1:2, :])).astype(BF)
+
+    gather = Gather(hidden_two, h2_full, chips, scratch[26:31])
+    line.relay(1)
     gather.pass_on()
     line.relay()
     gather.finish()
     dy_gather.finish()
     reduce.drain()
     line.finish()
-
-
-def forward_step(h_full, w_col, cosine, sine, starts, x_own, gain_row, dy_own, ffn_shard, heads, columns, layers):
-    seq, width = h_full.shape
-    rows = x_own.shape[0]
+    ffn_spread.drain()
+    if aligned:
+        attn_spread.drain()
+
+
+def forward_step(x_own, gains, docs, dy_own, attn, ffn_weights, attn_total, heads, columns, layers, aligned):
+    rows, width = x_own.shape
+    seq = rows * columns
     chips = columns // 2
+    ffn_rows = ffn_weights.shape[0]
+    place = np.arange(LANES)
+    frequency = np.where(
+        place < HEAD_SIZE, ROPE_THETA ** (-2.0 * (place % (HEAD_SIZE // 2)) / HEAD_SIZE), 0.0
+    ).astype(np.float32)[None, :]
+    attn_scratch = []
+    if aligned:
+        attn_scratch = [
+            pltpu.VMEM(attn.shape, BF),
+            pltpu.VMEM(attn.shape, BF),
+            pltpu.VMEM((layers * attn.shape[0], width), BF),
+            *Exchange.scratch(),
+            *LineGather.scratch(layers, 1),
+        ]
     return pl.pallas_call(
-        functools.partial(forward_kernel, columns, layers, heads),
+        functools.partial(
+            forward_kernel, columns, layers, heads, Homes(layers, columns, attn_total), aligned
+        ),
         out_shape=(
             jax.ShapeDtypeStruct((seq, heads * LANES), BF),
             jax.ShapeDtypeStruct((seq, LANES), BF),
@@ -1080,15 +1062,27 @@
             jax.ShapeDtypeStruct((seq, heads * LANES), F32),
             jax.ShapeDtypeStruct(((2 * heads + 2) * LANES, width), BF),
             jax.ShapeDtypeStruct((rows, width), F32),
+            jax.ShapeDtypeStruct((seq, LANES), F32),
+            jax.ShapeDtypeStruct((seq, LANES), F32),
+            jax.ShapeDtypeStruct((seq, LANES), jnp.int32),
             jax.ShapeDtypeStruct((seq, width), BF),
             jax.ShapeDtypeStruct((seq, width), BF),
-            jax.ShapeDtypeStruct((layers * ffn_shard.shape[0], width), BF),
+            jax.ShapeDtypeStruct((seq, width), BF),
+            jax.ShapeDtypeStruct((layers * ffn_rows, width), BF),
         ),
-        in_specs=vmem_specs(9),
-        out_specs=tuple(vmem_specs(7) + [pl.BlockSpec(memory_space=pl.ANY)] * 3),
+        in_specs=vmem_specs(7),
+        out_specs=tuple(vmem_specs(11) + [pl.BlockSpec(memory_space=pl.ANY)] * 3),
         scratch_shapes=[
             pltpu.VMEM((seq, width), BF),
             pltpu.VMEM((rows, width), BF),
+            pltpu.VMEM((rows, width), BF),
+            pltpu.VMEM((columns, rows), jnp.int32),
+            pltpu.VMEM((ffn_rows, width), BF),
+            pltpu.VMEM((ffn_rows, width), BF),
+            *attn_scratch,
+            *Docs.scratch(columns),
+            *Gather.scratch(chips),
+            *Exchange.scratch(),
             *LineGather.scratch(layers, 3),
             *Gather.scratch(chips),
             *Reduce.buffers(chips, rows, width),
@@ -1097,8 +1091,8 @@
         ],
         compiler_params=comm_params(3),
         name="forward_step",
-        cost_estimate=pl.CostEstimate(flops=6_000_000_000, bytes_accessed=150_000_000, transcendentals=2_000_000),
-    )(h_full, w_col, cosine, sine, starts, x_own, gain_row, dy_own, ffn_shard)
+        cost_estimate=pl.CostEstimate(flops=6_000_000_000, bytes_accessed=250_000_000, transcendentals=2_000_000),
+    )(x_own, gains, docs, jnp.asarray(frequency), dy_own, attn, ffn_weights)
 
 
 class Load:
@@ -1439,18 +1433,6 @@
     return out[:3], out[3:]
 
 
-def rope_tables(positions):
-    half_width = HEAD_SIZE // 2
-    frequency = ROPE_THETA ** (-2.0 * jnp.arange(half_width, dtype=F32) / HEAD_SIZE)
-    angles = positions.astype(F32)[:, None] * frequency[None, :]
-    cosine, sine = jnp.cos(angles), jnp.sin(angles)
-    blank = jnp.zeros((positions.shape[0], LANES - HEAD_SIZE), F32)
-    return (
-        jnp.concatenate([cosine, cosine, blank], axis=1),
-        jnp.concatenate([-sine, sine, blank], axis=1),
-    )
-
-
 def unpadded(rows, count):
     return jnp.concatenate([rows[k * LANES : k * LANES + HEAD_SIZE] for k in range(count)])
 
@@ -1478,47 +1460,37 @@
     swap = [(c, c + 1 - 2 * (c % 2)) for c in range(columns)]
 
     x_own, dy_own = block_input[0], cotangent[0]
-    aligned = attn_weights.shape[0] % (3 * CHUNK) == 0 and layers > 1
-    if aligned:
-        h_full, docs_full, attn_col, ffn_shard = open_step(
-            x_own, norm_gains[0:1], documents, attn_weights, ffn_weights, columns, layers
-        )
-    else:
-        residual = x_own.astype(F32)
-        first_hidden = (residual * rms_scale(residual) * (1.0 + norm_gains[0])).astype(BF)
-        h_full, docs_full = gather_docs(first_hidden, documents, columns)
+    attn_total = attn_weights.shape[0] * layers * columns
+    aligned = attn_weights.shape[0] % (3 * CHUNK) == 0
+    attn_source = attn_weights
+    if not aligned:
         attn_col = lax.all_gather(
             attn_plan.spread(attn_weights.astype(BF)), "fsdp", axis=0, tiled=True
         )
-        ffn_shard = ffn_plan.spread(ffn_weights.astype(BF))
-    query_rows = heads * HEAD_SIZE
-    if sharers > 1:
-        own_part = attn_col[query_rows : query_rows + 2 * share]
-        other = lax.ppermute(own_part, "context", swap)
-
-        def whole_head(first):
-            mine, theirs = own_part[first : first + share], other[first : first + share]
-            return jnp.where(
-                core == 0, jnp.concatenate([mine, theirs]), jnp.concatenate([theirs, mine])
+        if sharers > 1:
+            query_rows = heads * HEAD_SIZE
+            own_part = attn_col[query_rows : query_rows + 2 * share]
+            other = lax.ppermute(own_part, "context", swap)
+
+            def whole_head(first):
+                mine, theirs = own_part[first : first + share], other[first : first + share]
+                return jnp.where(
+                    core == 0, jnp.concatenate([mine, theirs]), jnp.concatenate([theirs, mine])
+                )
+
+            attn_col = jnp.concatenate(
+                [
+                    attn_col[:query_rows],
+                    whole_head(0),
+                    whole_head(share),
+                    attn_col[query_rows + 2 * share :],
+                ]
             )
-
-        attn_col = jnp.concatenate(
-            [
-                attn_col[:query_rows],
-                whole_head(0),
-                whole_head(share),
-                attn_col[query_rows + 2 * share :],
-            ]
-        )
-
-    all_docs = docs_full.reshape(seq)
-    starts = jnp.sum((all_docs[None, :] < all_docs[:, None]).astype(jnp.int32), axis=1)
-    cosine, sine = rope_tables(jnp.arange(seq, dtype=jnp.int32) - starts)
-    start_lanes = jnp.broadcast_to(starts[:, None], (seq, LANES))
-    tables = (cosine, sine, start_lanes)
-    *saved, padded, middle, h2_full, dy_full, ffn_col = forward_step(
-        h_full, attn_col, *tables, x_own, norm_gains[1:2], dy_own, ffn_shard, heads, columns, layers
+        attn_source = attn_col
+    *saved, padded, middle, cosine, sine, starts, h_full, h2_full, dy_full, ffn_col = forward_step(
+        x_own, norm_gains, documents, dy_own, attn_source, ffn_weights, attn_total, heads, columns, layers, aligned
     )
+    tables = (cosine, sine, starts)
 
     block_out, grad_middle, sums, ffn_sum, attn_term, in_part = backward_step(
         h2_full,

time: 317 us -> 306 us (0.965)
  other arithmetic: 6.45 us -> 1.24 us
  Pallas kernels: 302 us -> 298 us
    pallas_call x2 -> x1, Pallas kernels: 137 us -> 132 us  [forward_step(): pl.pallas_call(functools.partial(forward_kernel, columns, layers, heads,...]
where the time goes in v5:
time: 306 us; the launch traced here: 305 us
  Pallas kernels  298 us (97%)
  local copies, waits for them, and re-layouts  5.55 us (2%)
    pallas_call x1, Pallas kernels, forward_step(): pl.pallas_call(functools.partial(forward_kernel, columns, layers, heads,...  132 us
    pallas_call x1, Pallas kernels, backward_step(): pl.pallas_call(functools.partial(backward_kernel, columns, layers, heads,...  96.8 us
    pallas_call x1, Pallas kernels, last_step(): pl.pallas_call(functools.partial(last_kernel, columns, layers, homes), ou...  54.8 us
    pallas_call x1, Pallas kernels, update_all(): pl.pallas_call(functools.partial(update_kernel, steps), grid=(steps + res...  13.8 us

profile of v5, /device:TPU:0, one launch (start us, length us, event | category | flops | bytes accessed | tf_op | source)
XLA Modules:
  0.0 305.2 jit_solution(16790773422027171365)
XLA Ops:
  0.6 0.0 copy-start
  0.7 132.2 %forward_step.1 = (bf16[1024,256]{1,0:T(8,128)(2,1)}, bf16[1024,128]{1,0:T(8,128)(2,1)}, bf16[1024,128]{1,0:T(8,128)(2,1)}, bf16[1024,256]{1,0:T(8,128)(2,1)}, f...) custom-call(bf16[128,1536]{1,0:T(8,128)(2,1)} %bitcast.18, ...), custom_call_target="tpu_custom_call" | custom-call | flops 6000000000 | bytes 250000000 | tf_op jit(solution)/shard_map/forward_step/pallas_call | solution.py:1053
  132.9 0.0 copy-done
  132.9 0.6 fusion.1
  133.5 96.8 %backward_step.1 = (f32[128,1536]{1,0:T(8,128)}, f32[128,1536]{1,0:T(8,128)}, f32[8,1536]{1,0:T(8,128)}, bf16[384,1536]{1,0:T(8,128)(2,1)}, bf16[576,1536]{1,0:T(8,128)(2,1)}, /*index=5*/bf16[1024,1536]{1,0:T(8,128)(2,1)}) custom-call(bf16[1024,1536]{1,0:T(8,128)(2,1)} %get-tuple-element.41.refs_0_, bf16[1024,1536]{1,0:T(8,128)(2,1)} %get-tuple-element.42.refs_1_, ...), custom_call_target="tpu_custom_call" | custom-call | flops 28000000000 | bytes 150000000 | tf_op jit(solution)/shard_map/backward_step/pallas_call | solution.py:1332
  230.4 0.0 copy-start.1
  230.4 54.8 %last_step.1 = (f32[128,1536]{1,0:T(8,128)}, f32[8,1536]{1,0:T(8,128)}, bf16[144,1536]{1,0:T(8,128)(2,1)}, bf16[384,1536]{1,0:T(8,128)(2,1)}) custom-call(bf16[1024,1536]{1,0:T(8,128)(2,1)} %get-tuple-element.56.refs_0_, bf16[128,1536]{1,0:T(8,128)(2,1)} %bitcast.19, f32[128,1536]{1,0:T(8,128)} %get-tuple-element.57.refs_2_, ...), custom_call_target="tpu_custom_call" | custom-call | bytes 150000000 | tf_op jit(solution)/shard_map/last_step/pallas_call | solution.py:828
  285.2 0.8 slice.17
  286.0 0.0 copy-done.1
  286.0 0.7 multiply_subtract_fusion
  286.6 0.6 pad_maximum_fusion
  287.2 13.8 %update_all.1 = (f32[384,1536]{1,0:T(8,128)}, f32[384,1536]{1,0:T(8,128)}, f32[2,384,1536]{2,1,0:T(8,128)}, f32[144,1536]{1,0:T(8,128)}, f32[144,1536]{1,0:T(8,128)}, /*index=5*/f32[2,144,1536]{2,1,0:T(8,128)}) custom-call(bf16[384,1536]{1,0:T(8,128)(2,1)} %get-tuple-element.62.refs_0_, f32[384,1536]{1,0:T(8,128)} %refs_1_.3, f32[2,384,1536]{2,1,0:T(8,128)} %refs_2_.3, ...), custom_call_target="tpu_custom_call" | custom-call | flops 20000000 | bytes 25000000 | tf_op jit(solution)/shard_map/update_all/pallas_call | solution.py:1423
  301.0 2.1 copy.23
  303.1 2.1 copy.24
Async XLA Ops:
  0.6 132.3 %copy-start = (f32[2,1536]{1,0:T(2,128)S(1)}, f32[2,1536]{1,0:T(2,128)}, u32[]{:S(2)}) copy-start(f32[2,1536]{1,0:T(2,128)} %refs_1_.2) | copy-start | bytes 36868
  230.4 55.6 %copy-start.1 = (f32[2,2,48]{2,1,0:T(2,128)S(1)}, f32[2,2,48]{2,1,0:T(2,128)}, u32[]{:S(2)}) copy-start(f32[2,2,48]{2,1,0:T(2,128)} %param.18) | copy-start | bytes 2308

commit v6 on v5

--- a/solution.py
+++ b/solution.py
@@ -594,7 +594,7 @@
 class Reduce:
     @staticmethod
     def buffers(chips, rows, width):
-        return [pltpu.VMEM((chips, rows, width), BF), pltpu.VMEM((chips - 1, rows, width), BF)]
+        return [pltpu.VMEM((chips * rows, width), BF), pltpu.VMEM(((chips - 1) * rows, width), BF)]
 
     @staticmethod
     def semaphores(chips):
@@ -610,7 +610,7 @@
             block = partner(sibling_of(me), step, chips)
             self.near_copies[step] = send(
                 part.at[rows_at(block, rows), :],
-                self.near.at[step],
+                self.near.at[pl.ds(step * rows, rows), :],
                 near_send.at[step],
                 near_recv.at[step],
                 {"context": sibling_of(me)},
@@ -625,16 +625,16 @@
 
             @pl.loop(0, self.rows // CHUNK)
             def add(k):
-                at = chunk_rows(k)
+                at = chunk_rows(step * (self.rows // CHUNK) + k)
                 from_part = pl.ds(pl.multiple_of(first + k * CHUNK, CHUNK), CHUNK)
-                self.near[step, at, :] = (
-                    self.part[from_part, :].astype(F32) + self.near[step, at, :].astype(F32)
+                self.near[at, :] = (
+                    self.part[from_part, :].astype(F32) + self.near[at, :].astype(F32)
                 ).astype(BF)
 
             self.far_copies.append(
                 send(
-                    self.near.at[step],
-                    self.far.at[step - 1],
+                    self.near.at[pl.ds(step * self.rows, self.rows), :],
+                    self.far.at[pl.ds((step - 1) * self.rows, self.rows), :],
                     self.far_send.at[step],
                     self.far_recv.at[step],
                     {"context": target},
@@ -650,9 +650,10 @@
         at = chunk_rows(k)
         first = pl.multiple_of(self.me * self.rows, self.rows)
         value = self.part[pl.ds(pl.multiple_of(first + k * CHUNK, CHUNK), CHUNK), :].astype(F32)
-        value = value + self.near[0, at, :].astype(F32)
+        value = value + self.near[at, :].astype(F32)
         for step in range(1, self.chips):
-            value = value + self.far[step - 1, at, :].astype(F32)
+            there = chunk_rows((step - 1) * (self.rows // CHUNK) + k)
+            value = value + self.far[there, :].astype(F32)
         return value
 
     def drain(self):
@@ -706,135 +707,10 @@
         self.local.wait()
 
 
-def last_kernel(columns, layers, homes, *refs):
-    (part_in, x_ref, grad_ref, gain_ref, sums_ref), refs = refs[:5], refs[5:]
-    if homes is not None:
-        (term, ffn_sum), refs = refs[:2], refs[2:]
-    (input_grad_ref, gains_ref), refs = refs[:2], refs[2:]
-    if homes is not None:
-        (attn_back, ffn_back), refs = refs[:2], refs[2:]
-    (own_sums, plane_slots, plane_sums, line_slots), refs = refs[:4], refs[4:]
-    (plane_send, plane_recv, line_send, line_recv), scratch = refs[:4], refs[4:]
-    chips = columns // 2
-    rows = x_ref.shape[0]
-    if homes is None:
-        greet(columns, layers)
-    else:
-        attn_owners = homes.attn_owners()
-        greet(columns, layers, [spot[:2] for spot in homes.attn_targets() + attn_owners])
-    first = Reduce(part_in, chips, rows, scratch[0:2], scratch[2:6])
-    if homes is not None:
-        attn_rows, ffn_rows = term.shape[0] // layers, ffn_sum.shape[0]
-        attn_done = scratch[6]
-        line = LineReduce(term, layers, 3, scratch[7:13])
-        unit_ffn = ffn_rows // 3
-    first.exchange()
-    if homes is not None:
-        ffn_owned = Exchange(
-            [ffn_sum.at[pl.ds(k * unit_ffn, unit_ffn), :] for k in range(3)],
-            functools.partial(place_rows, ffn_back, unit_ffn),
-            homes.ffn_owners(),
-            scratch[13:15],
-        )
-        line.relay(3)
-    own_sums[...] = jnp.zeros_like(own_sums)
-    own_sums[1:2, :] = sums_ref[0:1, :]
-    if homes is not None:
-        line.relay(3)
-    first.arrive()
-
-    @pl.loop(0, rows // CHUNK)
-    def finish(k):
-        at = chunk_rows(k)
-        grad_hidden = first.total(k)
-        residual = x_ref[at, :].astype(F32)
-        scale = rms_scale(residual)
-        normed = residual * scale
-        own_sums[0:1, :] += jnp.sum(grad_hidden * normed, axis=0, keepdims=True)
-        input_grad_ref[at, :] = grad_ref[at, :] + norm_backward(
-            grad_hidden, normed, scale, gain_ref[...]
-        )
-
-    me = lax.axis_index("context")
-    layer = lax.axis_index("fsdp")
-    in_plane = [
-        send(
-            own_sums,
-            plane_slots.at[step],
-            plane_send.at[step],
-            plane_recv.at[step],
-            {"context": lax.rem(me + step, columns)},
-        )
-        for step in range(1, columns)
-    ]
-    if homes is not None:
-        line.finish(attn_done)
-        unit = attn_rows // 3
-        attn_owned = Exchange(
-            [attn_done.at[pl.ds(k * unit, unit), :] for k in range(3)],
-            functools.partial(place_rows, attn_back, unit),
-            attn_owners,
-            scratch[15:17],
-        )
-    total = own_sums[...]
-    for step, copy in enumerate(in_plane):
-        copy.wait_recv()
-        total = total + plane_slots[step + 1]
-    plane_sums[...] = total
-    in_line = [
-        send(
-            plane_sums,
-            line_slots.at[step],
-            line_send.at[step],
-            line_recv.at[step],
-            {"fsdp": lax.rem(layer + step, layers)},
-        )
-        for step in range(1, layers)
-    ]
-    for step, copy in enumerate(in_line):
-        copy.wait_recv()
-        total = total + line_slots[step + 1]
-    gains_ref[...] = total
-    if homes is not None:
-        ffn_owned.arrive()
-        attn_owned.arrive()
-        ffn_owned.drain()
-        attn_owned.drain()
-        line.drain()
-    for copy in in_plane + in_line:
-        copy.wait_send()
-    first.drain()
-
-
-def last_step(part_in, x_own, grad_middle, gain_row, sums, columns, layers, weight_sums=()):
-    rows, width = x_own.shape
-    chips = columns // 2
-    homes = None
-    back_shapes, back_scratch = [], []
-    if weight_sums:
-        term, ffn_sum = weight_sums
-        attn_rows = term.shape[0] // layers
-        homes = Homes(layers, columns, attn_rows * layers * columns)
-        back_shapes = [
-            jax.ShapeDtypeStruct((attn_rows, width), BF),
-            jax.ShapeDtypeStruct(ffn_sum.shape, BF),
-        ]
-        back_scratch = [
-            pltpu.VMEM((attn_rows, width), BF),
-            *LineReduce.scratch(layers, 3, attn_rows, width),
-            *Exchange.scratch(),
-            *Exchange.scratch(),
-        ]
-    return pl.pallas_call(
-        functools.partial(last_kernel, columns, layers, homes),
-        out_shape=(
-            jax.ShapeDtypeStruct((rows, width), F32),
-            jax.ShapeDtypeStruct((8, width), F32),
-            *back_shapes,
-        ),
-        in_specs=vmem_specs(5 + len(weight_sums)),
-        out_specs=tuple(vmem_specs(2) + [pl.BlockSpec(memory_space=pl.ANY)] * len(back_shapes)),
-        scratch_shapes=[
+class GainSums:
+    @staticmethod
+    def scratch(columns, layers, width):
+        return [
             pltpu.VMEM((8, width), F32),
             pltpu.VMEM((columns, 8, width), F32),
             pltpu.VMEM((8, width), F32),
@@ -843,14 +719,103 @@
             pltpu.SemaphoreType.DMA((columns,)),
             pltpu.SemaphoreType.DMA((layers,)),
             pltpu.SemaphoreType.DMA((layers,)),
+        ]
+
+    def __init__(self, columns, layers, scratch):
+        self.columns, self.layers = columns, layers
+        self.own, self.plane_slots, self.plane, self.line_slots, *self.sems = scratch
+        self.own[...] = jnp.zeros_like(self.own)
+
+    def start(self):
+        me = lax.axis_index("context")
+        plane_send, plane_recv, _, _ = self.sems
+        self.in_plane = [
+            send(
+                self.own,
+                self.plane_slots.at[step],
+                plane_send.at[step],
+                plane_recv.at[step],
+                {"context": lax.rem(me + step, self.columns)},
+            )
+            for step in range(1, self.columns)
+        ]
+
+    def along(self):
+        layer = lax.axis_index("fsdp")
+        _, _, line_send, line_recv = self.sems
+        total = self.own[...]
+        for step, copy in enumerate(self.in_plane):
+            copy.wait_recv()
+            total = total + self.plane_slots[step + 1]
+        self.plane[...] = total
+        self.in_line = [
+            send(
+                self.plane,
+                self.line_slots.at[step],
+                line_send.at[step],
+                line_recv.at[step],
+                {"fsdp": lax.rem(layer + step, self.layers)},
+            )
+            for step in range(1, self.layers)
+        ]
+
+    def finish(self, result):
+        total = self.plane[...]
+        for step, copy in enumerate(self.in_line):
+            copy.wait_recv()
+            total = total + self.line_slots[step + 1]
+        result[...] = total
+        for copy in self.in_plane + self.in_line:
+            copy.wait_send()
+
+
+def input_gradient(reduce, gains, x_ref, grad_ref, gain_row, result):
+    @pl.loop(0, x_ref.shape[0] // CHUNK)
+    def finish(k):
+        at = chunk_rows(k)
+        grad_hidden = reduce.total(k)
+        residual = x_ref[at, :].astype(F32)
+        scale = rms_scale(residual)
+        normed = residual * scale
+        gains.own[0:1, :] += jnp.sum(grad_hidden * normed, axis=0, keepdims=True)
+        result[at, :] = grad_ref[at, :] + norm_backward(grad_hidden, normed, scale, gain_row)
+
+
+def last_kernel(columns, layers, part_in, x_ref, grad_ref, gain_ref, sums_ref, input_grad_ref, gains_ref, *scratch):
+    rows, chips = x_ref.shape[0], columns // 2
+    greet(columns, layers)
+    reduce = Reduce(part_in, chips, rows, scratch[0:2], scratch[2:6])
+    gains = GainSums(columns, layers, scratch[6:])
+    gains.own[1:2, :] = sums_ref[0:1, :]
+    reduce.exchange()
+    reduce.arrive()
+    input_gradient(reduce, gains, x_ref, grad_ref, gain_ref[...], input_grad_ref)
+    gains.start()
+    gains.along()
+    gains.finish(gains_ref)
+    reduce.drain()
+
+
+def last_step(part_in, x_own, grad_middle, gain_row, sums, columns, layers):
+    rows, width = x_own.shape
+    chips = columns // 2
+    return pl.pallas_call(
+        functools.partial(last_kernel, columns, layers),
+        out_shape=(
+            jax.ShapeDtypeStruct((rows, width), F32),
+            jax.ShapeDtypeStruct((8, width), F32),
+        ),
+        in_specs=vmem_specs(5),
+        out_specs=tuple(vmem_specs(2)),
+        scratch_shapes=[
             *Reduce.buffers(chips, rows, width),
             *Reduce.semaphores(chips),
-            *back_scratch,
+            *GainSums.scratch(columns, layers, width),
         ],
         compiler_params=comm_params(5),
         name="last_step",
         cost_estimate=pl.CostEstimate(flops=0, bytes_accessed=150_000_000, transcendentals=0),
-    )(part_in, x_own, grad_middle, gain_row, sums, *weight_sums)
+    )(part_in, x_own, grad_middle, gain_row, sums)
 
 
 def turned(heads, low):
@@ -1117,11 +1082,16 @@
     return most, width // most
 
 
-def backward_kernel(columns, layers, heads, sharers, factor, *refs):
+def backward_kernel(columns, layers, heads, sharers, factor, homes, *refs):
     (h2_hbm, dy_hbm, w_hbm, h_hbm, pad_hbm), refs = refs[:5], refs[5:]
     (cos_hbm, sin_hbm, start_hbm, q_hbm, k_hbm, v_hbm, att_hbm, log_hbm), refs = refs[:8], refs[8:]
-    (middle_ref, dy_ref, gain_ref), refs = refs[:3], refs[3:]
-    (block_out_ref, grad_ref, sums_ref, ffn_sum, term_in, in_part), refs = refs[:6], refs[6:]
+    (middle_ref, dy_ref, gains_in, x_own), refs = refs[:4], refs[4:]
+    if homes is None:
+        (block_out_ref, grad_ref, sums_ref, ffn_sum, term_in, in_part), refs = refs[:6], refs[6:]
+    else:
+        (block_out_ref, input_grad_ref, gains_ref, attn_back, ffn_back), refs = refs[:5], refs[5:]
+        (grad_ref, sums_ref, ffn_sum, term_in, attn_done), refs = refs[:5], refs[5:]
+        last, refs = refs[:20], refs[20:]
     (x_ref, y_ref, w_ref, pad_ref, cos_ref, sin_ref, start_ref), refs = refs[:7], refs[7:]
     (q_ref, k_ref, v_ref, att_ref, log_ref), refs = refs[:5], refs[5:]
     (act_ref, gg_ref, gu_ref, act_t, gg_t, gu_t, term, part_ref), refs = refs[:8], refs[8:]
@@ -1151,7 +1121,11 @@
             )
         )
     ]
-    greet(columns, layers)
+    if homes is None:
+        greet(columns, layers)
+    else:
+        attn_owners = homes.attn_owners()
+        greet(columns, layers, [spot[:2] for spot in homes.attn_targets() + attn_owners])
     w_gate, w_up, w_down = (pl.ds(k * hidden, hidden) for k in range(3))
 
     w_load.wait()
@@ -1210,7 +1184,7 @@
         scale = rms_scale(middle)
         normed = middle * scale
         sums_ref[0:1, :] += jnp.sum(grad_hidden * normed, axis=0, keepdims=True)
-        grad = dy_ref[at, :].astype(F32) + norm_backward(grad_hidden, normed, scale, gain_ref[...])
+        grad = dy_ref[at, :].astype(F32) + norm_backward(grad_hidden, normed, scale, gains_in[1:2, :])
         grad_ref[at, :] = grad
         grad_bf[at, :] = grad.astype(BF)
 
@@ -1288,8 +1262,13 @@
         at = pl.ds(pl.multiple_of(i * TILE, TILE), TILE)
         part_ref[at, :] = plain_times(out_ref[at, :], pad_ref[0:width, :]).astype(BF)
 
-    store = pltpu.make_async_copy(part_ref, in_part, store_sem)
-    store.start()
+    if homes is None:
+        store = pltpu.make_async_copy(part_ref, in_part, store_sem)
+        store.start()
+    else:
+        near_rows = chips * own_rows
+        room = (w_ref.at[pl.ds(0, near_rows), :], w_ref.at[pl.ds(near_rows, near_rows - own_rows), :])
+        first = Reduce(part_ref, chips, own_rows, room, last[0:4])
     h_load.wait()
 
     @pl.loop(0, blocks)
@@ -1306,6 +1285,9 @@
                         k * LANES : k * LANES + HEAD_SIZE, :
                     ]
 
+    if homes is not None:
+        attn_line = LineReduce(term_in, layers, 3, last[4:10])
+        first.exchange()
     out.arrive()
 
     @pl.loop(0, own_rows // CHUNK)
@@ -1314,13 +1296,44 @@
         block_out_ref[at, :] = middle_ref[at, :] + out.total(k)
 
     line.finish(ffn_sum)
-    store.wait()
+    if homes is None:
+        store.wait()
+    else:
+        unit_ffn, unit = ffn_sum.shape[0] // 3, attn_done.shape[0] // 3
+        ffn_owned = Exchange(
+            [ffn_sum.at[pl.ds(k * unit_ffn, unit_ffn), :] for k in range(3)],
+            functools.partial(place_rows, ffn_back, unit_ffn),
+            homes.ffn_owners(),
+            last[10:12],
+        )
+        gains = GainSums(columns, layers, last[12:20])
+        gains.own[1:2, :] = sums_ref[0:1, :]
+        attn_line.relay(3)
+        first.arrive()
+        input_gradient(first, gains, x_own, grad_ref, gains_in[0:1, :], input_grad_ref)
+        gains.start()
+        attn_line.relay(4)
+        gains.along()
+        attn_line.finish(attn_done)
+        attn_owned = Exchange(
+            [attn_done.at[pl.ds(k * unit, unit), :] for k in range(3)],
+            functools.partial(place_rows, attn_back, unit),
+            attn_owners,
+            scratch[21:23],
+        )
+        gains.finish(gains_ref)
+        ffn_owned.arrive()
+        attn_owned.arrive()
+        ffn_owned.drain()
+        attn_owned.drain()
+        attn_line.drain()
+        first.drain()
     line.drain()
     out.drain()
 
 
 def backward_step(
-    h2_full, dy_full, ffn_col, h_full, padded, tables, saved, middle, dy_own, gain_row, heads, columns, layers, sharers
+    h2_full, dy_full, ffn_col, h_full, padded, tables, saved, middle, dy_own, gains, x_own, heads, columns, layers, sharers, joined
 ):
     seq, width = h2_full.shape
     rows = seq // columns
@@ -1328,22 +1341,53 @@
     hidden = ffn_col.shape[0] // 3
     ffn_rows = ffn_col.shape[0] // layers
     each = HEAD_SIZE if sharers == 1 else LANES
+    term_rows = (2 * heads + 2) * each
+    attn_rows = term_rows // layers
     loaded = [ffn_col, padded, *tables, *saved]
+    own = jax.ShapeDtypeStruct((rows, width), F32)
+    eight = jax.ShapeDtypeStruct((8, width), F32)
+    anywhere = pl.BlockSpec(memory_space=pl.ANY)
+    homes, last = None, []
+    if joined:
+        homes = Homes(layers, columns, attn_rows * layers * columns)
+        shapes = (
+            own,
+            own,
+            eight,
+            jax.ShapeDtypeStruct((attn_rows, width), BF),
+            jax.ShapeDtypeStruct((ffn_rows, width), BF),
+        )
+        specs = (*vmem_specs(3), anywhere, anywhere)
+        last = [
+            pltpu.VMEM((rows, width), F32),
+            pltpu.VMEM((8, width), F32),
+            pltpu.VMEM((ffn_rows, width), BF),
+            pltpu.VMEM((term_rows, width), BF),
+            pltpu.VMEM((attn_rows, width), BF),
+            *Reduce.semaphores(chips),
+            *LineReduce.scratch(layers, 3, attn_rows, width),
+            *Exchange.scratch(),
+            *GainSums.scratch(columns, layers, width),
+        ]
+    else:
+        shapes = (
+            own,
+            own,
+            eight,
+            jax.ShapeDtypeStruct((ffn_rows, width), BF),
+            jax.ShapeDtypeStruct((term_rows, width), BF),
+            jax.ShapeDtypeStruct((seq, width), BF),
+        )
+        specs = (*vmem_specs(5), anywhere)
     return pl.pallas_call(
         functools.partial(
-            backward_kernel, columns, layers, heads, sharers, float(seq * layers) ** (-0.5)
+            backward_kernel, columns, layers, heads, sharers, float(seq * layers) ** (-0.5), homes
         ),
-        out_shape=(
-            jax.ShapeDtypeStruct((rows, width), F32),
-            jax.ShapeDtypeStruct((rows, width), F32),
-            jax.ShapeDtypeStruct((8, width), F32),
-            jax.ShapeDtypeStruct((ffn_rows, width), BF),
-            jax.ShapeDtypeStruct(((2 * heads + 2) * each, width), BF),
-            jax.ShapeDtypeStruct((seq, width), BF),
-        ),
-        in_specs=[pl.BlockSpec(memory_space=pl.ANY)] * 13 + vmem_specs(3),
-        out_specs=tuple(vmem_specs(5) + [pl.BlockSpec(memory_space=pl.ANY)]),
+        out_shape=shapes,
+        in_specs=[anywhere] * 13 + vmem_specs(3) + (vmem_specs(1) if joined else [anywhere]),
+        out_specs=specs,
         scratch_shapes=[
+            *last,
             pltpu.VMEM((seq, width), BF),
             pltpu.VMEM((seq, width), BF),
             *[pltpu.VMEM(array.shape, array.dtype) for array in loaded],
@@ -1366,71 +1410,118 @@
             *Reduce.semaphores(chips),
             *Gather.scratch(chips),
             *Reduce.semaphores(chips),
+            *Exchange.scratch(),
         ],
         compiler_params=comm_params(4),
         name="backward_step",
-        cost_estimate=pl.CostEstimate(flops=28_000_000_000, bytes_accessed=150_000_000, transcendentals=4_000_000),
-    )(h2_full, dy_full, ffn_col, h_full, padded, *tables, *saved, middle, dy_own, gain_row)
-
-
-def update_rows(g_ref, p_ref, m_ref, grad_ref, new_p_ref, new_m_ref):
-    gradient = g_ref[...].astype(F32)
-    grad_ref[...] = gradient
-    parameter = p_ref[...]
-    first_moment = BETA_ONE * m_ref[0] + (1.0 - BETA_ONE) * gradient
-    second_moment = BETA_TWO * m_ref[1] + (1.0 - BETA_TWO) * gradient * gradient
-    new_m_ref[0] = first_moment
-    new_m_ref[1] = second_moment
-    below = jnp.sqrt(second_moment * (1.0 / (1.0 - BETA_TWO**STEP))) + ADAM_EPS
-    step = first_moment * (LEARN_RATE / (1.0 - BETA_ONE**STEP)) / below
-    new_p_ref[...] = parameter * (1.0 - LEARN_RATE * WEIGHT_DECAY) - step
-
-
-def update_kernel(steps, *refs):
-    first = pl.program_id(0) < steps
-
-    @pl.when(first)
-    def one():
-        update_rows(*refs[0:3], *refs[6:9])
-
-    @pl.when(jnp.logical_not(first))
-    def other():
-        update_rows(*refs[3:6], *refs[9:12])
-
-
-def update_all(first, second):
-    specs, shapes = [], []
-    blocks = []
-    for gradient, parameter, _ in (first, second):
+        cost_estimate=pl.CostEstimate(flops=28_000_000_000, bytes_accessed=250_000_000, transcendentals=4_000_000),
+    )(h2_full, dy_full, ffn_col, h_full, padded, *tables, *saved, middle, dy_own, gains, x_own)
+
+
+def update_kernel(counts, *refs):
+    sources, targets, held = refs[:8], refs[8:16], refs[16:26]
+    in_sems, out_sems, pass_in, pass_out = refs[26:]
+    pieces, leaving = [], []
+    for k in range(2):
+        size = sources[3 * k].shape[0] // counts[k]
+        for n in range(counts[k]):
+            pieces.append((k, pl.ds(n * size, size), size))
+
+    def ends(k, at):
+        g, p, m = sources[3 * k : 3 * k + 3]
+        g_held, p_held, m_held, grad_held = held[4 * k : 4 * k + 4]
+        grad_out, p_out, m_out = targets[3 * k : 3 * k + 3]
+        incoming = (
+            (g.at[at, :], g_held.at[at, :]),
+            (p.at[at, :], p_held.at[at, :]),
+            (m.at[:, at, :], m_held.at[:, at, :]),
+        )
+        outgoing = (
+            (grad_held.at[at, :], grad_out.at[at, :]),
+            (p_held.at[at, :], p_out.at[at, :]),
+            (m_held.at[:, at, :], m_out.at[:, at, :]),
+        )
+        return incoming, outgoing
+
+    arriving = []
+    for n, (k, at, _) in enumerate(pieces):
+        copies = [
+            pltpu.make_async_copy(source, target, in_sems.at[n, j])
+            for j, (source, target) in enumerate(ends(k, at)[0])
+        ]
+        for copy in copies:
+            copy.start()
+        arriving.append(copies)
+    passing = [
+        pltpu.make_async_copy(sources[6 + k], held[8 + k], pass_in.at[k]) for k in range(2)
+    ]
+    for copy in passing:
+        copy.start()
+    for n, (k, at, size) in enumerate(pieces):
+        for copy in arriving[n]:
+            copy.wait()
+        g_held, p_held, m_held, grad_held = held[4 * k : 4 * k + 4]
+        part = CHUNK if size % CHUNK == 0 else size
+
+        @pl.loop(0, size // part)
+        def rows(c):
+            here = pl.ds(pl.multiple_of(at.start + c * part, part), part)
+            gradient = g_held[here, :].astype(F32)
+            grad_held[here, :] = gradient
+            parameter = p_held[here, :]
+            first_moment = BETA_ONE * m_held[0, here, :] + (1.0 - BETA_ONE) * gradient
+            second_moment = BETA_TWO * m_held[1, here, :] + (1.0 - BETA_TWO) * gradient * gradient
+            m_held[0, here, :] = first_moment
+            m_held[1, here, :] = second_moment
+            below = jnp.sqrt(second_moment * (1.0 / (1.0 - BETA_TWO**STEP))) + ADAM_EPS
+            step = first_moment * (LEARN_RATE / (1.0 - BETA_ONE**STEP)) / below
+            p_held[here, :] = parameter * (1.0 - LEARN_RATE * WEIGHT_DECAY) - step
+
+        for j, (source, target) in enumerate(ends(k, at)[1]):
+            copy = pltpu.make_async_copy(source, target, out_sems.at[n, j])
+            copy.start()
+            leaving.append(copy)
+    for k in range(2):
+        passing[k].wait()
+        copy = pltpu.make_async_copy(held[8 + k], targets[6 + k], pass_out.at[k])
+        copy.start()
+        leaving.append(copy)
+    for copy in leaving:
+        copy.wait()
+
+
+def update_all(first, second, passed):
+    shapes, held, counts = [], [], []
+    for gradient, parameter, moments in (first, second):
         rows = parameter.shape[0]
-        whole = [n for n in (48, 32) if rows % n == 0]
-        blocks.append(whole[0] if whole else rows)
-    steps = first[1].shape[0] // blocks[0]
-    rest = second[1].shape[0] // blocks[1]
-    for block, place, (_, parameter, _) in (
-        (blocks[0], lambda i: jnp.minimum(i, steps - 1), first),
-        (blocks[1], lambda i: jnp.maximum(i - steps, 0), second),
-    ):
-        rows, width = parameter.shape
-        flat = pl.BlockSpec((block, width), lambda i, place=place: (place(i), 0))
-        pair = pl.BlockSpec((2, block, width), lambda i, place=place: (0, place(i), 0))
-        specs.append([flat, flat, pair])
-        shapes += [
-            jax.ShapeDtypeStruct((rows, width), F32),
-            jax.ShapeDtypeStruct((rows, width), F32),
-            jax.ShapeDtypeStruct((2, rows, width), F32),
+        counts.append(rows // 48 if rows % 48 == 0 else 1)
+        flat = jax.ShapeDtypeStruct(parameter.shape, F32)
+        shapes += [flat, flat, jax.ShapeDtypeStruct(moments.shape, F32)]
+        held += [
+            pltpu.VMEM(gradient.shape, BF),
+            pltpu.VMEM(parameter.shape, F32),
+            pltpu.VMEM(moments.shape, F32),
+            pltpu.VMEM(parameter.shape, F32),
         ]
+    shapes += [jax.ShapeDtypeStruct(array.shape, array.dtype) for array in passed]
+    held += [pltpu.VMEM(array.shape, array.dtype) for array in passed]
     out = pl.pallas_call(
-        functools.partial(update_kernel, steps),
-        grid=(steps + rest,),
+        functools.partial(update_kernel, counts),
         out_shape=tuple(shapes),
-        in_specs=specs[0] + specs[1],
-        out_specs=tuple(specs[0] + specs[1]),
+        in_specs=[pl.BlockSpec(memory_space=pl.ANY)] * 8,
+        out_specs=tuple([pl.BlockSpec(memory_space=pl.ANY)] * 8),
+        scratch_shapes=[
+            *held,
+            pltpu.SemaphoreType.DMA((sum(counts), 3)),
+            pltpu.SemaphoreType.DMA((sum(counts), 3)),
+            pltpu.SemaphoreType.DMA((2,)),
+            pltpu.SemaphoreType.DMA((2,)),
+        ],
         compiler_params=pltpu.CompilerParams(vmem_limit_bytes=VMEM_LIMIT),
         name="update_all",
         cost_estimate=pl.CostEstimate(flops=20_000_000, bytes_accessed=25_000_000, transcendentals=1_000_000),
-    )(*first, *second)
-    return out[:3], out[3:]
+    )(*first, *second, *passed)
+    return out[:3], out[3:6], out[6:]
 
 
 def unpadded(rows, count):
@@ -1492,7 +1583,7 @@
     )
     tables = (cosine, sine, starts)
 
-    block_out, grad_middle, sums, ffn_sum, attn_term, in_part = backward_step(
+    sums_of = backward_step(
         h2_full,
         dy_full,
         ffn_col,
@@ -1502,30 +1593,34 @@
         saved,
         middle,
         dy_own,
-        norm_gains[1:2],
+        norm_gains,
+        x_own,
         heads,
         columns,
         layers,
         sharers,
+        aligned,
     )
-    if sharers > 1:
-        own_rows = [
-            lax.dynamic_slice_in_dim(attn_term, (heads + k) * LANES + core * share, share, 0)
-            for k in range(2)
-        ]
-        attn_term = jnp.concatenate(
-            [
-                unpadded(attn_term, heads),
-                *own_rows,
-                unpadded(attn_term[(heads + 2) * LANES :], heads),
+    if aligned:
+        block_out, grad_input, gain_sums, attn_shard, ffn_shard = sums_of
+    else:
+        block_out, grad_middle, sums, ffn_sum, attn_term, in_part = sums_of
+        if sharers > 1:
+            own_rows = [
+                lax.dynamic_slice_in_dim(attn_term, (heads + k) * LANES + core * share, share, 0)
+                for k in range(2)
             ]
-        )
-    last_args = (in_part, x_own, grad_middle, norm_gains[0:1], sums, columns, layers)
-    if aligned:
-        grad_input, gain_sums, attn_shard, ffn_shard = last_step(*last_args, (attn_term, ffn_sum))
-    else:
+            attn_term = jnp.concatenate(
+                [
+                    unpadded(attn_term, heads),
+                    *own_rows,
+                    unpadded(attn_term[(heads + 2) * LANES :], heads),
+                ]
+            )
         attn_sum = lax.psum_scatter(attn_term, "fsdp", scatter_dimension=0, tiled=True)
-        grad_input, gain_sums = last_step(*last_args)
+        grad_input, gain_sums = last_step(
+            in_part, x_own, grad_middle, norm_gains[0:1], sums, columns, layers
+        )
         ffn_shard = ffn_plan.collect(ffn_sum)
         attn_shard = attn_plan.collect(attn_sum)
 
@@ -1533,9 +1628,13 @@
     first_column = lax.axis_index(EVERY) * column_count
     gain_shard = lax.dynamic_slice_in_dim(gain_sums[:2], first_column, column_count, 1) * grad_factor
     own_gains = lax.dynamic_slice_in_dim(norm_gains, first_column, column_count, 1)
-    (ffn_shard, new_ffn, ffn_states), (attn_shard, new_attn, attn_states) = update_all(
-        (ffn_shard, ffn_weights, ffn_moments), (attn_shard, attn_weights, attn_moments)
+    ffn_new, attn_new, (block_out, grad_input) = update_all(
+        (ffn_shard, ffn_weights, ffn_moments),
+        (attn_shard, attn_weights, attn_moments),
+        (block_out, grad_input),
     )
+    ffn_shard, new_ffn, ffn_states = ffn_new
+    attn_shard, new_attn, attn_states = attn_new
     new_gains, gain_states = adamw_update(own_gains, gain_shard, gain_moments, 0.0)
     return (
         block_out[None],

time: 306 us -> 287 us (0.938)
  Pallas kernels: 298 us -> 281 us
  local copies, waits for them, and re-layouts: 5.55 us -> 0.81 us
    pallas_call x2 -> x1, Pallas kernels: 68.6 us -> 10.4 us  [update_all(): pl.pallas_call(functools.partial(update_kernel, counts), out_shape=tuple(...]
    pallas_call x1, Pallas kernels: 96.8 us -> 139 us  [backward_step(): pl.pallas_call(functools.partial(backward_kernel, columns, layers, heads,...]
    unnamed x6 -> x2, local copies, waits for them, and re-layouts: 4.15 us -> 0.01 us
where the time goes in v6:
time: 287 us; the launch traced here: 285 us
  Pallas kernels  281 us (98%)
    pallas_call x1, Pallas kernels, backward_step(): pl.pallas_call(functools.partial(backward_kernel, columns, layers, heads,...  139 us
    pallas_call x1, Pallas kernels, forward_step(): pl.pallas_call(functools.partial(forward_kernel, columns, layers, heads,...  132 us
    pallas_call x1, Pallas kernels, update_all(): pl.pallas_call(functools.partial(update_kernel, counts), out_shape=tuple(...  10.4 us

profile of v6, /device:TPU:0, one launch (start us, length us, event | category | flops | bytes accessed | tf_op | source)
XLA Modules:
  0.0 284.9 jit_solution(13930631311758018559)
XLA Ops:
  0.6 132.0 %forward_step.1 = (bf16[1024,256]{1,0:T(8,128)(2,1)}, bf16[1024,128]{1,0:T(8,128)(2,1)}, bf16[1024,128]{1,0:T(8,128)(2,1)}, bf16[1024,256]{1,0:T(8,128)(2,1)}, f...) custom-call(bf16[128,1536]{1,0:T(8,128)(2,1)} %bitcast.19, ...), custom_call_target="tpu_custom_call" | custom-call | flops 6000000000 | bytes 250000000 | tf_op jit(solution)/shard_map/forward_step/pallas_call | solution.py:1018
  132.6 0.0 copy-start
  132.6 139.0 %backward_step.1 = (f32[128,1536]{1,0:T(8,128)}, f32[128,1536]{1,0:T(8,128)}, f32[8,1536]{1,0:T(8,128)}, bf16[144,1536]{1,0:T(8,128)(2,1)}, bf16[384,1536]{1,0:T(8,128)(2,1)}) custom-call(bf16[1024,1536]{1,0:T(8,128)(2,1)} %get-tuple-element.38.refs_0_, bf16[1024,1536]{1,0:T(8,128)(2,1)} %get-tuple-element.39.refs_1_, ...), custom_call_target="tpu_custom_call" | custom-call | flops 28000000000 | bytes 250000000 | tf_op jit(solution)/shard_map/backward_step/pallas_call | solution.py:1382
  271.7 0.8 slice.9
  272.5 0.0 copy-done
  272.5 1.3 multiply_subtract_fusion
  273.8 0.6 pad_maximum_fusion
  274.4 10.4 %update_all.1 = (f32[384,1536]{1,0:T(8,128)}, f32[384,1536]{1,0:T(8,128)}, f32[2,384,1536]{2,1,0:T(8,128)}, f32[144,1536]{1,0:T(8,128)}, f32[144,1536]{1,0:T(8,1...) custom-call(bf16[384,1536]{1,0:T(8,128)(2,1)} %get-tuple-element.52.refs_0_, ...), custom_call_target="tpu_custom_call" | custom-call | flops 20000000 | bytes 25000000 | tf_op jit(solution)/shard_map/update_all/pallas_call | solution.py:1508
Async XLA Ops:
  132.6 139.8 %copy-start = (f32[2,2,48]{2,1,0:T(2,128)S(1)}, f32[2,2,48]{2,1,0:T(2,128)}, u32[]{:S(2)}) copy-start(f32[2,2,48]{2,1,0:T(2,128)} %param.18) | copy-start | bytes 2308
